TPU v7x, 128 devices: a whole 4x4x4 slice. The times are simulated.
128 devices in a mesh: dev: 128 (over z, x, y, core).
Axes of the slice: x: 4, y: 4, z: 4, core: 2. Of those that a mesh axis runs over, the one named last changes fastest.
Arguments:
- gradient: bfloat16 [65536, 1024], P('dev'), may hold values from -0.1875 to 0.1875
- statistics: float32 [128, 1024, 1024], P('dev')
- held_roots: bfloat16 [128, 1024, 1024], P('dev')
- pending_roots: bfloat16 [256, 1024, 1024], P('dev')
- pending_stat: int32 [256], replicated, may hold values from -1 to 127, as said below
- refresh_stat: int32 [256], replicated, may hold values from -1 to 127, as said below
Outputs:
- new_statistics: float32 [128, 1024, 1024], P('dev')
- merged_roots: bfloat16 [128, 1024, 1024], P('dev')
- direction: bfloat16 [65536, 1024], P('dev')
- fresh_roots: bfloat16 [256, 1024, 1024], P('dev')
Inputs may be any that keep to these rules, and one draw needn't show every extreme that they name: `refresh_stat`: entry w * 2 + k is the slot k of device w. Exactly 64 entries are not -1, each naming a different statistic, and at least one device has all 2 of its slots used. `pending_stat`: entry w * 2 + k names the statistic whose root stands in pending_roots at that index. Exactly 64 entries are not -1, each naming a different statistic, and at least one device has all 2 of its slots used.
All inputs are finite; a program needn't handle non-finite values.
Results may differ from a plain program's by a relative error of at most 0.012.
Values may be sent and summed in bfloat16 or wider, within the bound.
No kernel may reach another device: no remote copies, remote signals or barrier semaphores. Data moves between devices by JAX's collectives and lax.ppermute only.
A program may use at most 128 MiB of HBM per device.

v0:
```python
import jax
import jax.numpy as jnp
from jax import lax
from jax.sharding import PartitionSpec as P

ITERS = 2


decay_rate = 0.9


def swapped(shard, axis, bit):
    return lax.ppermute(shard, axis, [(i, i ^ 1 << bit) for i in range(lax.axis_size(axis))])


def spread(parts):
    return lax.all_to_all(parts, "dev", split_axis=0, concat_axis=0, tiled=True)


def poly_times(first, second):
    result = [0.0] * (len(first) + len(second) - 1)
    for left_pos in range(len(first)):
        for right_pos in range(len(second)):
            result[left_pos + right_pos] += first[left_pos] * second[right_pos]
    return result


def root_polynomial(iteration_count):
    x_poly = [1.0]
    m_poly = [0.0, 1.0]
    for newton_turn in range(iteration_count):
        t_poly = [-value / 4.0 for value in m_poly]
        t_poly[0] += 5.0 / 4.0
        x_poly = poly_times(x_poly, t_poly)
        t_square = poly_times(t_poly, t_poly)
        m_poly = poly_times(poly_times(t_square, t_square), m_poly)
    return [float(value) for value in x_poly]


def matmul_exact(first, second):
    return jnp.dot(first, second, preferred_element_type=jnp.float32)


def inverse_root(statistic):
    size_b = statistic.shape[0]
    identity = jnp.eye(size_b, dtype=jnp.float32)
    norm_scale = 2.0 * jnp.trace(statistic) / size_b
    scaled = statistic / norm_scale
    coefficients = root_polynomial(ITERS)
    scaled_sq = matmul_exact(scaled, scaled)
    scaled_cube = matmul_exact(scaled_sq, scaled)
    lower_part = coefficients[0] * identity + coefficients[1] * scaled + coefficients[2] * scaled_sq
    upper_part = (
        coefficients[3] * identity
        + coefficients[4] * scaled
        + coefficients[5] * scaled_sq
        + coefficients[6] * scaled_cube
    )
    polynomial = lower_part + matmul_exact(scaled_cube, upper_part)
    return polynomial * norm_scale ** (-0.25)


def per_device(gradient, statistics, held_roots, pending_roots, pending_stat, refresh_stat):
    devices = lax.axis_size("dev")
    my_index = lax.axis_index("dev")
    parity = my_index % 2
    block_width = statistics.shape[1]
    piece_rows = block_width // devices
    slot_count = pending_roots.shape[0]
    half_rows = gradient.shape[0]
    slot_total = pending_stat.shape[0]

    pending_parts = spread(
        pending_roots.reshape(slot_count, devices, piece_rows, block_width).transpose(1, 0, 2, 3)
    ).reshape(slot_total, piece_rows, block_width)

    other_half = swapped(gradient, "dev", 0)
    top_half = jnp.where(parity == 0, gradient, other_half)
    bottom_half = jnp.where(parity == 0, other_half, gradient)
    full_grad = jnp.concatenate([top_half, bottom_half], axis=0)
    gram_term = lax.cond(
        parity == 0,
        lambda: lax.dot_general(
            full_grad, full_grad, (((1,), (1,)), ((), ())), preferred_element_type=jnp.float32
        ),
        lambda: lax.dot_general(
            full_grad, full_grad, (((0,), (0,)), ((), ())), preferred_element_type=jnp.float32
        ),
    )
    new_stat = decay_rate * statistics[0] + (1.0 - decay_rate) * gram_term
    my_root = lax.cond(
        jnp.any(refresh_stat == my_index),
        lambda: inverse_root(new_stat).astype(jnp.bfloat16),
        lambda: jnp.zeros(new_stat.shape, jnp.bfloat16),
    )
    root_parts = spread(my_root.reshape(devices, piece_rows, block_width))

    slot_match = pending_stat[None, :] == jnp.arange(devices, dtype=jnp.int32)[:, None]
    slot_of = jnp.sum(
        jnp.where(slot_match, jnp.arange(slot_total, dtype=jnp.int32)[None, :], 0), axis=1
    )
    returned = spread(jnp.take(pending_parts, slot_of, axis=0)).reshape(block_width, block_width)
    my_found = jnp.any(pending_stat == my_index)
    merged = jnp.where(my_found, returned, held_roots[0])

    routed = jnp.take(root_parts, jnp.maximum(refresh_stat, 0), axis=0)
    fresh = spread(routed.reshape(devices, slot_count, piece_rows, block_width))
    my_slots = lax.dynamic_slice_in_dim(refresh_stat, my_index * slot_count, slot_count, 0)
    fresh_roots = jnp.where(
        (my_slots >= 0)[:, None, None, None],
        fresh.transpose(1, 0, 2, 3),
        jnp.zeros((), jnp.bfloat16),
    ).reshape(slot_count, block_width, block_width)

    partner_root = swapped(merged, "dev", 0)
    left_root = jnp.where(parity == 0, merged, partner_root)
    right_root = jnp.where(parity == 0, partner_root, merged)
    left_rows = lax.dynamic_slice_in_dim(left_root, parity * half_rows, half_rows, 0)
    left_times = jnp.dot(left_rows, full_grad, preferred_element_type=jnp.float32).astype(
        jnp.bfloat16
    )
    product = jnp.dot(left_times, right_root, preferred_element_type=jnp.float32)
    own_square = jnp.sum(product * product)
    other_square = swapped(own_square, "dev", 0)
    rms_scale = lax.rsqrt((own_square + other_square) / (block_width * block_width) + 1e-06)
    direction = (product * rms_scale).astype(jnp.bfloat16)
    return (new_stat[None], merged[None], direction, fresh_roots)


def solution(mesh):
    in_specs = (
        P("dev", None),
        P("dev", None, None),
        P("dev", None, None),
        P("dev", None, None),
        P(),
        P(),
    )
    out_specs = (P("dev", None, None), P("dev", None, None), P("dev", None), P("dev", None, None))
    return jax.shard_map(
        per_device, mesh=mesh, in_specs=in_specs, out_specs=out_specs, check_vma=False
    )
```

profile of v0, /device:TPU:1, one launch (start us, length us, event | category | flops | bytes accessed | tf_op | source)
XLA Modules:
  0.0 218.2 jit_solution(2371243505754865445)
XLA Ops:
  0.6 4.8 %copy.14 = bf16[128,2,8,1024]{3,2,1,0:T(8,128)(2,1)} copy(bf16[128,2,8,1024]{3,2,0,1:T(8,128)(2,1)} %bitcast.33) | data formatting | bytes 8388608 | tf_op jit(solution)/shard_map/transpose | solution.py:74
  5.4 11.9 %all-to-all-start = ((bf16[128,2,8,1024]{3,2,1,0:T(8,128)(2,1)}), bf16[128,2,8,1024]{3,2,1,0:T(8,128)(2,1)}, u32[]{:S(2)}, u32[]{:S(2)}) async-start(bf16[128,2,8,1024]{3,2,1,0:T(8,128)(2,1)} %copy.14), calls=%async_computation | async-start | bytes 8388608 | tf_op jit(solution)/shard_map/all_to_all | solution.py:17
  17.4 1.2 collective-permute-start
  22.3 4.4 %conditional.2 = (f32[1024,1024]{1,0:T(8,128)}) conditional(s32[]{:T(128)} %convert_element_type.16, bf16[1024,1024]{1,0:T(8,128)(2,1)S(1)} %pad_maximum_fusion, bf16[1024,1024]{1,0:T(8,128)(2,1)S(1)} %pad_maximum_fusion), branch_computations={%region_0.1_spmd, %region_1.2_spmd} | conditional | flops 2147483648 | bytes 6291464 | solution.py:81
  22.3 4.4 %fusion.30 = f32[1024,1024]{1,0:T(8,128)} fusion(bf16[1024,1024]{1,0:T(8,128)(2,1)S(1)} %param), kind=kOutput, calls=%fused_computation.59 | convolution fusion | flops 2147483648 | bytes 6291456 | tf_op jit(solution)/shard_map/cond/branch_0_fun/dot_general | solution.py:86
  26.7 7.0 %bitcast_add_fusion = f32[1024,1024]{1,0:T(8,128)} fusion(f32[1024,1024]{1,0:T(8,128)} %get-tuple-element.19, f32[1,1024,1024]{2,1,0:T(8,128)} %param.11), kind=kLoop, calls=%fused_computation.26 | loop fusion | flops 3145728 | bytes 12582912 | tf_op jit(solution)/shard_map/add | solution.py:90
  34.1 36.0 %all-to-all-done = bf16[128,2,8,1024]{3,2,1,0:T(8,128)(2,1)} async-done(((bf16[128,2,8,1024]{3,2,1,0:T(8,128)(2,1)}), bf16[128,2,8,1024]{3,2,1,0:T(8,128)(2,1)}, u32[]{:S(2)}, u32[]{:S(2)}) %all-to-all-start) | async-done | bytes 4194336 | tf_op jit(solution)/shard_map/all_to_all | solution.py:17
  70.1 4.4 %all-to-all-start.2 = ((bf16[128,8,1024]{2,1,0:T(8,128)(2,1)}), bf16[128,8,1024]{2,1,0:T(8,128)(2,1)S(1)}, u32[]{:S(2)}, u32[]{:S(2)}) async-start(bf16[128,8,1024]{2,1,0:T(8,128)(2,1)} %bitcast.32), calls=%async_computation.2 | async-start | bytes 4194304 | tf_op jit(solution)/shard_map/all_to_all | solution.py:17
  74.7 4.2 %gather_fusion = bf16[128,8,1024]{2,1,0:T(8,128)(2,1)} fusion(bf16[256,8,1024]{2,1,0:T(8,128)(2,1)} %bitcast.4, s32[1024]{0:T(1024)S(1)} %pad_clamp_fusion.1), kind=kCustom, calls=%fused_computation | custom fusion | bytes 4194816 | tf_op jit(solution)/shard_map/jit(_take)/gather | solution.py:102
  78.8 3.2 %broadcast_select_fusion.1 = bf16[128,8,1024]{2,1,0:T(8,128)(2,1)} fusion(bf16[128,8,1024]{2,1,0:T(8,128)(2,1)} %gather_fusion, pred[128]{0:T(512)(128)(4,1)S(1)} %compare_and_fusion), kind=kLoop, calls=%fused_computation.37 | loop fusion | flops 1048576 | bytes 4194432 | tf_op jit(solution)/shard_map/jit(_take)/select_n | solution.py:102
  82.0 22.7 %all-to-all-done.2 = bf16[128,8,1024]{2,1,0:T(8,128)(2,1)S(1)} async-done(((bf16[128,8,1024]{2,1,0:T(8,128)(2,1)}), bf16[128,8,1024]{2,1,0:T(8,128)(2,1)S(1)}, u32[]{:S(2)}, u32[]{:S(2)}) %all-to-all-start.2) | async-done | bytes 2097184 | tf_op jit(solution)/shard_map/all_to_all | solution.py:17
  104.7 1.3 copy-done
  106.1 4.7 %all-to-all-start.1 = ((bf16[128,8,1024]{2,1,0:T(8,128)(2,1)}), bf16[128,8,1024]{2,1,0:T(8,128)(2,1)S(1)}, u32[]{:S(2)}, u32[]{:S(2)}) async-start(bf16[128,8,1024]{2,1,0:T(8,128)(2,1)} %broadcast_select_fusion.1), calls=%async_computation.1 | async-start | bytes 4194304 | tf_op jit(solution)/shard_map/all_to_all | solution.py:17
  111.0 4.4 %gather_fusion.1 = bf16[256,8,1024]{2,1,0:T(8,128)(2,1)} fusion(bf16[128,8,1024]{2,1,0:T(8,128)(2,1)} %copy-done, s32[1024]{0:T(1024)S(1)} %pad_clamp_fusion), kind=kCustom, calls=%fused_computation.1 | custom fusion | bytes 8389632 | tf_op jit(solution)/shard_map/jit(_take)/gather | solution.py:106
  115.4 3.9 %broadcast_select_fusion = bf16[128,2,8,1024]{3,2,1,0:T(8,128)(2,1)} fusion(bf16[128,2,8,1024]{3,2,1,0:T(8,128)(2,1)} %bitcast.31, pred[128,2]{1,0:T(8,128)(4,1)S(1)} %broadcast_in_dim.64), kind=kLoop, calls=%fused_computation.29 | loop fusion | flops 2097152 | bytes 8388864 | tf_op jit(solution)/shard_map/jit(_take)/select_n | solution.py:106
  119.3 21.8 %all-to-all-done.1 = bf16[128,8,1024]{2,1,0:T(8,128)(2,1)S(1)} async-done(((bf16[128,8,1024]{2,1,0:T(8,128)(2,1)}), bf16[128,8,1024]{2,1,0:T(8,128)(2,1)S(1)}, u32[]{:S(2)}, u32[]{:S(2)}) %all-to-all-start.1) | async-done | bytes 2097184 | tf_op jit(solution)/shard_map/all_to_all | solution.py:17
  141.1 5.9 %all-to-all-start.3 = ((bf16[128,2,8,1024]{3,2,1,0:T(8,128)(2,1)}), bf16[128,2,8,1024]{3,2,1,0:T(8,128)(2,1)}, u32[]{:S(2)}, u32[]{:S(2)}) async-start(bf16[128,2,8,1024]{3,2,1,0:T(8,128)(2,1)} %broadcast_select_fusion), calls=%async_computation.3 | async-start | bytes 8388608 | tf_op jit(solution)/shard_map/all_to_all | solution.py:17
  147.6 3.8 %bitcast_select_fusion = bf16[1024,1024]{1,0:T(8,128)(2,1)} fusion(bf16[1,1024,1024]{2,1,0:T(8,128)(2,1)} %param.12, bf16[128,8,1024]{2,1,0:T(8,128)(2,1)S(1)} %all-to-all-done.1, pred[]{:T(512)} %compare_reduce_fusion.1), kind=kLoop, calls=%fused_computation.31 | loop fusion | flops 1048576 | bytes 6291457 | tf_op jit(solution)/shard_map/jit(_where)/select_n | solution.py:104
  151.4 1.3 collective-permute-start.1
  152.7 3.7 %bitcast_select_fusion.1 = bf16[1,1024,1024]{2,1,0:T(8,128)(2,1)} fusion(bf16[1,1024,1024]{2,1,0:T(8,128)(2,1)} %param.12, bf16[128,8,1024]{2,1,0:T(8,128)(2,1)S(1)} %all-to-all-done.1, pred[]{:T(512)} %compare_reduce_fusion.1), kind=kLoop, calls=%fused_computation.32 | loop fusion | flops 1048576 | bytes 6291457 | tf_op jit(solution)/shard_map/jit(_where)/select_n | solution.py:104
  156.5 43.3 %all-to-all-done.3 = bf16[128,2,8,1024]{3,2,1,0:T(8,128)(2,1)} async-done(((bf16[128,2,8,1024]{3,2,1,0:T(8,128)(2,1)}), bf16[128,2,8,1024]{3,2,1,0:T(8,128)(2,1)}, u32[]{:S(2)}, u32[]{:S(2)}) %all-to-all-start.3) | async-done | bytes 4194336 | tf_op jit(solution)/shard_map/all_to_all | solution.py:17
  199.8 5.8 %copy_bitcast_fusion = bf16[2,1024,1024]{2,1,0:T(8,128)(2,1)} fusion(bf16[128,2,8,1024]{3,2,1,0:T(8,128)(2,1)} %all-to-all-done.3, pred[2]{0:T(512)(128)(4,1)S(1)} %dynamic-slice_compare_fusion), kind=kLoop, calls=%fused_computation.27 | loop fusion | flops 2097152 | bytes 8388610 | tf_op jit(solution)/shard_map/reshape | solution.py:113
  205.6 6.5 %multiply_reduce_fusion = (f32[]{:T(128)}, f32[512,1024]{1,0:T(8,128)}) fusion(bf16[1024,1024]{1,0:T(8,128)(2,1)} %collective-permute-done.1, bf16[1024,1024]{1,0:T(8,128)(2,1)} %bitcast_select_fusion, pred[]{:T(512)S(6)} %eq.41, s32[]{:T(128)S(6)} %select_n.106, bf16[512,1024]{1,0:T(8,128)(2,1)S(1)} %copy-done.4, bf16[512,1024]{1,0:T(8,128)(2,1)S(1)} %get-tuple-element.13), kind=kOutput, calls=%fused_computation.34 | convolution fusion | flops 2154823680 | bytes 10487300 | tf_op jit(solution)/shard_map/dot_general | solution.py:122
  215.4 2.8 %multiply_convert_fusion.1 = bf16[512,1024]{1,0:T(8,128)(2,1)} fusion(f32[512,1024]{1,0:T(8,128)} %get-tuple-element.18, f32[]{:T(128)S(6)} %rsqrt.3), kind=kLoop, calls=%fused_computation.33 | loop fusion | flops 1048576 | bytes 3145732 | tf_op jit(solution)/shard_map/convert_element_type | solution.py:126
  (31 shorter events, 6.7 us)
Async XLA Ops:
  5.4 12.0 %copy-start.5 = (bf16[512,1024]{1,0:T(8,128)(2,1)S(1)}, bf16[512,1024]{1,0:T(8,128)(2,1)}, u32[]{:S(2)}) copy-start(bf16[512,1024]{1,0:T(8,128)(2,1)} %param.10) | copy-start | bytes 3145732
  5.4 13.2 %copy-start.6 = (s32[256]{0:T(256)S(1)}, s32[256]{0:T(256)}, u32[]{:S(2)}) copy-start(s32[256]{0:T(256)} %param.15) | copy-start | bytes 3076
  5.4 64.7 %all-to-all-start = ((bf16[128,2,8,1024]{3,2,1,0:T(8,128)(2,1)}), bf16[128,2,8,1024]{3,2,1,0:T(8,128)(2,1)}, u32[]{:S(2)}, u32[]{:S(2)}) async-start(bf16[128,2,8,1024]{3,2,1,0:T(8,128)(2,1)} %copy.14), calls=%async_computation | async-start | bytes 8388608 | tf_op jit(solution)/shard_map/all_to_all | solution.py:17
  17.4 3.5 %collective-permute-start = (bf16[512,1024]{1,0:T(8,128)(2,1)S(1)}, bf16[512,1024]{1,0:T(8,128)(2,1)S(1)}, u32[]{:S(2)}, u32[]{:S(2)}) collective-permute-start(bf16[512,1024]{1,0:T(8,128)(2,1)S(1)} %copy-done.5), channel_id=1, source_target_pairs={{0,1},{1,0},{2,3},{3,2},{4,5},{5,4},{6,7},{7,6},{8,9},{9,8},{10,11... | collective-permute-start | bytes 3145736 | tf_op jit(solution)/shard_map/ppermute | solution.py:13
  21.1 1.0 copy-start.3
  34.1 36.0 %copy-start.2 = (bf16[1024,1024]{1,0:T(8,128)(2,1)}, bf16[1024,1024]{1,0:T(8,128)(2,1)S(1)}, u32[]{:S(2)}) copy-start(bf16[1024,1024]{1,0:T(8,128)(2,1)S(1)} %get-tuple-element.20) | copy-start | bytes 6291460
  34.1 40.4 %copy-start.7 = (s32[256]{0:T(256)S(1)}, s32[256]{0:T(256)}, u32[]{:S(2)}) copy-start(s32[256]{0:T(256)} %param.14) | copy-start | bytes 3076
  70.1 34.6 %all-to-all-start.2 = ((bf16[128,8,1024]{2,1,0:T(8,128)(2,1)}), bf16[128,8,1024]{2,1,0:T(8,128)(2,1)S(1)}, u32[]{:S(2)}, u32[]{:S(2)}) async-start(bf16[128,8,1024]{2,1,0:T(8,128)(2,1)} %bitcast.32), calls=%async_computation.2 | async-start | bytes 4194304 | tf_op jit(solution)/shard_map/all_to_all | solution.py:17
  104.7 1.3 copy-start
  106.1 35.0 %all-to-all-start.1 = ((bf16[128,8,1024]{2,1,0:T(8,128)(2,1)}), bf16[128,8,1024]{2,1,0:T(8,128)(2,1)S(1)}, u32[]{:S(2)}, u32[]{:S(2)}) async-start(bf16[128,8,1024]{2,1,0:T(8,128)(2,1)} %broadcast_select_fusion.1), calls=%async_computation.1 | async-start | bytes 4194304 | tf_op jit(solution)/shard_map/all_to_all | solution.py:17
  141.1 58.7 %all-to-all-start.3 = ((bf16[128,2,8,1024]{3,2,1,0:T(8,128)(2,1)}), bf16[128,2,8,1024]{3,2,1,0:T(8,128)(2,1)}, u32[]{:S(2)}, u32[]{:S(2)}) async-start(bf16[128,2,8,1024]{3,2,1,0:T(8,128)(2,1)} %broadcast_select_fusion), calls=%async_computation.3 | async-start | bytes 8388608 | tf_op jit(solution)/shard_map/all_to_all | solution.py:17
  151.4 54.2 %collective-permute-start.1 = (bf16[1024,1024]{1,0:T(8,128)(2,1)}, bf16[1024,1024]{1,0:T(8,128)(2,1)}, u32[]{:S(2)}, u32[]{:S(2)}) collective-permute-start(bf16[1024,1024]{1,0:T(8,128)(2,1)} %bitcast_select_fusion), channel_id=1, source_target_pairs={{0,1},{1,0},{2,3},{3,2},{4,5},{5,4},{6,7},{7,6},{8,9},{9,8},{10,11... | collective-permute-start | bytes 6291464 | tf_op jit(solution)/shard_map/ppermute | solution.py:13
  156.5 49.1 %copy-start.4 = (bf16[512,1024]{1,0:T(8,128)(2,1)S(1)}, bf16[512,1024]{1,0:T(8,128)(2,1)}, u32[]{:S(2)}) copy-start(bf16[512,1024]{1,0:T(8,128)(2,1)} %copy-done.3) | copy-start | bytes 3145732
  212.1 1.9 collective-permute-start.2
where the time goes:
time: 219 us; the launch traced here: 218 us
  waiting for transfers between devices  126 us (58%)
  other arithmetic  32.1 us (15%)
  starting transfers between devices  30.3 us (14%)
  local copies, waits for them, and re-layouts  16.1 us (7%)
  matrix products  10.9 us (5%)
  between operations  2.8 us (1%)
    all_to_all x4, waiting for transfers between devices, spread(): return lax.all_to_all(parts, 'dev', split_axis=0, concat_axis=0, tiled=True)  124 us
    all_to_all x4, starting transfers between devices, spread(): return lax.all_to_all(parts, 'dev', split_axis=0, concat_axis=0, tiled=True)  26.9 us
    select_n x2, other arithmetic, per_device(): merged = jnp.where(my_found, returned, held_roots[0])  7.51 us
    add x1, other arithmetic, per_device(): new_stat = decay_rate * statistics[0] + (1.0 - decay_rate) * gram_term  6.97 us
    dot_general x1, matrix products, per_device(): jnp.dot(left_times, right_root, preferred_element_type=jnp.float32)  6.53 us
    reshape x1, other arithmetic, per_device(): fresh_roots = jnp.where((my_slots >= 0)[:, None, None, None], fresh.trans...  5.8 us
    transpose x1, local copies, waits for them, and re-layouts, per_device(): pending_roots.reshape(slot_count, devices, piece_rows, block_width)  4.81 us
    gather x1, local copies, waits for them, and re-layouts, per_device(): routed = jnp.take(root_parts, jnp.maximum(refresh_stat, 0), axis=0)  4.43 us
  transfers between devices with their start and end apart: 7, of which 6 were waited for; matrix products, arithmetic and copies ran while one was open for 20% of the time, Pallas kernels for 0%

commit v1 on v0

--- a/solution.py
+++ b/solution.py
@@ -1,7 +1,12 @@
+import functools
+
 import jax
 import jax.numpy as jnp
 from jax import lax
+from jax.experimental import pallas as pl
+from jax.experimental.pallas import tpu as pltpu
 from jax.sharding import PartitionSpec as P
+
 
 ITERS = 2
 
@@ -15,6 +20,67 @@
 
 def spread(parts):
     return lax.all_to_all(parts, "dev", split_axis=0, concat_axis=0, tiled=True)
+
+
+FIRST, OWN, SHARED, EXTRA = range(4)
+
+
+def pick_kernel(width, kind_ref, row_ref, *refs):
+    tables, out_ref, sem = refs[:-2], refs[-2], refs[-1]
+    half = width // 2
+
+    def issue(item, carry):
+        kind, row = kind_ref[item], row_ref[item]
+
+        def start(src, dst):
+            pltpu.make_async_copy(src, dst, sem).start()
+
+        @pl.when(kind == OWN)
+        def _():
+            start(tables[0].at[row, :, pl.ds(0, width)], out_ref.at[item])
+
+        if len(tables) > 1:
+
+            @pl.when(kind == FIRST)
+            def _():
+                start(tables[1].at[row], out_ref.at[item])
+
+            @pl.when(kind == SHARED)
+            def _():
+                for core in range(2):
+                    start(
+                        tables[0].at[row // 2 * 2 + core, :, pl.ds(width, half)],
+                        out_ref.at[item, :, pl.ds(core * half, half)],
+                    )
+
+        if len(tables) > 2:
+
+            @pl.when(kind == EXTRA)
+            def _():
+                start(tables[2].at[row], out_ref.at[item])
+
+        return carry
+
+    lax.fori_loop(0, out_ref.shape[0], issue, 0, unroll=4)
+    pltpu.make_async_copy(out_ref, out_ref, sem).wait()
+
+
+def pick(kind, row, width, *tables):
+    items, piece_rows = kind.shape[0], tables[0].shape[1]
+    out_bytes = items * piece_rows * width * 2
+    return pl.pallas_call(
+        functools.partial(pick_kernel, width),
+        out_shape=jax.ShapeDtypeStruct((items, piece_rows, width), tables[0].dtype),
+        in_specs=[pl.BlockSpec(memory_space=pltpu.SMEM)] * 2
+        + [pl.BlockSpec(memory_space=pl.ANY)] * len(tables),
+        out_specs=pl.BlockSpec(memory_space=pltpu.VMEM),
+        scratch_shapes=[pltpu.SemaphoreType.DMA],
+        compiler_params=pltpu.CompilerParams(vmem_limit_bytes=16 * 1024 * 1024),
+        cost_estimate=pl.CostEstimate(
+            flops=4 * 1000 * 1000 * 1000, bytes_accessed=2 * out_bytes, transcendentals=0
+        ),
+        name="pick",
+    )(kind, row, *tables)
 
 
 def poly_times(first, second):
@@ -28,7 +94,7 @@
 def root_polynomial(iteration_count):
     x_poly = [1.0]
     m_poly = [0.0, 1.0]
-    for newton_turn in range(iteration_count):
+    for _ in range(iteration_count):
         t_poly = [-value / 4.0 for value in m_poly]
         t_poly[0] += 5.0 / 4.0
         x_poly = poly_times(x_poly, t_poly)
@@ -68,11 +134,22 @@
     piece_rows = block_width // devices
     slot_count = pending_roots.shape[0]
     half_rows = gradient.shape[0]
+    half_columns = block_width // 2
     slot_total = pending_stat.shape[0]
-
-    pending_parts = spread(
-        pending_roots.reshape(slot_count, devices, piece_rows, block_width).transpose(1, 0, 2, 3)
-    ).reshape(slot_total, piece_rows, block_width)
+    device_ids = jnp.arange(devices, dtype=jnp.int32)
+
+    has_first = pending_stat.reshape(devices, slot_count)[:, 0] >= 0
+    has_second = has_first & (pending_stat.reshape(devices, slot_count)[:, 1] >= 0)
+    refreshed = jnp.any(refresh_stat[None, :] == device_ids[:, None], axis=1)
+    sharing = has_second & refreshed
+    sharing_pairs = sharing.reshape(devices // 2, 2)
+    unplaced = jnp.any(sharing_pairs[:, 0] & sharing_pairs[:, 1])
+
+    my_first = lax.dynamic_slice_in_dim(pending_stat, my_index * slot_count, 1, 0)[0] >= 0
+    first_root = lax.dynamic_index_in_dim(
+        pending_roots, jnp.where(my_first, 0, 1), 0, keepdims=False
+    )
+    first_parts = spread(first_root.reshape(devices, piece_rows, block_width))
 
     other_half = swapped(gradient, "dev", 0)
     top_half = jnp.where(parity == 0, gradient, other_half)
@@ -88,42 +165,86 @@
         ),
     )
     new_stat = decay_rate * statistics[0] + (1.0 - decay_rate) * gram_term
-    my_root = lax.cond(
-        jnp.any(refresh_stat == my_index),
-        lambda: inverse_root(new_stat).astype(jnp.bfloat16),
-        lambda: jnp.zeros(new_stat.shape, jnp.bfloat16),
-    )
-    root_parts = spread(my_root.reshape(devices, piece_rows, block_width))
-
-    slot_match = pending_stat[None, :] == jnp.arange(devices, dtype=jnp.int32)[:, None]
+
+    second_root = pending_roots[1]
+    my_refreshed = jnp.any(refresh_stat == my_index)
+    first_of_pair = lax.dynamic_slice_in_dim(sharing, my_index - parity, 1, 0)[0]
+    from_other = jnp.where(first_of_pair, parity == 1, parity == 0)
+    left_columns, right_columns = second_root[:, :half_columns], second_root[:, half_columns:]
+    other_columns = swapped(jnp.where(parity == 0, right_columns, left_columns), "dev", 0)
+    own_columns = jnp.where(parity == 0, left_columns, right_columns)
+    shared_columns = jnp.where(from_other, other_columns, own_columns)
+    own_matrix = lax.cond(
+        my_refreshed, lambda: inverse_root(new_stat).astype(jnp.bfloat16), lambda: second_root
+    )
+    root_parts = spread(
+        jnp.concatenate([own_matrix, shared_columns], axis=1).reshape(
+            devices, piece_rows, block_width + half_columns
+        ),
+    )
+
+    slot_match = pending_stat[None, :] == device_ids[:, None]
     slot_of = jnp.sum(
         jnp.where(slot_match, jnp.arange(slot_total, dtype=jnp.int32)[None, :], 0), axis=1
     )
-    returned = spread(jnp.take(pending_parts, slot_of, axis=0)).reshape(block_width, block_width)
+    source = slot_of // slot_count
+    is_second = jnp.any(
+        slot_match & (jnp.arange(slot_total) % slot_count == 1) & jnp.repeat(has_first, slot_count),
+        axis=1,
+    )
+    is_shared = jnp.any(slot_match & jnp.repeat(refreshed, slot_count), axis=1)
+    is_extra = jnp.any(
+        slot_match
+        & (jnp.arange(slot_total) // slot_count % 2 == 1)
+        & jnp.repeat(jnp.repeat(sharing_pairs[:, 0], 2), slot_count),
+        axis=1,
+    )
+    kind = jnp.where(is_second, jnp.where(is_shared, SHARED, OWN), FIRST).astype(jnp.int32)
+    kind_extra = jnp.where(is_second & is_shared & is_extra, EXTRA, kind).astype(jnp.int32)
+    chosen = lax.cond(
+        unplaced,
+        lambda: pick(
+            kind_extra,
+            source,
+            block_width,
+            root_parts,
+            first_parts,
+            spread(second_root.reshape(devices, piece_rows, block_width)),
+        ),
+        lambda: pick(kind, source, block_width, root_parts, first_parts),
+    )
+    returned = spread(chosen).reshape(block_width, block_width)
     my_found = jnp.any(pending_stat == my_index)
     merged = jnp.where(my_found, returned, held_roots[0])
 
-    routed = jnp.take(root_parts, jnp.maximum(refresh_stat, 0), axis=0)
+    routed = pick(
+        jnp.full((slot_total,), OWN, jnp.int32),
+        jnp.maximum(refresh_stat, 0),
+        block_width,
+        root_parts,
+    )
     fresh = spread(routed.reshape(devices, slot_count, piece_rows, block_width))
+
+    partner_root = swapped(merged, "dev", 0)
+    left_root = jnp.where(parity == 0, merged, partner_root)
+    right_root = jnp.where(parity == 0, partner_root, merged)
+    left_rows = lax.dynamic_slice_in_dim(left_root, parity * half_rows, half_rows, 0)
+    left_times = jnp.dot(left_rows, full_grad, preferred_element_type=jnp.float32).astype(
+        jnp.bfloat16
+    )
+    product = jnp.dot(left_times, right_root, preferred_element_type=jnp.float32)
+    own_square = jnp.sum(product * product)
+    other_square = swapped(own_square, "dev", 0)
+    rms_scale = lax.rsqrt((own_square + other_square) / (block_width * block_width) + 1e-06)
+    direction = (product * rms_scale).astype(jnp.bfloat16)
+
+    fresh, direction = lax.optimization_barrier((fresh, direction))
     my_slots = lax.dynamic_slice_in_dim(refresh_stat, my_index * slot_count, slot_count, 0)
     fresh_roots = jnp.where(
         (my_slots >= 0)[:, None, None, None],
         fresh.transpose(1, 0, 2, 3),
         jnp.zeros((), jnp.bfloat16),
     ).reshape(slot_count, block_width, block_width)
-
-    partner_root = swapped(merged, "dev", 0)
-    left_root = jnp.where(parity == 0, merged, partner_root)
-    right_root = jnp.where(parity == 0, partner_root, merged)
-    left_rows = lax.dynamic_slice_in_dim(left_root, parity * half_rows, half_rows, 0)
-    left_times = jnp.dot(left_rows, full_grad, preferred_element_type=jnp.float32).astype(
-        jnp.bfloat16
-    )
-    product = jnp.dot(left_times, right_root, preferred_element_type=jnp.float32)
-    own_square = jnp.sum(product * product)
-    other_square = swapped(own_square, "dev", 0)
-    rms_scale = lax.rsqrt((own_square + other_square) / (block_width * block_width) + 1e-06)
-    direction = (product * rms_scale).astype(jnp.bfloat16)
     return (new_stat[None], merged[None], direction, fresh_roots)
 
 

time: 219 us -> 228 us (1.041)
  waiting for transfers between devices: 126 us -> 101 us
  starting transfers between devices: 30.3 us -> 54.5 us
  Pallas kernels: 0 us -> 13.7 us
  other arithmetic: 32.1 us -> 29.1 us
    all_to_all x4, starting transfers between devices: 26.9 us -> 51.3 us  [spread(): return lax.all_to_all(parts, 'dev', split_axis=0, concat_axis=0, tiled=True)]
    all_to_all x4, waiting for transfers between devices: 124 us -> 99.3 us  [spread(): return lax.all_to_all(parts, 'dev', split_axis=0, concat_axis=0, tiled=True)]
    pallas_call x0 -> x2, Pallas kernels: none -> 13.7 us  [pick(): pl.pallas_call(functools.partial(pick_kernel, width), out_shape=jax.Shape...]
    gather x2 -> x0, local copies, waits for them, and re-layouts: 8.61 us -> none  [the longest x1 4.43 us: per_device(): routed = jnp.take(root_parts, jnp.maximum(refresh_stat, 0), axis=0)]
    select_n x3, other arithmetic: 7.05 us -> 1.23 us  [the longest x1 1.07 us: per_device(): jnp.where(parity == 0, right_columns, left_columns)]
    slice x0 -> x2, local copies, waits for them, and re-layouts: none -> 5.41 us  [the longest x1 5.23 us: per_device(): second_root = pending_roots[1]]
    transpose x1 -> x0, local copies, waits for them, and re-layouts: 4.81 us -> none  [per_device(): pending_roots.reshape(slot_count, devices, piece_rows, block_width)]
  transfers between devices with their start and end apart: 7 -> 8, of which waited for: 6 -> 6; matrix products, arithmetic and copies ran while one was open for 20% -> 19% of each run, Pallas kernels for 0% -> 4%
where the time goes in v1:
time: 228 us; the launch traced here: 227 us
  waiting for transfers between devices  101 us (44%)
  starting transfers between devices  54.5 us (24%)
  other arithmetic  29.1 us (13%)
  local copies, waits for them, and re-layouts  14 us (6%)
  Pallas kernels  13.7 us (6%)
  matrix products  10.1 us (4%)
  between operations  4.77 us (2%)
    all_to_all x4, waiting for transfers between devices, spread(): return lax.all_to_all(parts, 'dev', split_axis=0, concat_axis=0, tiled=True)  99.3 us
    all_to_all x4, starting transfers between devices, spread(): return lax.all_to_all(parts, 'dev', split_axis=0, concat_axis=0, tiled=True)  51.3 us
    pallas_call x2, Pallas kernels, pick(): pl.pallas_call(functools.partial(pick_kernel, width), out_shape=jax.Shape...  13.7 us
    select_n x2, other arithmetic, per_device(): merged = jnp.where(my_found, returned, held_roots[0])  7.56 us
    add x1, other arithmetic, per_device(): new_stat = decay_rate * statistics[0] + (1.0 - decay_rate) * gram_term  6.97 us
    reshape x1, other arithmetic, per_device(): fresh_roots = jnp.where((my_slots >= 0)[:, None, None, None], fresh.trans...  5.8 us
    dot_general x1, matrix products, per_device(): jnp.dot(left_times, right_root, preferred_element_type=jnp.float32)  5.68 us
    slice x1, local copies, waits for them, and re-layouts, per_device(): second_root = pending_roots[1]  5.23 us
  transfers between devices with their start and end apart: 8, of which 6 were waited for; matrix products, arithmetic and copies ran while one was open for 19% of the time, Pallas kernels for 4%

profile of v1, /device:TPU:1, one launch (start us, length us, event | category | flops | bytes accessed | tf_op | source)
XLA Modules:
  0.0 226.9 jit_solution(274931039337161599)
XLA Ops:
  0.6 1.5 collective-permute-start
  4.0 5.2 %fusion.34 = (bf16[1,1024,1024]{2,1,0:T(8,128)(2,1)}, bf16[1024,1024]{1,0:T(8,128)(2,1)S(1)}, bf16[128,8,1024]{2,1,0:T(8,128)(2,1)}) fusion(bf16[2,1024,1024]{2,1,0:T(8,128)(2,1)} %param.15, s32[]{:T(128)} %bitcast.6), kind=kLoop, calls=%fused_computation.81 | loop fusion | bytes 10485764 | tf_op jit(solution)/shard_map/slice | solution.py:169
  10.3 11.0 %all-to-all-start.2 = ((bf16[128,8,1024]{2,1,0:T(8,128)(2,1)}), bf16[128,8,1024]{2,1,0:T(8,128)(2,1)}, u32[]{:S(2)}, u32[]{:S(2)}) async-start(bf16[128,8,1024]{2,1,0:T(8,128)(2,1)} %get-tuple-element.137), calls=%async_computation.2 | async-start | bytes 4194304 | tf_op jit(solution)/shard_map/all_to_all | solution.py:22
  24.5 1.7 broadcast_select_fusion.2
  27.3 4.5 %conditional.3 = (f32[1024,1024]{1,0:T(8,128)}) conditional(s32[]{:T(128)} %convert_element_type.19, bf16[1024,1024]{1,0:T(8,128)(2,1)S(1)} %pad_maximum_fusion, bf16[1024,1024]{1,0:T(8,128)(2,1)S(1)} %pad_maximum_fusion), branch_computations={%region_0.1_spmd, %region_1.2_spmd} | conditional | flops 2147483648 | bytes 6291464 | solution.py:158
  27.3 4.4 %fusion.35 = f32[1024,1024]{1,0:T(8,128)} fusion(bf16[1024,1024]{1,0:T(8,128)(2,1)S(1)} %param), kind=kOutput, calls=%fused_computation.82 | convolution fusion | flops 2147483648 | bytes 6291456 | tf_op jit(solution)/shard_map/cond/branch_0_fun/dot_general | solution.py:163
  31.8 7.0 %bitcast_add_fusion = f32[1024,1024]{1,0:T(8,128)} fusion(f32[1024,1024]{1,0:T(8,128)} %get-tuple-element.147, f32[1,1024,1024]{2,1,0:T(8,128)} %param.13), kind=kLoop, calls=%fused_computation.33 | loop fusion | flops 3145728 | bytes 12582912 | tf_op jit(solution)/shard_map/add | solution.py:167
  40.3 1.4 copy-done.2
  41.7 1.9 maximum_bitcast_fusion
  43.6 7.5 %all-to-all-done.2 = bf16[128,8,1024]{2,1,0:T(8,128)(2,1)} async-done(((bf16[128,8,1024]{2,1,0:T(8,128)(2,1)}), bf16[128,8,1024]{2,1,0:T(8,128)(2,1)}, u32[]{:S(2)}, u32[]{:S(2)}) %all-to-all-start.2) | async-done | bytes 2097184 | tf_op jit(solution)/shard_map/all_to_all | solution.py:22
  51.1 30.0 %all-to-all-start.1 = ((bf16[128,8,1536]{2,1,0:T(8,128)(2,1)}), bf16[128,8,1536]{2,1,0:T(8,128)(2,1)}, u32[]{:S(2)}, u32[]{:S(2)}) async-start(bf16[128,8,1536]{2,1,0:T(8,128)(2,1)} %maximum_bitcast_fusion), calls=%async_computation.1 | async-start | bytes 6291456 | tf_op jit(solution)/shard_map/all_to_all | solution.py:22
  83.7 38.8 %all-to-all-done.1.refs_0_ = bf16[128,8,1536]{2,1,0:T(8,128)(2,1)} async-done(((bf16[128,8,1536]{2,1,0:T(8,128)(2,1)}), bf16[128,8,1536]{2,1,0:T(8,128)(2,1)}, u32[]{:S(2)}, u32[]{:S(2)}) %all-to-all-start.1) | async-done | bytes 3145760 | tf_op jit(solution)/shard_map/all_to_all | solution.py:22
  122.5 5.2 %conditional.5 = (bf16[128,8,1024]{2,1,0:T(8,128)(2,1)}) conditional(s32[]{:T(128)} %convert_element_type.20, (s32[128]{0:T(128)S(1)}, s32[128]{0:T(128)S(1)}, bf16[128,8,1536]{2,1,0:T(8,128)(2,1)}, bf16[128,8,1024]{2,1,0:T(8,128)(2,1)}) %tuple.46, (pred[128]{0:T(512)(128)(4,1)S(1)}, pred[128]{0:T(512)(128)(4,1)S(1)}, s32[1,256]{1,0:T(1,128)S(1)}, ...), branch_computations={%region_12.13_spmd, %region_13.15_spmd} | conditional | flops 4000103680 | bytes 10527344 | solution.py:204
  122.5 5.2 %pick.3 = bf16[128,8,1024]{2,1,0:T(8,128)(2,1)} custom-call(s32[128]{0:T(128)S(1)} %get-tuple-element.86.kind_ref, s32[128]{0:T(128)S(1)} %get-tuple-element.87.row_ref, bf16[128,8,1536]{2,1,0:T(8,128)(2,1)} %get-tuple-element.88.refs_0_, bf16[128,8,1024]{2,1,0:T(8,128)(2,1)} %get-tuple-element.89.refs_1_), custom_call_target="tpu_custom_call" | custom-call | flops 4000000000 | bytes 4194304 | tf_op jit(solution)/shard_map/cond/branch_0_fun/pick/pallas_call | solution.py:71
  127.7 4.5 %all-to-all-start.3 = ((bf16[128,8,1024]{2,1,0:T(8,128)(2,1)}), bf16[128,8,1024]{2,1,0:T(8,128)(2,1)S(1)}, u32[]{:S(2)}, u32[]{:S(2)}) async-start(bf16[128,8,1024]{2,1,0:T(8,128)(2,1)} %get-tuple-element.149), calls=%async_computation.3 | async-start | bytes 4194304 | tf_op jit(solution)/shard_map/all_to_all | solution.py:22
  132.2 8.6 %pick.5 = bf16[256,8,1024]{2,1,0:T(8,128)(2,1)S(1)} custom-call(s32[256]{0:T(256)S(1)} %rem.70.kind_ref, s32[256]{0:T(256)S(1)} %broadcast_maximum_fusion.row_ref, bf16[128,8,1536]{2,1,0:T(8,128)(2,1)} %all-to-all-done.1.refs_0_), custom_call_target="tpu_custom_call" | custom-call | flops 4000000000 | bytes 8388608 | tf_op jit(solution)/shard_map/pick/pallas_call | solution.py:71
  140.8 2.0 copy-done
  142.8 19.6 %all-to-all-done.3 = bf16[128,8,1024]{2,1,0:T(8,128)(2,1)S(1)} async-done(((bf16[128,8,1024]{2,1,0:T(8,128)(2,1)}), bf16[128,8,1024]{2,1,0:T(8,128)(2,1)S(1)}, u32[]{:S(2)}, u32[]{:S(2)}) %all-to-all-start.3) | async-done | bytes 2097184 | tf_op jit(solution)/shard_map/all_to_all | solution.py:22
  162.4 5.8 %all-to-all-start.4 = ((bf16[128,2,8,1024]{3,2,1,0:T(8,128)(2,1)}), bf16[128,2,8,1024]{3,2,1,0:T(8,128)(2,1)}, u32[]{:S(2)}, u32[]{:S(2)}) async-start(bf16[128,2,8,1024]{3,2,1,0:T(8,128)(2,1)} %bitcast.30), calls=%async_computation.4 | async-start | bytes 8388608 | tf_op jit(solution)/shard_map/all_to_all | solution.py:22
  168.9 3.8 %bitcast_select_fusion = bf16[1024,1024]{1,0:T(8,128)(2,1)} fusion(bf16[1,1024,1024]{2,1,0:T(8,128)(2,1)} %param.14, bf16[128,8,1024]{2,1,0:T(8,128)(2,1)S(1)} %all-to-all-done.3, pred[]{:T(512)} %compare_reduce_fusion.2), kind=kLoop, calls=%fused_computation.38 | loop fusion | flops 1048576 | bytes 6291457 | tf_op jit(solution)/shard_map/jit(_where)/select_n | solution.py:218
  174.1 3.8 %bitcast_select_fusion.1 = bf16[1,1024,1024]{2,1,0:T(8,128)(2,1)} fusion(bf16[1,1024,1024]{2,1,0:T(8,128)(2,1)} %param.14, bf16[128,8,1024]{2,1,0:T(8,128)(2,1)S(1)} %all-to-all-done.3, pred[]{:T(512)} %compare_reduce_fusion.2), kind=kLoop, calls=%fused_computation.39 | loop fusion | flops 1048576 | bytes 6291457 | tf_op jit(solution)/shard_map/jit(_where)/select_n | solution.py:218
  178.1 5.7 %multiply_reduce_fusion = (f32[]{:T(128)}, f32[512,1024]{1,0:T(8,128)S(1)}) fusion(bf16[1024,1024]{1,0:T(8,128)(2,1)} %collective-permute-done.2, bf16[1024,1024]{1,0:T(8,128)(2,1)} %bitcast_select_fusion, pred[]{:T(512)S(6)} %eq.75, s32[]{:T(128)S(6)} %select_n.173, bf16[512,1024]{1,0:T(8,128)(2,1)} %copy-done.3, bf16[512,1024]{1,0:T(8,128)(2,1)S(1)} %get-tuple-element.138), kind=kOutput, calls=%fused_computation.41 | convolution fusion | flops 2154823680 | bytes 10487300 | tf_op jit(solution)/shard_map/dot_general | solution.py:235
  187.8 33.4 %all-to-all-done.4 = bf16[128,2,8,1024]{3,2,1,0:T(8,128)(2,1)} async-done(((bf16[128,2,8,1024]{3,2,1,0:T(8,128)(2,1)}), bf16[128,2,8,1024]{3,2,1,0:T(8,128)(2,1)}, u32[]{:S(2)}, u32[]{:S(2)}) %all-to-all-start.4) | async-done | bytes 4194336 | tf_op jit(solution)/shard_map/all_to_all | solution.py:22
  221.1 5.8 %copy_bitcast_fusion = bf16[2,1024,1024]{2,1,0:T(8,128)(2,1)} fusion(bf16[128,2,8,1024]{3,2,1,0:T(8,128)(2,1)} %all-to-all-done.4, pred[2]{0:T(512)(128)(4,1)S(1)} %dynamic-slice_compare_fusion), kind=kLoop, calls=%fused_computation.34 | loop fusion | flops 2097152 | bytes 8388610 | tf_op jit(solution)/shard_map/reshape | solution.py:247
  (48 shorter events, 15.0 us)
Async XLA Ops:
  0.6 23.8 %collective-permute-start = (bf16[512,1024]{1,0:T(8,128)(2,1)}, bf16[512,1024]{1,0:T(8,128)(2,1)}, u32[]{:S(2)}, u32[]{:S(2)}) collective-permute-start(bf16[512,1024]{1,0:T(8,128)(2,1)} %param.12), channel_id=1, source_target_pairs={{0,1},{1,0},{2,3},{3,2},{4,5},{5,4},{6,7},{7,6},{8,9},{9,8},{10,11... | collective-permute-start | bytes 3145736 | tf_op jit(solution)/shard_map/ppermute | solution.py:18
  9.2 12.2 %copy-start.4 = (s32[256]{0:T(256)S(1)}, s32[256]{0:T(256)}, u32[]{:S(2)}) copy-start(s32[256]{0:T(256)} %param.16) | copy-start | bytes 3076
  9.2 12.6 %copy-start.5 = (s32[256]{0:T(256)S(1)}, s32[256]{0:T(256)}, u32[]{:S(2)}) copy-start(s32[256]{0:T(256)} %param.17) | copy-start | bytes 3076
  10.3 29.8 %collective-permute-start.1 = (bf16[1024,512]{1,0:T(8,128)(2,1)}, bf16[1024,512]{1,0:T(8,128)(2,1)}, u32[]{:S(2)}, u32[]{:S(2)}) collective-permute-start(bf16[1024,512]{1,0:T(8,128)(2,1)} %broadcast_select_fusion), channel_id=1, source_target_pairs={{0,1},{1,0},{2,3},{3,2},{4,5},{5,4},{6,7},{7,6},{8,9},{9,8},{10,11... | collective-permute-start | bytes 3145736 | tf_op jit(solution)/shard_map/ppermute | solution.py:18
  10.3 40.8 %all-to-all-start.2 = ((bf16[128,8,1024]{2,1,0:T(8,128)(2,1)}), bf16[128,8,1024]{2,1,0:T(8,128)(2,1)}, u32[]{:S(2)}, u32[]{:S(2)}) async-start(bf16[128,8,1024]{2,1,0:T(8,128)(2,1)} %get-tuple-element.137), calls=%async_computation.2 | async-start | bytes 4194304 | tf_op jit(solution)/shard_map/all_to_all | solution.py:22
  26.2 1.0 copy-start.3
  40.1 1.6 copy-start.2
  51.1 71.3 %all-to-all-start.1 = ((bf16[128,8,1536]{2,1,0:T(8,128)(2,1)}), bf16[128,8,1536]{2,1,0:T(8,128)(2,1)}, u32[]{:S(2)}, u32[]{:S(2)}) async-start(bf16[128,8,1536]{2,1,0:T(8,128)(2,1)} %maximum_bitcast_fusion), calls=%async_computation.1 | async-start | bytes 6291456 | tf_op jit(solution)/shard_map/all_to_all | solution.py:22
  127.7 34.7 %all-to-all-start.3 = ((bf16[128,8,1024]{2,1,0:T(8,128)(2,1)}), bf16[128,8,1024]{2,1,0:T(8,128)(2,1)S(1)}, u32[]{:S(2)}, u32[]{:S(2)}) async-start(bf16[128,8,1024]{2,1,0:T(8,128)(2,1)} %get-tuple-element.149), calls=%async_computation.3 | async-start | bytes 4194304 | tf_op jit(solution)/shard_map/all_to_all | solution.py:22
  140.8 2.0 copy-start
  162.4 58.7 %all-to-all-start.4 = ((bf16[128,2,8,1024]{3,2,1,0:T(8,128)(2,1)}), bf16[128,2,8,1024]{3,2,1,0:T(8,128)(2,1)}, u32[]{:S(2)}, u32[]{:S(2)}) async-start(bf16[128,2,8,1024]{3,2,1,0:T(8,128)(2,1)} %bitcast.30), calls=%async_computation.4 | async-start | bytes 8388608 | tf_op jit(solution)/shard_map/all_to_all | solution.py:22
  172.7 5.4 %collective-permute-start.2 = (bf16[1024,1024]{1,0:T(8,128)(2,1)}, bf16[1024,1024]{1,0:T(8,128)(2,1)}, u32[]{:S(2)}, u32[]{:S(2)}) collective-permute-start(bf16[1024,1024]{1,0:T(8,128)(2,1)} %bitcast_select_fusion), channel_id=1, source_target_pairs={{0,1},{1,0},{2,3},{3,2},{4,5},{5,4},{6,7},{7,6},{8,9},{9,8},{10,11... | collective-permute-start | bytes 6291464 | tf_op jit(solution)/shard_map/ppermute | solution.py:18
  183.8 1.5 collective-permute-start.3

commit v2 on v1

--- a/solution.py
+++ b/solution.py
@@ -29,21 +29,25 @@
     tables, out_ref, sem = refs[:-2], refs[-2], refs[-1]
     half = width // 2
 
+    def start(src, dst):
+        pltpu.make_async_copy(src, dst, sem).start()
+
     def issue(item, carry):
-        kind, row = kind_ref[item], row_ref[item]
-
-        def start(src, dst):
-            pltpu.make_async_copy(src, dst, sem).start()
-
-        @pl.when(kind == OWN)
+        row = row_ref[item]
+        if len(tables) == 1:
+            start(tables[0].at[row, :, pl.ds(0, width)], out_ref.at[item])
+            return carry
+        kind = kind_ref[item]
+
+        @pl.when(kind == FIRST)
         def _():
-            start(tables[0].at[row, :, pl.ds(0, width)], out_ref.at[item])
-
-        if len(tables) > 1:
-
-            @pl.when(kind == FIRST)
+            start(tables[1].at[row], out_ref.at[item])
+
+        @pl.when(kind != FIRST)
+        def _():
+            @pl.when(kind == OWN)
             def _():
-                start(tables[1].at[row], out_ref.at[item])
+                start(tables[0].at[row, :, pl.ds(0, width)], out_ref.at[item])
 
             @pl.when(kind == SHARED)
             def _():
@@ -53,20 +57,20 @@
                         out_ref.at[item, :, pl.ds(core * half, half)],
                     )
 
-        if len(tables) > 2:
-
-            @pl.when(kind == EXTRA)
-            def _():
-                start(tables[2].at[row], out_ref.at[item])
+            if len(tables) > 2:
+
+                @pl.when(kind == EXTRA)
+                def _():
+                    start(tables[2].at[row], out_ref.at[item])
 
         return carry
 
-    lax.fori_loop(0, out_ref.shape[0], issue, 0, unroll=4)
+    lax.fori_loop(0, out_ref.shape[0], issue, 0, unroll=8)
     pltpu.make_async_copy(out_ref, out_ref, sem).wait()
 
 
 def pick(kind, row, width, *tables):
-    items, piece_rows = kind.shape[0], tables[0].shape[1]
+    items, piece_rows = row.shape[0], tables[0].shape[1]
     out_bytes = items * piece_rows * width * 2
     return pl.pallas_call(
         functools.partial(pick_kernel, width),
@@ -83,6 +87,26 @@
     )(kind, row, *tables)
 
 
+def first_kernel(index_ref, stat_ref, pending_ref, out_ref, sem):
+    slot = jnp.where(stat_ref[index_ref[0] * 2] >= 0, 0, 1)
+    copy = pltpu.make_async_copy(pending_ref.at[slot], out_ref, sem)
+    copy.start()
+    copy.wait()
+
+
+def first_used(my_index, pending_stat, pending_roots):
+    return pl.pallas_call(
+        first_kernel,
+        out_shape=jax.ShapeDtypeStruct(pending_roots.shape[1:], pending_roots.dtype),
+        in_specs=[pl.BlockSpec(memory_space=pltpu.SMEM)] * 2
+        + [pl.BlockSpec(memory_space=pl.ANY)],
+        out_specs=pl.BlockSpec(memory_space=pltpu.VMEM),
+        scratch_shapes=[pltpu.SemaphoreType.DMA],
+        compiler_params=pltpu.CompilerParams(vmem_limit_bytes=8 * 1024 * 1024),
+        name="first_used",
+    )(my_index.reshape(1), pending_stat, pending_roots)
+
+
 def poly_times(first, second):
     result = [0.0] * (len(first) + len(second) - 1)
     for left_pos in range(len(first)):
@@ -103,27 +127,149 @@
     return [float(value) for value in x_poly]
 
 
-def matmul_exact(first, second):
-    return jnp.dot(first, second, preferred_element_type=jnp.float32)
-
-
-def inverse_root(statistic):
-    size_b = statistic.shape[0]
-    identity = jnp.eye(size_b, dtype=jnp.float32)
-    norm_scale = 2.0 * jnp.trace(statistic) / size_b
-    scaled = statistic / norm_scale
-    coefficients = root_polynomial(ITERS)
-    scaled_sq = matmul_exact(scaled, scaled)
-    scaled_cube = matmul_exact(scaled_sq, scaled)
-    lower_part = coefficients[0] * identity + coefficients[1] * scaled + coefficients[2] * scaled_sq
-    upper_part = (
-        coefficients[3] * identity
-        + coefficients[4] * scaled
-        + coefficients[5] * scaled_sq
-        + coefficients[6] * scaled_cube
-    )
-    polynomial = lower_part + matmul_exact(scaled_cube, upper_part)
-    return polynomial * norm_scale ** (-0.25)
+TILE = 256
+
+
+def root_kernel(
+    flag_ref,
+    gram_ref,
+    stat_ref,
+    pending_ref,
+    other_ref,
+    new_ref,
+    own_ref,
+    scaled_ref,
+    scaled16_ref,
+    square_ref,
+    square16_ref,
+    cube16_ref,
+    upper_ref,
+    diagonal_ref,
+    sems,
+):
+    width = stat_ref.shape[0]
+    half = width // 2
+    refreshed, from_other, parity = flag_ref[0], flag_ref[1], flag_ref[2]
+    poly = root_polynomial(ITERS)
+    shared = own_ref.at[:, pl.ds(width, half)]
+
+    @pl.when(from_other > 0)
+    def _():
+        pltpu.make_async_copy(other_ref, shared, sems.at[0]).start()
+
+    @pl.when(from_other == 0)
+    def _():
+        columns = pl.ds(pl.multiple_of(parity * half, half), half)
+        pltpu.make_async_copy(pending_ref.at[1, :, columns], shared, sems.at[0]).start()
+
+    second = pltpu.make_async_copy(pending_ref.at[1], own_ref.at[:, pl.ds(0, width)], sems.at[1])
+
+    @pl.when(refreshed == 0)
+    def _():
+        second.start()
+
+    diagonal_ref[...] = jnp.zeros_like(diagonal_ref)
+
+    @pl.loop(0, width // 128)
+    def _(step):
+        rows = pl.ds(pl.multiple_of(step * 128, 128), 128)
+        new_ref[rows, :] = decay_rate * stat_ref[rows, :] + (1.0 - decay_rate) * gram_ref[rows, :]
+        on_diagonal = lax.broadcasted_iota(jnp.int32, (128, 128), 0) == lax.broadcasted_iota(
+            jnp.int32, (128, 128), 1
+        )
+        diagonal_ref[...] += jnp.where(on_diagonal, new_ref[rows, rows], 0.0)
+
+    @pl.when(refreshed > 0)
+    def _():
+        trace = jnp.sum(jnp.sum(diagonal_ref[...], axis=1, keepdims=True), axis=0, keepdims=True)
+        norm_scale = 2.0 * trace / width
+        factor = lax.rsqrt(jnp.sqrt(norm_scale))
+
+        @pl.loop(0, width // 128)
+        def _(step):
+            rows = pl.ds(pl.multiple_of(step * 128, 128), 128)
+            scaled = new_ref[rows, :] / norm_scale
+            scaled_ref[rows, :] = scaled
+            scaled16_ref[rows, :] = scaled.astype(jnp.bfloat16)
+
+        def columns_of(step):
+            return pl.ds(pl.multiple_of(step * TILE, TILE), TILE)
+
+        def identity(step):
+            return (
+                lax.broadcasted_iota(jnp.int32, (width, TILE), 0)
+                == lax.broadcasted_iota(jnp.int32, (width, TILE), 1) + step * TILE
+            )
+
+        def dot(first, second):
+            return jnp.dot(first, second, preferred_element_type=jnp.float32)
+
+        @pl.loop(0, width // TILE)
+        def _(step):
+            columns = columns_of(step)
+            square = dot(scaled16_ref[...], scaled16_ref[:, columns])
+            square_ref[:, columns] = square
+            square16_ref[:, columns] = square.astype(jnp.bfloat16)
+
+        @pl.loop(0, width // TILE)
+        def _(step):
+            columns = columns_of(step)
+            cube = dot(square16_ref[...], scaled16_ref[:, columns])
+            cube16_ref[:, columns] = cube.astype(jnp.bfloat16)
+            upper = (
+                jnp.where(identity(step), poly[3], 0.0)
+                + poly[4] * scaled_ref[:, columns]
+                + poly[5] * square_ref[:, columns]
+                + poly[6] * cube
+            )
+            upper_ref[:, columns] = upper.astype(jnp.bfloat16)
+
+        @pl.loop(0, width // TILE)
+        def _(step):
+            columns = columns_of(step)
+            total = dot(cube16_ref[...], upper_ref[:, columns])
+            total += (
+                jnp.where(identity(step), poly[0], 0.0)
+                + poly[1] * scaled_ref[:, columns]
+                + poly[2] * square_ref[:, columns]
+            )
+            own_ref[:, columns] = (total * factor).astype(jnp.bfloat16)
+
+    @pl.when(refreshed == 0)
+    def _():
+        second.wait()
+
+    pltpu.make_async_copy(other_ref, shared, sems.at[0]).wait()
+
+
+def updated_and_root(flags, gram, statistic, pending_roots, other_columns):
+    width = statistic.shape[0]
+    vmem = pl.BlockSpec(memory_space=pltpu.VMEM)
+    anywhere = pl.BlockSpec(memory_space=pl.ANY)
+    return pl.pallas_call(
+        root_kernel,
+        out_shape=(
+            jax.ShapeDtypeStruct((width, width), jnp.float32),
+            jax.ShapeDtypeStruct((width, width + width // 2), jnp.bfloat16),
+        ),
+        in_specs=[pl.BlockSpec(memory_space=pltpu.SMEM), vmem, vmem, anywhere, anywhere],
+        out_specs=(vmem, vmem),
+        scratch_shapes=[
+            pltpu.VMEM((width, width), jnp.float32),
+            pltpu.VMEM((width, width), jnp.bfloat16),
+            pltpu.VMEM((width, width), jnp.float32),
+            pltpu.VMEM((width, width), jnp.bfloat16),
+            pltpu.VMEM((width, width), jnp.bfloat16),
+            pltpu.VMEM((width, width), jnp.bfloat16),
+            pltpu.VMEM((128, 128), jnp.float32),
+            pltpu.SemaphoreType.DMA((2,)),
+        ],
+        compiler_params=pltpu.CompilerParams(vmem_limit_bytes=44 * 1024 * 1024),
+        cost_estimate=pl.CostEstimate(
+            flops=6 * width**3, bytes_accessed=15 * width * width, transcendentals=0
+        ),
+        name="root",
+    )(flags, gram, statistic, pending_roots, other_columns)
 
 
 def per_device(gradient, statistics, held_roots, pending_roots, pending_stat, refresh_stat):
@@ -145,10 +291,7 @@
     sharing_pairs = sharing.reshape(devices // 2, 2)
     unplaced = jnp.any(sharing_pairs[:, 0] & sharing_pairs[:, 1])
 
-    my_first = lax.dynamic_slice_in_dim(pending_stat, my_index * slot_count, 1, 0)[0] >= 0
-    first_root = lax.dynamic_index_in_dim(
-        pending_roots, jnp.where(my_first, 0, 1), 0, keepdims=False
-    )
+    first_root = first_used(my_index, pending_stat, pending_roots)
     first_parts = spread(first_root.reshape(devices, piece_rows, block_width))
 
     other_half = swapped(gradient, "dev", 0)
@@ -164,24 +307,22 @@
             full_grad, full_grad, (((0,), (0,)), ((), ())), preferred_element_type=jnp.float32
         ),
     )
-    new_stat = decay_rate * statistics[0] + (1.0 - decay_rate) * gram_term
-
     second_root = pending_roots[1]
     my_refreshed = jnp.any(refresh_stat == my_index)
     first_of_pair = lax.dynamic_slice_in_dim(sharing, my_index - parity, 1, 0)[0]
     from_other = jnp.where(first_of_pair, parity == 1, parity == 0)
-    left_columns, right_columns = second_root[:, :half_columns], second_root[:, half_columns:]
-    other_columns = swapped(jnp.where(parity == 0, right_columns, left_columns), "dev", 0)
-    own_columns = jnp.where(parity == 0, left_columns, right_columns)
-    shared_columns = jnp.where(from_other, other_columns, own_columns)
-    own_matrix = lax.cond(
-        my_refreshed, lambda: inverse_root(new_stat).astype(jnp.bfloat16), lambda: second_root
-    )
-    root_parts = spread(
-        jnp.concatenate([own_matrix, shared_columns], axis=1).reshape(
-            devices, piece_rows, block_width + half_columns
-        ),
-    )
+    other_columns = swapped(
+        lax.dynamic_slice(
+            pending_roots, (1, 0, (1 - parity) * half_columns), (1, block_width, half_columns)
+        )[0],
+        "dev",
+        0,
+    )
+    flags = jnp.stack([my_refreshed, from_other, parity]).astype(jnp.int32)
+    new_stat, own_matrix = updated_and_root(
+        flags, gram_term, statistics[0], pending_roots, other_columns
+    )
+    root_parts = spread(own_matrix.reshape(devices, piece_rows, block_width + half_columns))
 
     slot_match = pending_stat[None, :] == device_ids[:, None]
     slot_of = jnp.sum(

time: 228 us -> 205 us (0.90)
  starting transfers between devices: 54.5 us -> 36.9 us
  Pallas kernels: 13.7 us -> 24.5 us
  other arithmetic: 29.1 us -> 19.2 us
  local copies, waits for them, and re-layouts: 14 us -> 9.72 us
    all_to_all x4, starting transfers between devices: 51.3 us -> 32.6 us  [spread(): return lax.all_to_all(parts, 'dev', split_axis=0, concat_axis=0, tiled=True)]
    pallas_call x0 -> x2, Pallas kernels: none -> 10.7 us  [the longest x1 7.23 us: updated_and_root(): pl.pallas_call(root_kernel, out_shape=(jax.ShapeDtypeStruct((width, width...]
    add x1 -> x0, other arithmetic: 6.97 us -> none  [per_device(): new_stat = decay_rate * statistics[0] + (1.0 - decay_rate) * gram_term]
    slice x1 -> x0, local copies, waits for them, and re-layouts: 5.23 us -> none  [per_device(): second_root = pending_roots[1]]
    unnamed x10 -> x12, local copies, waits for them, and re-layouts: 4.42 us -> 5.77 us
  transfers between devices with their start and end apart: 8 -> 8, of which waited for: 6 -> 6; matrix products, arithmetic and copies ran while one was open for 19% -> 13% of each run, Pallas kernels for 4% -> 9%
where the time goes in v2:
time: 205 us; the launch traced here: 204 us
  waiting for transfers between devices  99.6 us (49%)
  starting transfers between devices  36.9 us (18%)
  Pallas kernels  24.5 us (12%)
  other arithmetic  19.2 us (9%)
  matrix products  10.1 us (5%)
  local copies, waits for them, and re-layouts  9.72 us (5%)
  between operations  4.16 us (2%)
    all_to_all x4, waiting for transfers between devices, spread(): return lax.all_to_all(parts, 'dev', split_axis=0, concat_axis=0, tiled=True)  98.3 us
    all_to_all x4, starting transfers between devices, spread(): return lax.all_to_all(parts, 'dev', split_axis=0, concat_axis=0, tiled=True)  32.6 us
    pallas_call x2, Pallas kernels, pick(): pl.pallas_call(functools.partial(pick_kernel, width), out_shape=jax.Shape...  13.8 us
    select_n x2, other arithmetic, per_device(): merged = jnp.where(my_found, returned, held_roots[0])  7.61 us
    pallas_call x1, Pallas kernels, updated_and_root(): pl.pallas_call(root_kernel, out_shape=(jax.ShapeDtypeStruct((width, width...  7.23 us
    reshape x1, other arithmetic, per_device(): fresh_roots = jnp.where((my_slots >= 0)[:, None, None, None], fresh.trans...  5.79 us
    unnamed x12, local copies, waits for them, and re-layouts  5.77 us
    dot_general x1, matrix products, per_device(): jnp.dot(left_times, right_root, preferred_element_type=jnp.float32)  5.68 us
  transfers between devices with their start and end apart: 8, of which 6 were waited for; matrix products, arithmetic and copies ran while one was open for 13% of the time, Pallas kernels for 9%

profile of v2, /device:TPU:1, one launch (start us, length us, event | category | flops | bytes accessed | tf_op | source)
XLA Modules:
  0.0 204.2 jit_solution(15575015784357870542)
XLA Ops:
  0.6 1.5 collective-permute-start
  2.8 3.5 %first_used.1 = bf16[1024,1024]{1,0:T(8,128)(2,1)} custom-call(s32[1]{0:T(128)} %bitcast.9.index_ref, s32[256]{0:T(256)S(1)} %copy-done.1, bf16[2,1024,1024]{2,1,0:T(8,128)(2,1)} %pending_ref.3), custom_call_target="tpu_custom_call" | custom-call | tf_op jit(solution)/shard_map/first_used/pallas_call | solution.py:98
  6.2 10.7 %all-to-all-start.2 = ((bf16[128,8,1024]{2,1,0:T(8,128)(2,1)}), bf16[128,8,1024]{2,1,0:T(8,128)(2,1)}, u32[]{:S(2)}, u32[]{:S(2)}) async-start(bf16[128,8,1024]{2,1,0:T(8,128)(2,1)} %bitcast.10), calls=%async_computation.2 | async-start | bytes 4194304 | tf_op jit(solution)/shard_map/all_to_all | solution.py:22
  17.0 2.3 %dynamic-slice_bitcast_fusion = bf16[1024,512]{1,0:T(8,128)(2,1)} fusion(bf16[2,1024,1024]{2,1,0:T(8,128)(2,1)} %pending_ref.3, s32[]{:T(128)S(6)} %select_n.121), kind=kLoop, calls=%fused_computation.21 | loop fusion | bytes 2097156 | tf_op jit(solution)/shard_map/squeeze | solution.py:315
  23.5 1.7 broadcast_select_fusion.1
  26.3 4.4 %conditional.2 = (f32[1024,1024]{1,0:T(8,128)}) conditional(s32[]{:T(128)} %convert_element_type.14, bf16[1024,1024]{1,0:T(8,128)(2,1)S(1)} %pad_maximum_fusion, bf16[1024,1024]{1,0:T(8,128)(2,1)S(1)} %pad_maximum_fusion), branch_computations={%region_2.3_spmd, %region_3.4_spmd} | conditional | flops 2147483648 | bytes 6291464 | solution.py:301
  26.3 4.4 %fusion.10 = f32[1024,1024]{1,0:T(8,128)} fusion(bf16[1024,1024]{1,0:T(8,128)(2,1)S(1)} %param), kind=kOutput, calls=%fused_computation.56 | convolution fusion | flops 2147483648 | bytes 6291456 | tf_op jit(solution)/shard_map/cond/branch_0_fun/dot_general | solution.py:306
  30.7 2.2 %copy-done.3 = f32[1,1024,1024]{2,1,0:T(8,128)S(1)} copy-done((f32[1,1024,1024]{2,1,0:T(8,128)S(1)}, f32[1,1024,1024]{2,1,0:T(8,128)}, u32[]{:S(2)}) %copy-start.3) | copy-done | bytes 4194328
  32.9 7.2 %root.1 = (f32[1024,1024]{1,0:T(8,128)}, bf16[1024,1536]{1,0:T(8,128)(2,1)}) custom-call(s32[3]{0:T(128)S(1)} %pad_add_fusion.flag_ref, f32[1024,1024]{1,0:T(8,128)} %get-tuple-element.124.gram_ref, f32[1024,1024]{1,0:T(8,128)S(1)} %bitcast.30, bf16[2,1024,1024]{2,1,0:T(8,128)(2,1)} %pending_ref.3, bf16[1024,512]{1,0:T(8,128)(2,1)S(1)} %collective-permute-done.1.other_ref), custom_call_target="tpu_custom_call" | custom-call | flops 6442450944 | bytes 15728640 | tf_op jit(solution)/shard_map/root/pallas_call | solution.py:249
  40.2 6.5 %all-to-all-done.2 = bf16[128,8,1024]{2,1,0:T(8,128)(2,1)} async-done(((bf16[128,8,1024]{2,1,0:T(8,128)(2,1)}), bf16[128,8,1024]{2,1,0:T(8,128)(2,1)}, u32[]{:S(2)}, u32[]{:S(2)}) %all-to-all-start.2) | async-done | bytes 2097184 | tf_op jit(solution)/shard_map/all_to_all | solution.py:22
  46.7 11.6 %all-to-all-start.1 = ((bf16[128,8,1536]{2,1,0:T(8,128)(2,1)}), bf16[128,8,1536]{2,1,0:T(8,128)(2,1)}, u32[]{:S(2)}, u32[]{:S(2)}) async-start(bf16[128,8,1536]{2,1,0:T(8,128)(2,1)} %bitcast.8), calls=%async_computation.1 | async-start | bytes 6291456 | tf_op jit(solution)/shard_map/all_to_all | solution.py:22
  60.9 38.8 %all-to-all-done.1.refs_0_ = bf16[128,8,1536]{2,1,0:T(8,128)(2,1)} async-done(((bf16[128,8,1536]{2,1,0:T(8,128)(2,1)}), bf16[128,8,1536]{2,1,0:T(8,128)(2,1)}, u32[]{:S(2)}, u32[]{:S(2)}) %all-to-all-start.1) | async-done | bytes 3145760 | tf_op jit(solution)/shard_map/all_to_all | solution.py:22
  99.7 5.3 %conditional.3 = (bf16[128,8,1024]{2,1,0:T(8,128)(2,1)}) conditional(s32[]{:T(128)} %convert_element_type.15, (s32[128]{0:T(128)S(1)}, s32[128]{0:T(128)S(1)}, bf16[128,8,1536]{2,1,0:T(8,128)(2,1)}, bf16[128,8,1024]{2,1,0:T(8,128)(2,1)}) %tuple.39, (pred[128]{0:T(512)(128)(4,1)S(1)}, pred[128]{0:T(512)(128)(4,1)S(1)}, ...), branch_computations={%region_9.10_spmd, %region_10.12_spmd} | conditional | flops 4000101376 | bytes 14721132 | solution.py:345
  99.7 5.2 %pick.3 = bf16[128,8,1024]{2,1,0:T(8,128)(2,1)} custom-call(s32[128]{0:T(128)S(1)} %get-tuple-element.69.kind_ref, s32[128]{0:T(128)S(1)} %get-tuple-element.70.row_ref, bf16[128,8,1536]{2,1,0:T(8,128)(2,1)} %get-tuple-element.71.refs_0_, bf16[128,8,1024]{2,1,0:T(8,128)(2,1)} %get-tuple-element.72.refs_1_), custom_call_target="tpu_custom_call" | custom-call | flops 4000000000 | bytes 4194304 | tf_op jit(solution)/shard_map/cond/branch_0_fun/pick/pallas_call | solution.py:75
  104.9 4.5 %all-to-all-start.3 = ((bf16[128,8,1024]{2,1,0:T(8,128)(2,1)}), bf16[128,8,1024]{2,1,0:T(8,128)(2,1)S(1)}, u32[]{:S(2)}, u32[]{:S(2)}) async-start(bf16[128,8,1024]{2,1,0:T(8,128)(2,1)} %get-tuple-element.125), calls=%async_computation.3 | async-start | bytes 4194304 | tf_op jit(solution)/shard_map/all_to_all | solution.py:22
  109.4 8.6 %pick.5 = bf16[256,8,1024]{2,1,0:T(8,128)(2,1)S(1)} custom-call(s32[256]{0:T(256)S(1)} %rem.70.kind_ref, s32[256]{0:T(256)S(1)} %broadcast_maximum_fusion.row_ref, bf16[128,8,1536]{2,1,0:T(8,128)(2,1)} %all-to-all-done.1.refs_0_), custom_call_target="tpu_custom_call" | custom-call | flops 4000000000 | bytes 8388608 | tf_op jit(solution)/shard_map/pick/pallas_call | solution.py:75
  118.0 2.0 copy-done
  120.0 19.6 %all-to-all-done.3 = bf16[128,8,1024]{2,1,0:T(8,128)(2,1)S(1)} async-done(((bf16[128,8,1024]{2,1,0:T(8,128)(2,1)}), bf16[128,8,1024]{2,1,0:T(8,128)(2,1)S(1)}, u32[]{:S(2)}, u32[]{:S(2)}) %all-to-all-start.3) | async-done | bytes 2097184 | tf_op jit(solution)/shard_map/all_to_all | solution.py:22
  139.7 5.8 %all-to-all-start.4 = ((bf16[128,2,8,1024]{3,2,1,0:T(8,128)(2,1)}), bf16[128,2,8,1024]{3,2,1,0:T(8,128)(2,1)}, u32[]{:S(2)}, u32[]{:S(2)}) async-start(bf16[128,2,8,1024]{3,2,1,0:T(8,128)(2,1)} %bitcast.29), calls=%async_computation.4 | async-start | bytes 8388608 | tf_op jit(solution)/shard_map/all_to_all | solution.py:22
  146.1 3.8 %bitcast_select_fusion = bf16[1024,1024]{1,0:T(8,128)(2,1)} fusion(bf16[1,1024,1024]{2,1,0:T(8,128)(2,1)} %param.12, bf16[128,8,1024]{2,1,0:T(8,128)(2,1)S(1)} %all-to-all-done.3, pred[]{:T(512)} %compare_reduce_fusion.1), kind=kLoop, calls=%fused_computation.11 | loop fusion | flops 1048576 | bytes 6291457 | tf_op jit(solution)/shard_map/jit(_where)/select_n | solution.py:359
  151.3 3.8 %bitcast_select_fusion.1 = bf16[1,1024,1024]{2,1,0:T(8,128)(2,1)} fusion(bf16[1,1024,1024]{2,1,0:T(8,128)(2,1)} %param.12, bf16[128,8,1024]{2,1,0:T(8,128)(2,1)S(1)} %all-to-all-done.3, pred[]{:T(512)} %compare_reduce_fusion.1), kind=kLoop, calls=%fused_computation.12 | loop fusion | flops 1048576 | bytes 6291457 | tf_op jit(solution)/shard_map/jit(_where)/select_n | solution.py:359
  155.4 5.7 %multiply_reduce_fusion = (f32[]{:T(128)}, f32[512,1024]{1,0:T(8,128)S(1)}) fusion(bf16[1024,1024]{1,0:T(8,128)(2,1)} %collective-permute-done.2, bf16[1024,1024]{1,0:T(8,128)(2,1)} %bitcast_select_fusion, pred[]{:T(512)S(6)} %eq.70, s32[]{:T(128)S(6)} %select_n.134, bf16[512,1024]{1,0:T(8,128)(2,1)} %copy-done.4, bf16[512,1024]{1,0:T(8,128)(2,1)S(1)} %get-tuple-element.115), kind=kOutput, calls=%fused_computation.14 | convolution fusion | flops 2154823680 | bytes 10487300 | tf_op jit(solution)/shard_map/dot_general | solution.py:376
  165.0 33.3 %all-to-all-done.4 = bf16[128,2,8,1024]{3,2,1,0:T(8,128)(2,1)} async-done(((bf16[128,2,8,1024]{3,2,1,0:T(8,128)(2,1)}), bf16[128,2,8,1024]{3,2,1,0:T(8,128)(2,1)}, u32[]{:S(2)}, u32[]{:S(2)}) %all-to-all-start.4) | async-done | bytes 4194336 | tf_op jit(solution)/shard_map/all_to_all | solution.py:22
  198.4 5.8 %copy_bitcast_fusion = bf16[2,1024,1024]{2,1,0:T(8,128)(2,1)} fusion(bf16[128,2,8,1024]{3,2,1,0:T(8,128)(2,1)} %all-to-all-done.4, pred[2]{0:T(512)(128)(4,1)S(1)} %dynamic-slice_compare_fusion), kind=kLoop, calls=%fused_computation.8 | loop fusion | flops 2097152 | bytes 8388610 | tf_op jit(solution)/shard_map/reshape | solution.py:388
  (47 shorter events, 11.5 us)
Async XLA Ops:
  0.6 22.9 %collective-permute-start = (bf16[512,1024]{1,0:T(8,128)(2,1)}, bf16[512,1024]{1,0:T(8,128)(2,1)}, u32[]{:S(2)}, u32[]{:S(2)}) collective-permute-start(bf16[512,1024]{1,0:T(8,128)(2,1)} %param.10), channel_id=1, source_target_pairs={{0,1},{1,0},{2,3},{3,2},{4,5},{5,4},{6,7},{7,6},{8,9},{9,8},{10,11... | collective-permute-start | bytes 3145736 | tf_op jit(solution)/shard_map/ppermute | solution.py:18
  2.1 0.7 copy-start.1
  6.2 40.4 %all-to-all-start.2 = ((bf16[128,8,1024]{2,1,0:T(8,128)(2,1)}), bf16[128,8,1024]{2,1,0:T(8,128)(2,1)}, u32[]{:S(2)}, u32[]{:S(2)}) async-start(bf16[128,8,1024]{2,1,0:T(8,128)(2,1)} %bitcast.10), calls=%async_computation.2 | async-start | bytes 4194304 | tf_op jit(solution)/shard_map/all_to_all | solution.py:22
  16.9 3.5 %copy-start.2 = (s32[256]{0:T(256)S(1)}, s32[256]{0:T(256)}, u32[]{:S(2)}) copy-start(s32[256]{0:T(256)} %stat_ref.1) | copy-start | bytes 3076
  17.0 3.8 %copy-start.5 = (s32[256]{0:T(256)S(1)}, s32[256]{0:T(256)}, u32[]{:S(2)}) copy-start(s32[256]{0:T(256)} %param.15) | copy-start | bytes 3076
  19.2 11.5 %collective-permute-start.1 = (bf16[1024,512]{1,0:T(8,128)(2,1)}, bf16[1024,512]{1,0:T(8,128)(2,1)S(1)}, u32[]{:S(2)}, u32[]{:S(2)}) collective-permute-start(bf16[1024,512]{1,0:T(8,128)(2,1)} %dynamic-slice_bitcast_fusion), channel_id=1, source_target_pairs={{0,1},{1,0},{2,3},{3,2},{4,5},{5,4},{6,7},{7,6},{8,9},{9,8},{10,11... | collective-permute-start | bytes 3145736 | tf_op jit(solution)/shard_map/ppermute | solution.py:18
  25.2 1.1 copy-start.4
  30.7 2.2 %copy-start.3 = (f32[1,1024,1024]{2,1,0:T(8,128)S(1)}, f32[1,1024,1024]{2,1,0:T(8,128)}, u32[]{:S(2)}) copy-start(f32[1,1024,1024]{2,1,0:T(8,128)} %param.11) | copy-start | bytes 12582916
  46.7 53.0 %all-to-all-start.1 = ((bf16[128,8,1536]{2,1,0:T(8,128)(2,1)}), bf16[128,8,1536]{2,1,0:T(8,128)(2,1)}, u32[]{:S(2)}, u32[]{:S(2)}) async-start(bf16[128,8,1536]{2,1,0:T(8,128)(2,1)} %bitcast.8), calls=%async_computation.1 | async-start | bytes 6291456 | tf_op jit(solution)/shard_map/all_to_all | solution.py:22
  104.9 34.7 %all-to-all-start.3 = ((bf16[128,8,1024]{2,1,0:T(8,128)(2,1)}), bf16[128,8,1024]{2,1,0:T(8,128)(2,1)S(1)}, u32[]{:S(2)}, u32[]{:S(2)}) async-start(bf16[128,8,1024]{2,1,0:T(8,128)(2,1)} %get-tuple-element.125), calls=%async_computation.3 | async-start | bytes 4194304 | tf_op jit(solution)/shard_map/all_to_all | solution.py:22
  118.0 2.0 copy-start
  139.7 58.7 %all-to-all-start.4 = ((bf16[128,2,8,1024]{3,2,1,0:T(8,128)(2,1)}), bf16[128,2,8,1024]{3,2,1,0:T(8,128)(2,1)}, u32[]{:S(2)}, u32[]{:S(2)}) async-start(bf16[128,2,8,1024]{3,2,1,0:T(8,128)(2,1)} %bitcast.29), calls=%async_computation.4 | async-start | bytes 8388608 | tf_op jit(solution)/shard_map/all_to_all | solution.py:22
  149.9 5.4 %collective-permute-start.2 = (bf16[1024,1024]{1,0:T(8,128)(2,1)}, bf16[1024,1024]{1,0:T(8,128)(2,1)}, u32[]{:S(2)}, u32[]{:S(2)}) collective-permute-start(bf16[1024,1024]{1,0:T(8,128)(2,1)} %bitcast_select_fusion), channel_id=1, source_target_pairs={{0,1},{1,0},{2,3},{3,2},{4,5},{5,4},{6,7},{7,6},{8,9},{9,8},{10,11... | collective-permute-start | bytes 6291464 | tf_op jit(solution)/shard_map/ppermute | solution.py:18
  161.0 1.5 collective-permute-start.3

commit v3 on v2

--- a/solution.py
+++ b/solution.py
@@ -87,24 +87,54 @@
     )(kind, row, *tables)
 
 
-def first_kernel(index_ref, stat_ref, pending_ref, out_ref, sem):
+CHUNKS = 4
+
+
+def first_kernel(index_ref, stat_ref, pending_ref, first_ref, columns_ref, held, cut, sems):
+    rows, width = first_ref.shape
+    half, step = width // 2, rows // CHUNKS
     slot = jnp.where(stat_ref[index_ref[0] * 2] >= 0, 0, 1)
-    copy = pltpu.make_async_copy(pending_ref.at[slot], out_ref, sem)
-    copy.start()
-    copy.wait()
+    other_half = pl.ds(pl.multiple_of((1 - index_ref[0] % 2) * half, half), half)
+    moves = []
+    for chunk in range(CHUNKS):
+        part = pl.ds(chunk * step, step)
+        moves.append((pending_ref.at[slot, part, :], held.at[part, :], first_ref.at[part, :]))
+    moves.append((pending_ref.at[1, :, other_half], cut, columns_ref))
+    loads = [
+        pltpu.make_async_copy(src, mid, sems.at[0, pos]) for pos, (src, mid, dst) in enumerate(moves)
+    ]
+    stores = [
+        pltpu.make_async_copy(mid, dst, sems.at[1, pos]) for pos, (src, mid, dst) in enumerate(moves)
+    ]
+    for load in loads:
+        load.start()
+    for load, store in zip(loads, stores):
+        load.wait()
+        store.start()
+    for store in stores:
+        store.wait()
 
 
 def first_used(my_index, pending_stat, pending_roots):
+    rows, width = pending_roots.shape[1:]
+    kind = pending_roots.dtype
+    anywhere = pl.BlockSpec(memory_space=pl.ANY)
     return pl.pallas_call(
         first_kernel,
-        out_shape=jax.ShapeDtypeStruct(pending_roots.shape[1:], pending_roots.dtype),
-        in_specs=[pl.BlockSpec(memory_space=pltpu.SMEM)] * 2
-        + [pl.BlockSpec(memory_space=pl.ANY)],
-        out_specs=pl.BlockSpec(memory_space=pltpu.VMEM),
-        scratch_shapes=[pltpu.SemaphoreType.DMA],
+        out_shape=(
+            jax.ShapeDtypeStruct((rows, width), kind),
+            jax.ShapeDtypeStruct((rows, width // 2), kind),
+        ),
+        in_specs=[pl.BlockSpec(memory_space=pltpu.SMEM)] * 2 + [anywhere],
+        out_specs=(anywhere, anywhere),
+        scratch_shapes=[
+            pltpu.VMEM((rows, width), kind),
+            pltpu.VMEM((rows, width // 2), kind),
+            pltpu.SemaphoreType.DMA((2, CHUNKS + 1)),
+        ],
         compiler_params=pltpu.CompilerParams(vmem_limit_bytes=8 * 1024 * 1024),
         name="first_used",
-    )(my_index.reshape(1), pending_stat, pending_roots)
+    )(my_index, pending_stat, pending_roots)
 
 
 def poly_times(first, second):
@@ -131,69 +161,144 @@
 
 
 def root_kernel(
-    flag_ref,
-    gram_ref,
+    index_ref,
+    pending_stat_ref,
+    refresh_stat_ref,
+    own_grad_ref,
+    other_grad_ref,
     stat_ref,
     pending_ref,
     other_ref,
     new_ref,
     own_ref,
-    scaled_ref,
-    scaled16_ref,
-    square_ref,
-    square16_ref,
-    cube16_ref,
-    upper_ref,
-    diagonal_ref,
+    grad_ref,
+    grad,
+    factor16,
+    stat,
+    scaled,
+    scaled16,
+    square,
+    square16,
+    cube16,
+    upper16,
+    root16,
+    shared,
     sems,
 ):
     width = stat_ref.shape[0]
     half = width // 2
-    refreshed, from_other, parity = flag_ref[0], flag_ref[1], flag_ref[2]
+    tiles = width // TILE
+    me = index_ref[0]
+    parity = me % 2
     poly = root_polynomial(ITERS)
-    shared = own_ref.at[:, pl.ds(width, half)]
-
-    @pl.when(from_other > 0)
-    def _():
-        pltpu.make_async_copy(other_ref, shared, sems.at[0]).start()
-
-    @pl.when(from_other == 0)
-    def _():
-        columns = pl.ds(pl.multiple_of(parity * half, half), half)
-        pltpu.make_async_copy(pending_ref.at[1, :, columns], shared, sems.at[0]).start()
-
-    second = pltpu.make_async_copy(pending_ref.at[1], own_ref.at[:, pl.ds(0, width)], sems.at[1])
-
-    @pl.when(refreshed == 0)
+
+    def columns_of(step):
+        return pl.ds(pl.multiple_of(step * TILE, TILE), TILE)
+
+    def half_of(side):
+        return pl.ds(pl.multiple_of(side * half, half), half)
+
+    own_half = pltpu.make_async_copy(own_grad_ref, grad.at[half_of(parity), :], sems.at[0])
+    other_half = pltpu.make_async_copy(other_grad_ref, grad.at[half_of(1 - parity), :], sems.at[1])
+    statistic = pltpu.make_async_copy(stat_ref, stat, sems.at[2])
+    grad_out = pltpu.make_async_copy(grad, grad_ref, sems.at[3])
+    new_out = pltpu.make_async_copy(stat, new_ref, sems.at[4])
+    second = pltpu.make_async_copy(pending_ref.at[1], root16, sems.at[5])
+    shared_in = pltpu.make_async_copy(other_ref, shared, sems.at[6])
+    shared_out = pltpu.make_async_copy(shared, own_ref.at[:, pl.ds(width, half)], sems.at[7])
+
+    def root_out(step):
+        return pltpu.make_async_copy(
+            root16.at[:, columns_of(step)], own_ref.at[:, columns_of(step)], sems.at[8]
+        )
+
+    own_half.start()
+    other_half.start()
+    statistic.start()
+
+    def look(item, found):
+        entry = refresh_stat_ref[item]
+        return found[0] | (entry == me), found[1] | (entry == me - parity)
+
+    refreshed, core_refreshed = lax.fori_loop(
+        0, refresh_stat_ref.shape[0], look, (jnp.bool_(False), jnp.bool_(False)), unroll=16
+    )
+    core = (me - parity) * 2
+    core_shares = (
+        core_refreshed & (pending_stat_ref[core] >= 0) & (pending_stat_ref[core + 1] >= 0)
+    )
+    from_other = core_shares == (parity == 1)
+
+    @pl.when(from_other)
+    def _():
+        shared_in.start()
+
+    @pl.when(jnp.logical_not(from_other))
+    def _():
+        pltpu.make_async_copy(
+            pending_ref.at[1, :, half_of(parity)], shared, sems.at[6]
+        ).start()
+
+    @pl.when(jnp.logical_not(refreshed))
     def _():
         second.start()
 
-    diagonal_ref[...] = jnp.zeros_like(diagonal_ref)
-
-    @pl.loop(0, width // 128)
-    def _(step):
-        rows = pl.ds(pl.multiple_of(step * 128, 128), 128)
-        new_ref[rows, :] = decay_rate * stat_ref[rows, :] + (1.0 - decay_rate) * gram_ref[rows, :]
-        on_diagonal = lax.broadcasted_iota(jnp.int32, (128, 128), 0) == lax.broadcasted_iota(
-            jnp.int32, (128, 128), 1
+    own_half.wait()
+    other_half.wait()
+    grad_out.start()
+
+    @pl.when(parity == 0)
+    def _():
+        factor16[...] = grad[...]
+
+    @pl.when(parity == 1)
+    def _():
+        @pl.loop(0, tiles)
+        def _(step):
+            columns = columns_of(step)
+            factor16[columns, :] = jnp.transpose(grad[:, columns])
+
+    statistic.wait()
+
+    def update(step, trace):
+        columns = columns_of(step)
+        gram = lax.dot_general(
+            factor16[...],
+            factor16[columns, :],
+            (((1,), (1,)), ((), ())),
+            preferred_element_type=jnp.float32,
         )
-        diagonal_ref[...] += jnp.where(on_diagonal, new_ref[rows, rows], 0.0)
-
-    @pl.when(refreshed > 0)
-    def _():
-        trace = jnp.sum(jnp.sum(diagonal_ref[...], axis=1, keepdims=True), axis=0, keepdims=True)
-        norm_scale = 2.0 * trace / width
+        stat[:, columns] = decay_rate * stat[:, columns] + (1.0 - decay_rate) * gram
+        block = stat[columns, columns]
+        on_diagonal = lax.broadcasted_iota(jnp.int32, (TILE, TILE), 0) == lax.broadcasted_iota(
+            jnp.int32, (TILE, TILE), 1
+        )
+        return trace + jnp.sum(jnp.where(on_diagonal, block, 0.0), axis=0, keepdims=True)
+
+    diagonal = lax.fori_loop(0, tiles, update, jnp.zeros((1, TILE), jnp.float32))
+    shared_in.wait()
+    shared_out.start()
+
+    @pl.when(jnp.logical_not(refreshed))
+    def _():
+        second.wait()
+        new_out.start()
+        for step in range(tiles):
+            root_out(step).start()
+
+    @pl.when(refreshed)
+    def _():
+        norm_scale = 2.0 * jnp.sum(diagonal, axis=1, keepdims=True) / width
         factor = lax.rsqrt(jnp.sqrt(norm_scale))
 
         @pl.loop(0, width // 128)
         def _(step):
             rows = pl.ds(pl.multiple_of(step * 128, 128), 128)
-            scaled = new_ref[rows, :] / norm_scale
-            scaled_ref[rows, :] = scaled
-            scaled16_ref[rows, :] = scaled.astype(jnp.bfloat16)
-
-        def columns_of(step):
-            return pl.ds(pl.multiple_of(step * TILE, TILE), TILE)
+            part = stat[rows, :] / norm_scale
+            scaled[rows, :] = part
+            scaled16[rows, :] = part.astype(jnp.bfloat16)
+
+        new_out.start()
 
         def identity(step):
             return (
@@ -204,72 +309,97 @@
         def dot(first, second):
             return jnp.dot(first, second, preferred_element_type=jnp.float32)
 
-        @pl.loop(0, width // TILE)
+        @pl.loop(0, tiles)
         def _(step):
             columns = columns_of(step)
-            square = dot(scaled16_ref[...], scaled16_ref[:, columns])
-            square_ref[:, columns] = square
-            square16_ref[:, columns] = square.astype(jnp.bfloat16)
-
-        @pl.loop(0, width // TILE)
+            tile = dot(scaled16[...], scaled16[:, columns])
+            square[:, columns] = tile
+            square16[:, columns] = tile.astype(jnp.bfloat16)
+
+        @pl.loop(0, tiles)
         def _(step):
             columns = columns_of(step)
-            cube = dot(square16_ref[...], scaled16_ref[:, columns])
-            cube16_ref[:, columns] = cube.astype(jnp.bfloat16)
+            cube = dot(square16[...], scaled16[:, columns])
+            cube16[:, columns] = cube.astype(jnp.bfloat16)
             upper = (
                 jnp.where(identity(step), poly[3], 0.0)
-                + poly[4] * scaled_ref[:, columns]
-                + poly[5] * square_ref[:, columns]
+                + poly[4] * scaled[:, columns]
+                + poly[5] * square[:, columns]
                 + poly[6] * cube
             )
-            upper_ref[:, columns] = upper.astype(jnp.bfloat16)
-
-        @pl.loop(0, width // TILE)
+            upper16[:, columns] = upper.astype(jnp.bfloat16)
+
+        @pl.loop(0, tiles)
         def _(step):
             columns = columns_of(step)
-            total = dot(cube16_ref[...], upper_ref[:, columns])
+            total = dot(cube16[...], upper16[:, columns])
             total += (
                 jnp.where(identity(step), poly[0], 0.0)
-                + poly[1] * scaled_ref[:, columns]
-                + poly[2] * square_ref[:, columns]
+                + poly[1] * scaled[:, columns]
+                + poly[2] * square[:, columns]
             )
-            own_ref[:, columns] = (total * factor).astype(jnp.bfloat16)
-
-    @pl.when(refreshed == 0)
-    def _():
-        second.wait()
-
-    pltpu.make_async_copy(other_ref, shared, sems.at[0]).wait()
-
-
-def updated_and_root(flags, gram, statistic, pending_roots, other_columns):
+            root16[:, columns] = (total * factor).astype(jnp.bfloat16)
+
+            @pl.when(step > 0)
+            def _():
+                root_out(step - 1).start()
+
+    grad_out.wait()
+    new_out.wait()
+
+    @pl.when(refreshed)
+    def _():
+        root_out(tiles - 1).start()
+
+    shared_out.wait()
+    pltpu.make_async_copy(root16, own_ref.at[:, pl.ds(0, width)], sems.at[8]).wait()
+
+
+def updated_and_root(
+    my_index, pending_stat, refresh_stat, own_grad, other_grad, statistic, pending_roots, columns
+):
     width = statistic.shape[0]
-    vmem = pl.BlockSpec(memory_space=pltpu.VMEM)
     anywhere = pl.BlockSpec(memory_space=pl.ANY)
+    plain = pltpu.VMEM((width, width), jnp.float32)
+    short = pltpu.VMEM((width, width), jnp.bfloat16)
     return pl.pallas_call(
         root_kernel,
         out_shape=(
             jax.ShapeDtypeStruct((width, width), jnp.float32),
             jax.ShapeDtypeStruct((width, width + width // 2), jnp.bfloat16),
+            jax.ShapeDtypeStruct((width, width), jnp.bfloat16),
         ),
-        in_specs=[pl.BlockSpec(memory_space=pltpu.SMEM), vmem, vmem, anywhere, anywhere],
-        out_specs=(vmem, vmem),
+        in_specs=[pl.BlockSpec(memory_space=pltpu.SMEM)] * 3 + [anywhere] * 5,
+        out_specs=(anywhere,) * 3,
         scratch_shapes=[
-            pltpu.VMEM((width, width), jnp.float32),
-            pltpu.VMEM((width, width), jnp.bfloat16),
-            pltpu.VMEM((width, width), jnp.float32),
-            pltpu.VMEM((width, width), jnp.bfloat16),
-            pltpu.VMEM((width, width), jnp.bfloat16),
-            pltpu.VMEM((width, width), jnp.bfloat16),
-            pltpu.VMEM((128, 128), jnp.float32),
-            pltpu.SemaphoreType.DMA((2,)),
+            short,
+            short,
+            plain,
+            plain,
+            short,
+            plain,
+            short,
+            short,
+            short,
+            short,
+            pltpu.VMEM((width, width // 2), jnp.bfloat16),
+            pltpu.SemaphoreType.DMA((9,)),
         ],
         compiler_params=pltpu.CompilerParams(vmem_limit_bytes=44 * 1024 * 1024),
         cost_estimate=pl.CostEstimate(
-            flops=6 * width**3, bytes_accessed=15 * width * width, transcendentals=0
+            flops=8 * width**3, bytes_accessed=17 * width * width, transcendentals=0
         ),
         name="root",
-    )(flags, gram, statistic, pending_roots, other_columns)
+    )(
+        my_index,
+        pending_stat,
+        refresh_stat,
+        own_grad,
+        other_grad,
+        statistic,
+        pending_roots,
+        columns,
+    )
 
 
 def per_device(gradient, statistics, held_roots, pending_roots, pending_stat, refresh_stat):
@@ -291,37 +421,21 @@
     sharing_pairs = sharing.reshape(devices // 2, 2)
     unplaced = jnp.any(sharing_pairs[:, 0] & sharing_pairs[:, 1])
 
-    first_root = first_used(my_index, pending_stat, pending_roots)
+    index_table = my_index.reshape(1)
+    first_root, cut_columns = first_used(index_table, pending_stat, pending_roots)
     first_parts = spread(first_root.reshape(devices, piece_rows, block_width))
 
-    other_half = swapped(gradient, "dev", 0)
-    top_half = jnp.where(parity == 0, gradient, other_half)
-    bottom_half = jnp.where(parity == 0, other_half, gradient)
-    full_grad = jnp.concatenate([top_half, bottom_half], axis=0)
-    gram_term = lax.cond(
-        parity == 0,
-        lambda: lax.dot_general(
-            full_grad, full_grad, (((1,), (1,)), ((), ())), preferred_element_type=jnp.float32
-        ),
-        lambda: lax.dot_general(
-            full_grad, full_grad, (((0,), (0,)), ((), ())), preferred_element_type=jnp.float32
-        ),
+    new_stat, own_matrix, full_grad = updated_and_root(
+        index_table,
+        pending_stat,
+        refresh_stat,
+        gradient,
+        swapped(gradient, "dev", 0),
+        statistics[0],
+        pending_roots,
+        swapped(cut_columns, "dev", 0),
     )
     second_root = pending_roots[1]
-    my_refreshed = jnp.any(refresh_stat == my_index)
-    first_of_pair = lax.dynamic_slice_in_dim(sharing, my_index - parity, 1, 0)[0]
-    from_other = jnp.where(first_of_pair, parity == 1, parity == 0)
-    other_columns = swapped(
-        lax.dynamic_slice(
-            pending_roots, (1, 0, (1 - parity) * half_columns), (1, block_width, half_columns)
-        )[0],
-        "dev",
-        0,
-    )
-    flags = jnp.stack([my_refreshed, from_other, parity]).astype(jnp.int32)
-    new_stat, own_matrix = updated_and_root(
-        flags, gram_term, statistics[0], pending_roots, other_columns
-    )
     root_parts = spread(own_matrix.reshape(devices, piece_rows, block_width + half_columns))
 
     slot_match = pending_stat[None, :] == device_ids[:, None]

time: 205 us -> 199 us (0.971)
  waiting for transfers between devices: 99.6 us -> 108 us
  starting transfers between devices: 36.9 us -> 30.7 us
  local copies, waits for them, and re-layouts: 9.72 us -> 5.14 us
  matrix products: 10.1 us -> 6.54 us
    all_to_all x4, waiting for transfers between devices: 98.3 us -> 103 us  [spread(): return lax.all_to_all(parts, 'dev', split_axis=0, concat_axis=0, tiled=True)]
    all_to_all x4, starting transfers between devices: 32.6 us -> 28.1 us  [spread(): return lax.all_to_all(parts, 'dev', split_axis=0, concat_axis=0, tiled=True)]
    dot_general x1 -> x0, matrix products: 4.43 us -> none  [per_device(): lax.dot_general(full_grad, full_grad, (((0,), (0,)), ((), ())), preferred...]
    ppermute x4, waiting for transfers between devices: 1.34 us -> 5.11 us  [swapped(): lax.ppermute(shard, axis, [(i, i ^ 1 << bit) for i in range(lax.axis_size...]
    squeeze x1 -> x0, local copies, waits for them, and re-layouts: 2.27 us -> none  [per_device(): lax.dynamic_slice(pending_roots, (1, 0, (1 - parity) * half_columns), (1,...]
    unnamed x12 -> x16, local copies, waits for them, and re-layouts: 5.77 us -> 4.03 us
  transfers between devices with their start and end apart: 8 -> 8, of which waited for: 6 -> 7; matrix products, arithmetic and copies ran while one was open for 13% -> 11% of each run, Pallas kernels for 9% -> 9%
where the time goes in v3:
time: 199 us; the launch traced here: 198 us
  waiting for transfers between devices  108 us (54%)
  starting transfers between devices  30.7 us (15%)
  Pallas kernels  25.8 us (13%)
  other arithmetic  19 us (10%)
  matrix products  6.54 us (3%)
  local copies, waits for them, and re-layouts  5.14 us (3%)
  between operations  2.78 us (1%)
    all_to_all x4, waiting for transfers between devices, spread(): return lax.all_to_all(parts, 'dev', split_axis=0, concat_axis=0, tiled=True)  103 us
    all_to_all x4, starting transfers between devices, spread(): return lax.all_to_all(parts, 'dev', split_axis=0, concat_axis=0, tiled=True)  28.1 us
    pallas_call x2, Pallas kernels, pick(): pl.pallas_call(functools.partial(pick_kernel, width), out_shape=jax.Shape...  13.8 us
    pallas_call x1, Pallas kernels, updated_and_root(): pl.pallas_call(root_kernel, out_shape=(jax.ShapeDtypeStruct((width, width...  9.04 us
    select_n x2, other arithmetic, per_device(): merged = jnp.where(my_found, returned, held_roots[0])  8.39 us
    dot_general x1, matrix products, per_device(): jnp.dot(left_times, right_root, preferred_element_type=jnp.float32)  6.54 us
    reshape x1, other arithmetic, per_device(): fresh_roots = jnp.where((my_slots >= 0)[:, None, None, None], fresh.trans...  5.79 us
    ppermute x4, waiting for transfers between devices, swapped(): lax.ppermute(shard, axis, [(i, i ^ 1 << bit) for i in range(lax.axis_size...  5.11 us
  transfers between devices with their start and end apart: 8, of which 7 were waited for; matrix products, arithmetic and copies ran while one was open for 11% of the time, Pallas kernels for 9%

profile of v3, /device:TPU:1, one launch (start us, length us, event | category | flops | bytes accessed | tf_op | source)
XLA Modules:
  0.0 197.9 jit_solution(11818861963993929728)
XLA Ops:
  1.3 3.0 %first_used.1 = (bf16[1024,1024]{1,0:T(8,128)(2,1)}, bf16[1024,512]{1,0:T(8,128)(2,1)S(1)}) custom-call(s32[1]{0:T(128)} %bitcast.1.index_ref, s32[256]{0:T(256)S(1)} %copy-done.1, bf16[2,1024,1024]{2,1,0:T(8,128)(2,1)} %pending_ref.3), custom_call_target="tpu_custom_call" | custom-call | tf_op jit(solution)/shard_map/first_used/pallas_call | solution.py:122
  4.4 12.0 %all-to-all-start.2 = ((bf16[128,8,1024]{2,1,0:T(8,128)(2,1)}), bf16[128,8,1024]{2,1,0:T(8,128)(2,1)}, u32[]{:S(2)}, u32[]{:S(2)}) async-start(bf16[128,8,1024]{2,1,0:T(8,128)(2,1)} %bitcast.5), calls=%async_computation.2 | async-start | bytes 4194304 | tf_op jit(solution)/shard_map/all_to_all | solution.py:22
  17.6 2.2 %collective-permute-done.1.other_ref = bf16[1024,512]{1,0:T(8,128)(2,1)S(1)} collective-permute-done((bf16[1024,512]{1,0:T(8,128)(2,1)S(1)}, bf16[1024,512]{1,0:T(8,128)(2,1)S(1)}, u32[]{:S(2)}, u32[]{:S(2)}) %collective-permute-start.1) | collective-permute-done | bytes 1048608 | tf_op jit(solution)/shard_map/ppermute | solution.py:18
  19.8 1.5 collective-permute-done.other_grad_ref
  21.3 9.0 %root.1 = (f32[1024,1024]{1,0:T(8,128)}, bf16[1024,1536]{1,0:T(8,128)(2,1)}, bf16[1024,1024]{1,0:T(8,128)(2,1)S(1)}) custom-call(s32[1]{0:T(128)} %bitcast.1.index_ref, s32[256]{0:T(256)S(1)} %copy-done.2, s32[256]{0:T(256)S(1)} %copy-done.3, bf16[512,1024]{1,0:T(8,128)(2,1)S(1)} %copy-done.4, bf16[512,1024]{1,0:T(8,128)(2,1)S(1)} %collective-permute-done.other_grad_ref, ...), custom_call_target="tpu_custom_call" | custom-call | flops 8589934592 | bytes 17825792 | tf_op jit(solution)/shard_map/root/pallas_call | solution.py:365
  30.4 1.3 copy-done.5
  31.7 14.4 %all-to-all-done.2 = bf16[128,8,1024]{2,1,0:T(8,128)(2,1)} async-done(((bf16[128,8,1024]{2,1,0:T(8,128)(2,1)}), bf16[128,8,1024]{2,1,0:T(8,128)(2,1)}, u32[]{:S(2)}, u32[]{:S(2)}) %all-to-all-start.2) | async-done | bytes 2097184 | tf_op jit(solution)/shard_map/all_to_all | solution.py:22
  46.1 5.8 %all-to-all-start.1 = ((bf16[128,8,1536]{2,1,0:T(8,128)(2,1)}), bf16[128,8,1536]{2,1,0:T(8,128)(2,1)}, u32[]{:S(2)}, u32[]{:S(2)}) async-start(bf16[128,8,1536]{2,1,0:T(8,128)(2,1)} %bitcast.4), calls=%async_computation.1 | async-start | bytes 6291456 | tf_op jit(solution)/shard_map/all_to_all | solution.py:22
  54.9 38.4 %all-to-all-done.1.refs_0_ = bf16[128,8,1536]{2,1,0:T(8,128)(2,1)} async-done(((bf16[128,8,1536]{2,1,0:T(8,128)(2,1)}), bf16[128,8,1536]{2,1,0:T(8,128)(2,1)}, u32[]{:S(2)}, u32[]{:S(2)}) %all-to-all-start.1) | async-done | bytes 3145760 | tf_op jit(solution)/shard_map/all_to_all | solution.py:22
  93.3 5.3 %conditional.1 = (bf16[128,8,1024]{2,1,0:T(8,128)(2,1)}) conditional(s32[]{:T(128)} %convert_element_type.9, (s32[128]{0:T(128)S(1)}, s32[128]{0:T(128)S(1)}, bf16[128,8,1536]{2,1,0:T(8,128)(2,1)}, bf16[128,8,1024]{2,1,0:T(8,128)(2,1)}) %tuple.33, (pred[128]{0:T(512)(128)(4,1)S(1)}, pred[128]{0:T(512)(128)(4,1)S(1)}, pred[1,256]{1,0:T(4,128)(4,1)S(1)}, ...), branch_computations={%region_6.7_spmd, %region_7.9_spmd} | conditional | flops 4000101376 | bytes 14721132 | solution.py:459
  93.3 5.2 %pick.3 = bf16[128,8,1024]{2,1,0:T(8,128)(2,1)} custom-call(s32[128]{0:T(128)S(1)} %get-tuple-element.64.kind_ref, s32[128]{0:T(128)S(1)} %get-tuple-element.65.row_ref, bf16[128,8,1536]{2,1,0:T(8,128)(2,1)} %get-tuple-element.66.refs_0_, bf16[128,8,1024]{2,1,0:T(8,128)(2,1)} %get-tuple-element.67.refs_1_), custom_call_target="tpu_custom_call" | custom-call | flops 4000000000 | bytes 4194304 | tf_op jit(solution)/shard_map/cond/branch_0_fun/pick/pallas_call | solution.py:75
  98.6 4.5 %all-to-all-start.3 = ((bf16[128,8,1024]{2,1,0:T(8,128)(2,1)}), bf16[128,8,1024]{2,1,0:T(8,128)(2,1)S(1)}, u32[]{:S(2)}, u32[]{:S(2)}) async-start(bf16[128,8,1024]{2,1,0:T(8,128)(2,1)} %get-tuple-element.118), calls=%async_computation.3 | async-start | bytes 4194304 | tf_op jit(solution)/shard_map/all_to_all | solution.py:22
  103.1 8.6 %pick.5 = bf16[256,8,1024]{2,1,0:T(8,128)(2,1)S(1)} custom-call(s32[256]{0:T(256)S(1)} %rem.64.kind_ref, s32[256]{0:T(256)S(1)} %broadcast_maximum_fusion.row_ref, bf16[128,8,1536]{2,1,0:T(8,128)(2,1)} %all-to-all-done.1.refs_0_), custom_call_target="tpu_custom_call" | custom-call | flops 4000000000 | bytes 8388608 | tf_op jit(solution)/shard_map/pick/pallas_call | solution.py:75
  111.7 2.0 %copy-done = bf16[256,8,1024]{2,1,0:T(8,128)(2,1)} copy-done((bf16[256,8,1024]{2,1,0:T(8,128)(2,1)}, bf16[256,8,1024]{2,1,0:T(8,128)(2,1)S(1)}, u32[]{:S(2)}) %copy-start) | copy-done | bytes 4194328
  113.7 19.6 %all-to-all-done.3 = bf16[128,8,1024]{2,1,0:T(8,128)(2,1)S(1)} async-done(((bf16[128,8,1024]{2,1,0:T(8,128)(2,1)}), bf16[128,8,1024]{2,1,0:T(8,128)(2,1)S(1)}, u32[]{:S(2)}, u32[]{:S(2)}) %all-to-all-start.3) | async-done | bytes 2097184 | tf_op jit(solution)/shard_map/all_to_all | solution.py:22
  133.3 5.9 %all-to-all-start.4 = ((bf16[128,2,8,1024]{3,2,1,0:T(8,128)(2,1)}), bf16[128,2,8,1024]{3,2,1,0:T(8,128)(2,1)}, u32[]{:S(2)}, u32[]{:S(2)}) async-start(bf16[128,2,8,1024]{3,2,1,0:T(8,128)(2,1)} %bitcast.20), calls=%async_computation.4 | async-start | bytes 8388608 | tf_op jit(solution)/shard_map/all_to_all | solution.py:22
  139.9 3.9 %bitcast_select_fusion = bf16[1024,1024]{1,0:T(8,128)(2,1)} fusion(bf16[1,1024,1024]{2,1,0:T(8,128)(2,1)} %param.10, bf16[128,8,1024]{2,1,0:T(8,128)(2,1)S(1)} %all-to-all-done.3, pred[]{:T(512)} %compare_reduce_fusion.1), kind=kLoop, calls=%fused_computation.10 | loop fusion | flops 1048576 | bytes 6291457 | tf_op jit(solution)/shard_map/jit(_where)/select_n | solution.py:473
  143.8 1.3 collective-permute-start.2
  145.1 4.5 %bitcast_select_fusion.1 = bf16[1,1024,1024]{2,1,0:T(8,128)(2,1)} fusion(bf16[1,1024,1024]{2,1,0:T(8,128)(2,1)} %param.10, bf16[128,8,1024]{2,1,0:T(8,128)(2,1)} %copy-done.7, pred[]{:T(512)} %compare_reduce_fusion.1), kind=kLoop, calls=%fused_computation.11 | loop fusion | flops 1048576 | bytes 6291457 | tf_op jit(solution)/shard_map/jit(_where)/select_n | solution.py:473
  149.7 6.5 %multiply_reduce_fusion = (f32[]{:T(128)}, f32[512,1024]{1,0:T(8,128)}) fusion(bf16[1024,1024]{1,0:T(8,128)(2,1)} %collective-permute-done.2, bf16[1024,1024]{1,0:T(8,128)(2,1)} %bitcast_select_fusion, pred[]{:T(512)S(6)} %eq.62, bf16[1024,1024]{1,0:T(8,128)(2,1)S(1)} %copy-done.6, s32[]{:T(128)S(6)} %select_n.106), kind=kOutput, calls=%fused_computation.13 | convolution fusion | flops 2150629376 | bytes 10487300 | tf_op jit(solution)/shard_map/dot_general | solution.py:490
  156.2 1.4 collective-permute-done.3
  158.9 2.8 %multiply_convert_fusion = bf16[512,1024]{1,0:T(8,128)(2,1)} fusion(f32[512,1024]{1,0:T(8,128)} %get-tuple-element.117, f32[]{:T(128)S(6)} %rsqrt.3), kind=kLoop, calls=%fused_computation.12 | loop fusion | flops 1048576 | bytes 3145732 | tf_op jit(solution)/shard_map/convert_element_type | solution.py:494
  161.7 30.4 %all-to-all-done.4 = bf16[128,2,8,1024]{3,2,1,0:T(8,128)(2,1)} async-done(((bf16[128,2,8,1024]{3,2,1,0:T(8,128)(2,1)}), bf16[128,2,8,1024]{3,2,1,0:T(8,128)(2,1)}, u32[]{:S(2)}, u32[]{:S(2)}) %all-to-all-start.4) | async-done | bytes 4194336 | tf_op jit(solution)/shard_map/all_to_all | solution.py:22
  192.1 5.8 %copy_bitcast_fusion = bf16[2,1024,1024]{2,1,0:T(8,128)(2,1)} fusion(bf16[128,2,8,1024]{3,2,1,0:T(8,128)(2,1)} %all-to-all-done.4, pred[2]{0:T(512)(128)(4,1)S(1)} %dynamic-slice_compare_fusion), kind=kLoop, calls=%fused_computation.8 | loop fusion | flops 2097152 | bytes 8388610 | tf_op jit(solution)/shard_map/reshape | solution.py:502
  (42 shorter events, 5.1 us)
Async XLA Ops:
  0.6 0.7 copy-start.1
  4.3 13.2 %copy-start.4 = (bf16[512,1024]{1,0:T(8,128)(2,1)S(1)}, bf16[512,1024]{1,0:T(8,128)(2,1)}, u32[]{:S(2)}) copy-start(bf16[512,1024]{1,0:T(8,128)(2,1)} %own_grad_ref.1) | copy-start | bytes 3145732
  4.3 17.0 %copy-start.2 = (s32[256]{0:T(256)S(1)}, s32[256]{0:T(256)}, u32[]{:S(2)}) copy-start(s32[256]{0:T(256)} %pending_stat_ref.1) | copy-start | bytes 3076
  4.3 17.0 %copy-start.3 = (s32[256]{0:T(256)S(1)}, s32[256]{0:T(256)}, u32[]{:S(2)}) copy-start(s32[256]{0:T(256)} %refresh_stat_ref.1) | copy-start | bytes 3076
  4.4 41.7 %all-to-all-start.2 = ((bf16[128,8,1024]{2,1,0:T(8,128)(2,1)}), bf16[128,8,1024]{2,1,0:T(8,128)(2,1)}, u32[]{:S(2)}, u32[]{:S(2)}) async-start(bf16[128,8,1024]{2,1,0:T(8,128)(2,1)} %bitcast.5), calls=%async_computation.2 | async-start | bytes 4194304 | tf_op jit(solution)/shard_map/all_to_all | solution.py:22
  16.3 3.5 %collective-permute-start.1 = (bf16[1024,512]{1,0:T(8,128)(2,1)S(1)}, bf16[1024,512]{1,0:T(8,128)(2,1)S(1)}, u32[]{:S(2)}, u32[]{:S(2)}) collective-permute-start(bf16[1024,512]{1,0:T(8,128)(2,1)S(1)} %get-tuple-element.91), channel_id=1, source_target_pairs={{0,1},{1,0},{2,3},{3,2},{4,5},{5,4},{6,7},{7,6},{8,9},{9,8},{10,11... | collective-permute-start | bytes 3145736 | tf_op jit(solution)/shard_map/ppermute | solution.py:18
  17.5 3.8 %collective-permute-start = (bf16[512,1024]{1,0:T(8,128)(2,1)S(1)}, bf16[512,1024]{1,0:T(8,128)(2,1)S(1)}, u32[]{:S(2)}, u32[]{:S(2)}) collective-permute-start(bf16[512,1024]{1,0:T(8,128)(2,1)S(1)} %copy-done.4), channel_id=1, source_target_pairs={{0,1},{1,0},{2,3},{3,2},{4,5},{5,4},{6,7},{7,6},{8,9},{9,8},{10,11... | collective-permute-start | bytes 3145736 | tf_op jit(solution)/shard_map/ppermute | solution.py:18
  30.4 1.3 copy-start.5
  46.1 47.3 %all-to-all-start.1 = ((bf16[128,8,1536]{2,1,0:T(8,128)(2,1)}), bf16[128,8,1536]{2,1,0:T(8,128)(2,1)}, u32[]{:S(2)}, u32[]{:S(2)}) async-start(bf16[128,8,1536]{2,1,0:T(8,128)(2,1)} %bitcast.4), calls=%async_computation.1 | async-start | bytes 6291456 | tf_op jit(solution)/shard_map/all_to_all | solution.py:22
  98.6 34.7 %all-to-all-start.3 = ((bf16[128,8,1024]{2,1,0:T(8,128)(2,1)}), bf16[128,8,1024]{2,1,0:T(8,128)(2,1)S(1)}, u32[]{:S(2)}, u32[]{:S(2)}) async-start(bf16[128,8,1024]{2,1,0:T(8,128)(2,1)} %get-tuple-element.118), calls=%async_computation.3 | async-start | bytes 4194304 | tf_op jit(solution)/shard_map/all_to_all | solution.py:22
  111.7 2.0 %copy-start = (bf16[256,8,1024]{2,1,0:T(8,128)(2,1)}, bf16[256,8,1024]{2,1,0:T(8,128)(2,1)S(1)}, u32[]{:S(2)}) copy-start(bf16[256,8,1024]{2,1,0:T(8,128)(2,1)S(1)} %pick.5) | copy-start | bytes 12582916
  133.3 6.6 %copy-start.7 = (bf16[128,8,1024]{2,1,0:T(8,128)(2,1)}, bf16[128,8,1024]{2,1,0:T(8,128)(2,1)S(1)}, u32[]{:S(2)}) copy-start(bf16[128,8,1024]{2,1,0:T(8,128)(2,1)S(1)} %all-to-all-done.3) | copy-start | bytes 6291460
  133.3 58.8 %all-to-all-start.4 = ((bf16[128,2,8,1024]{3,2,1,0:T(8,128)(2,1)}), bf16[128,2,8,1024]{3,2,1,0:T(8,128)(2,1)}, u32[]{:S(2)}, u32[]{:S(2)}) async-start(bf16[128,2,8,1024]{3,2,1,0:T(8,128)(2,1)} %bitcast.20), calls=%async_computation.4 | async-start | bytes 8388608 | tf_op jit(solution)/shard_map/all_to_all | solution.py:22
  143.8 5.9 %collective-permute-start.2 = (bf16[1024,1024]{1,0:T(8,128)(2,1)}, bf16[1024,1024]{1,0:T(8,128)(2,1)}, u32[]{:S(2)}, u32[]{:S(2)}) collective-permute-start(bf16[1024,1024]{1,0:T(8,128)(2,1)} %bitcast_select_fusion), channel_id=1, source_target_pairs={{0,1},{1,0},{2,3},{3,2},{4,5},{5,4},{6,7},{7,6},{8,9},{9,8},{10,11... | collective-permute-start | bytes 6291464 | tf_op jit(solution)/shard_map/ppermute | solution.py:18
  145.1 4.5 %copy-start.6 = (bf16[1024,1024]{1,0:T(8,128)(2,1)S(1)}, bf16[1024,1024]{1,0:T(8,128)(2,1)}, u32[]{:S(2)}) copy-start(bf16[1024,1024]{1,0:T(8,128)(2,1)} %copy-done.5) | copy-start | bytes 6291460
  156.2 1.4 collective-permute-start.3

commit v4 on v3

--- a/solution.py
+++ b/solution.py
@@ -1,5 +1,3 @@
-import functools
-
 import jax
 import jax.numpy as jnp
 from jax import lax
@@ -23,45 +21,47 @@
 
 
 FIRST, OWN, SHARED, EXTRA = range(4)
-
-
-def pick_kernel(width, kind_ref, row_ref, *refs):
-    tables, out_ref, sem = refs[:-2], refs[-2], refs[-1]
+EMPTY, PLAIN, HALVES, LATE = range(4)
+
+
+def pick_kernel(kind_ref, row_ref, own_ref, *refs):
+    tables, out_ref, sem = refs[:-3], refs[-3], refs[-1]
+    width = out_ref.shape[2]
     half = width // 2
 
     def start(src, dst):
         pltpu.make_async_copy(src, dst, sem).start()
 
     def issue(item, carry):
-        row = row_ref[item]
-        if len(tables) == 1:
-            start(tables[0].at[row, :, pl.ds(0, width)], out_ref.at[item])
-            return carry
-        kind = kind_ref[item]
+        row, kind = row_ref[item], kind_ref[item]
 
         @pl.when(kind == FIRST)
         def _():
-            start(tables[1].at[row], out_ref.at[item])
+            start(tables[0].at[row], out_ref.at[item])
 
         @pl.when(kind != FIRST)
         def _():
             @pl.when(kind == OWN)
             def _():
-                start(tables[0].at[row, :, pl.ds(0, width)], out_ref.at[item])
+                start(own_ref.at[row, :, pl.ds(0, width)], out_ref.at[item])
 
             @pl.when(kind == SHARED)
             def _():
                 for core in range(2):
                     start(
-                        tables[0].at[row // 2 * 2 + core, :, pl.ds(width, half)],
+                        own_ref.at[row // 2 * 2 + core, :, pl.ds(width, half)],
                         out_ref.at[item, :, pl.ds(core * half, half)],
                     )
 
-            if len(tables) > 2:
+            if len(tables) > 1:
 
                 @pl.when(kind == EXTRA)
                 def _():
-                    start(tables[2].at[row], out_ref.at[item])
+                    for core in range(2):
+                        start(
+                            tables[1].at[row // 2 * 2 + core],
+                            out_ref.at[item, :, pl.ds(core * half, half)],
+                        )
 
         return carry
 
@@ -69,22 +69,129 @@
     pltpu.make_async_copy(out_ref, out_ref, sem).wait()
 
 
-def pick(kind, row, width, *tables):
-    items, piece_rows = row.shape[0], tables[0].shape[1]
-    out_bytes = items * piece_rows * width * 2
+def pick(kind, row, *tables):
+    items, (_, piece_rows, width) = row.shape[0], tables[1].shape
+    shape = jax.ShapeDtypeStruct((items, piece_rows, width), tables[0].dtype)
+    anywhere = pl.BlockSpec(memory_space=pl.ANY)
     return pl.pallas_call(
-        functools.partial(pick_kernel, width),
-        out_shape=jax.ShapeDtypeStruct((items, piece_rows, width), tables[0].dtype),
-        in_specs=[pl.BlockSpec(memory_space=pltpu.SMEM)] * 2
-        + [pl.BlockSpec(memory_space=pl.ANY)] * len(tables),
-        out_specs=pl.BlockSpec(memory_space=pltpu.VMEM),
+        pick_kernel,
+        out_shape=(shape, shape),
+        in_specs=[pl.BlockSpec(memory_space=pltpu.SMEM)] * 2 + [anywhere] * len(tables),
+        out_specs=(pl.BlockSpec(memory_space=pltpu.VMEM), anywhere),
         scratch_shapes=[pltpu.SemaphoreType.DMA],
-        compiler_params=pltpu.CompilerParams(vmem_limit_bytes=16 * 1024 * 1024),
+        compiler_params=pltpu.CompilerParams(vmem_limit_bytes=8 * 1024 * 1024),
         cost_estimate=pl.CostEstimate(
-            flops=4 * 1000 * 1000 * 1000, bytes_accessed=2 * out_bytes, transcendentals=0
+            flops=4 * 1000 * 1000 * 1000, bytes_accessed=8 * 1000 * 1000, transcendentals=0
         ),
         name="pick",
     )(kind, row, *tables)
+
+
+def route_kernel(row_ref, shared_row_ref, own_ref, out_ref, sem):
+    half = out_ref.shape[2] // 3
+
+    def issue(chip, carry):
+        shared_row = shared_row_ref[chip]
+        for core in range(2):
+            item = chip * 2 + core
+            pltpu.make_async_copy(
+                own_ref.at[row_ref[item], :, pl.ds(0, 2 * half)],
+                out_ref.at[item, :, pl.ds(0, 2 * half)],
+                sem,
+            ).start()
+            pltpu.make_async_copy(
+                own_ref.at[shared_row, :, pl.ds(core * half, half)],
+                out_ref.at[item, :, pl.ds(2 * half, half)],
+                sem,
+            ).start()
+        return carry
+
+    lax.fori_loop(0, out_ref.shape[0] // 2, issue, 0, unroll=4)
+    pltpu.make_async_copy(out_ref, out_ref, sem).wait()
+
+
+def route(row, shared_row, own):
+    return pl.pallas_call(
+        route_kernel,
+        out_shape=jax.ShapeDtypeStruct(own.shape, own.dtype),
+        in_specs=[pl.BlockSpec(memory_space=pltpu.SMEM)] * 2
+        + [pl.BlockSpec(memory_space=pl.ANY)],
+        out_specs=pl.BlockSpec(memory_space=pltpu.VMEM),
+        scratch_shapes=[pltpu.SemaphoreType.DMA],
+        compiler_params=pltpu.CompilerParams(vmem_limit_bytes=8 * 1024 * 1024),
+        cost_estimate=pl.CostEstimate(
+            flops=4 * 1000 * 1000 * 1000, bytes_accessed=12 * 1000 * 1000, transcendentals=0
+        ),
+        name="route",
+    )(row, shared_row, own)
+
+
+def place_kernel(code_ref, got_ref, other_ref, late_ref, zero_ref, out_ref, held, zeros, sems):
+    rows, width = late_ref.shape
+    half, step = width // 2, rows // CHUNKS
+    first, second, parity = code_ref[0], code_ref[1], code_ref[2]
+
+    def side(core):
+        return pl.ds(pl.multiple_of(core * half, half), half)
+
+    def loads(slot, code, sem):
+        into = held.at[slot]
+
+        @pl.when(code == PLAIN)
+        def _():
+            pltpu.make_async_copy(got_ref.at[:, pl.ds(0, width)], into, sem).start()
+
+        @pl.when(code == LATE)
+        def _():
+            pltpu.make_async_copy(late_ref, into, sem).start()
+
+        @pl.when(code == HALVES)
+        def _():
+            pltpu.make_async_copy(
+                got_ref.at[:, pl.ds(width, half)], into.at[:, side(parity)], sem
+            ).start()
+            pltpu.make_async_copy(other_ref, into.at[:, side(1 - parity)], sem).start()
+
+    for slot, code in enumerate((first, second)):
+        loads(slot, code, sems.at[slot])
+
+    pltpu.make_async_copy(zero_ref, zeros, sems.at[3]).start()
+    for slot, code in enumerate((first, second)):
+
+        @pl.when(code != EMPTY)
+        def _():
+            pltpu.make_async_copy(late_ref, held.at[slot], sems.at[slot]).wait()
+            pltpu.make_async_copy(held.at[slot], out_ref.at[slot], sems.at[2]).start()
+
+    pltpu.make_async_copy(zero_ref, zeros, sems.at[3]).wait()
+    for slot, code in enumerate((first, second)):
+
+        @pl.when(code == EMPTY)
+        def _():
+            for chunk in range(CHUNKS):
+                pltpu.make_async_copy(
+                    zeros, out_ref.at[slot, pl.ds(chunk * step, step), :], sems.at[2]
+                ).start()
+
+    pltpu.make_async_copy(held, out_ref, sems.at[2]).wait()
+
+
+def place(codes, got, other, late):
+    rows, width = late.shape
+    anywhere = pl.BlockSpec(memory_space=pl.ANY)
+    return pl.pallas_call(
+        place_kernel,
+        out_shape=jax.ShapeDtypeStruct((2, rows, width), late.dtype),
+        in_specs=[pl.BlockSpec(memory_space=pltpu.SMEM)] + [anywhere] * 4,
+        out_specs=anywhere,
+        scratch_shapes=[
+            pltpu.VMEM((2, rows, width), late.dtype),
+            pltpu.VMEM((rows // CHUNKS, width), late.dtype),
+            pltpu.SemaphoreType.DMA((4,)),
+        ],
+        compiler_params=pltpu.CompilerParams(vmem_limit_bytes=8 * 1024 * 1024),
+        name="place",
+    )(codes, got, other, late, jnp.zeros((rows // CHUNKS, width), late.dtype))
 
 
 CHUNKS = 4
@@ -414,16 +521,10 @@
     slot_total = pending_stat.shape[0]
     device_ids = jnp.arange(devices, dtype=jnp.int32)
 
-    has_first = pending_stat.reshape(devices, slot_count)[:, 0] >= 0
-    has_second = has_first & (pending_stat.reshape(devices, slot_count)[:, 1] >= 0)
-    refreshed = jnp.any(refresh_stat[None, :] == device_ids[:, None], axis=1)
-    sharing = has_second & refreshed
-    sharing_pairs = sharing.reshape(devices // 2, 2)
-    unplaced = jnp.any(sharing_pairs[:, 0] & sharing_pairs[:, 1])
-
     index_table = my_index.reshape(1)
     first_root, cut_columns = first_used(index_table, pending_stat, pending_roots)
     first_parts = spread(first_root.reshape(devices, piece_rows, block_width))
+    other_columns = swapped(cut_columns, "dev", 0)
 
     new_stat, own_matrix, full_grad = updated_and_root(
         index_table,
@@ -433,52 +534,86 @@
         swapped(gradient, "dev", 0),
         statistics[0],
         pending_roots,
-        swapped(cut_columns, "dev", 0),
-    )
-    second_root = pending_roots[1]
+        other_columns,
+    )
     root_parts = spread(own_matrix.reshape(devices, piece_rows, block_width + half_columns))
 
+    has_first = pending_stat.reshape(devices, slot_count)[:, 0] >= 0
+    has_second = has_first & (pending_stat.reshape(devices, slot_count)[:, 1] >= 0)
+    refreshed = jnp.any(refresh_stat[None, :] == device_ids[:, None], axis=1)
+    sharing_pairs = (has_second & refreshed).reshape(devices // 2, 2)
+    unplaced = jnp.any(sharing_pairs[:, 0] & sharing_pairs[:, 1])
+    slot_ids = jnp.arange(slot_total, dtype=jnp.int32)
     slot_match = pending_stat[None, :] == device_ids[:, None]
-    slot_of = jnp.sum(
-        jnp.where(slot_match, jnp.arange(slot_total, dtype=jnp.int32)[None, :], 0), axis=1
-    )
-    source = slot_of // slot_count
+    found = jnp.any(slot_match, axis=1)
+    slot_of = jnp.sum(jnp.where(slot_match, slot_ids[None, :], 0), axis=1)
     is_second = jnp.any(
-        slot_match & (jnp.arange(slot_total) % slot_count == 1) & jnp.repeat(has_first, slot_count),
-        axis=1,
+        slot_match & (slot_ids % slot_count == 1) & jnp.repeat(has_first, slot_count), axis=1
     )
     is_shared = jnp.any(slot_match & jnp.repeat(refreshed, slot_count), axis=1)
     is_extra = jnp.any(
         slot_match
-        & (jnp.arange(slot_total) // slot_count % 2 == 1)
-        & jnp.repeat(jnp.repeat(sharing_pairs[:, 0], 2), slot_count),
+        & (slot_ids // slot_count % 2 == 1)
+        & jnp.repeat(sharing_pairs[:, 0], 2 * slot_count),
         axis=1,
     )
-    kind = jnp.where(is_second, jnp.where(is_shared, SHARED, OWN), FIRST).astype(jnp.int32)
-    kind_extra = jnp.where(is_second & is_shared & is_extra, EXTRA, kind).astype(jnp.int32)
-    chosen = lax.cond(
-        unplaced,
-        lambda: pick(
-            kind_extra,
-            source,
-            block_width,
-            root_parts,
-            first_parts,
-            spread(second_root.reshape(devices, piece_rows, block_width)),
+    shared_kind = jnp.where(is_extra, EXTRA, SHARED)
+    kind = jnp.where(is_second, jnp.where(is_shared, shared_kind, OWN), FIRST)
+
+    wanted = refresh_stat.reshape(devices, slot_count)
+    wants_two = (wanted[:, 0] >= 0) & (wanted[:, 1] >= 0)
+    two_pairs = wants_two.reshape(devices // 2, 2)
+    second_pairs = jnp.maximum(wanted[:, 1], 0).reshape(devices // 2, 2)
+    first_wanted = jnp.maximum(jnp.where(wanted[:, 0] >= 0, wanted[:, 0], wanted[:, 1]), 0)
+    shared_wanted = jnp.where(two_pairs[:, 0], second_pairs[:, 0], second_pairs[:, 1])
+    fourth = two_pairs[:, 0] & two_pairs[:, 1]
+    found_pairs = found.reshape(devices // 2, 2)
+    unrouted = jnp.any(fourth & found_pairs[:, 0] & found_pairs[:, 1])
+    carries = (
+        jnp.repeat(fourth, 2)
+        & jnp.logical_not(found)
+        & ((device_ids % 2 == 1) | jnp.repeat(found_pairs[:, 1], 2))
+    )
+    kind = jnp.where(carries, OWN, kind).astype(jnp.int32)
+    source = jnp.where(carries, jnp.repeat(second_pairs[:, 1], 2), slot_of // slot_count)
+
+    def choose(more_pending, more_fresh):
+        def run():
+            tables = [root_parts, first_parts]
+            if more_pending:
+                columns = jnp.where(
+                    parity == 0, other_columns, pending_roots[1][:, half_columns:]
+                )
+                tables.append(spread(columns.reshape(devices, piece_rows, half_columns)))
+            chosen, spare = pick(kind, source, *tables)
+            if more_fresh:
+                late, _ = pick(
+                    jnp.full((devices,), OWN, jnp.int32), jnp.maximum(wanted[:, 1], 0), *tables[:2]
+                )
+                spare = spread(late)
+            return chosen, spare
+
+        return run
+
+    chosen, spare = lax.switch(
+        unplaced + 2 * unrouted.astype(jnp.int32),
+        [choose(more % 2 == 1, more // 2 == 1) for more in range(4)],
+    )
+    chosen, spare = lax.optimization_barrier((chosen, spare))
+    returned = spread(chosen).reshape(block_width, block_width)
+    routed = route(first_wanted, shared_wanted, root_parts)
+    fresh = spread(routed).reshape(block_width, block_width + half_columns)
+
+    my_found = jnp.any(pending_stat == my_index)
+    partner_found = jnp.any(pending_stat == my_index + 1 - 2 * parity)
+    merged = jnp.where(my_found, returned, held_roots[0])
+    late = jnp.where(
+        my_found,
+        jnp.where(
+            partner_found, spare.reshape(block_width, block_width), swapped(returned, "dev", 0)
         ),
-        lambda: pick(kind, source, block_width, root_parts, first_parts),
-    )
-    returned = spread(chosen).reshape(block_width, block_width)
-    my_found = jnp.any(pending_stat == my_index)
-    merged = jnp.where(my_found, returned, held_roots[0])
-
-    routed = pick(
-        jnp.full((slot_total,), OWN, jnp.int32),
-        jnp.maximum(refresh_stat, 0),
-        block_width,
-        root_parts,
-    )
-    fresh = spread(routed.reshape(devices, slot_count, piece_rows, block_width))
+        returned,
+    )
 
     partner_root = swapped(merged, "dev", 0)
     left_root = jnp.where(parity == 0, merged, partner_root)
@@ -493,13 +628,21 @@
     rms_scale = lax.rsqrt((own_square + other_square) / (block_width * block_width) + 1e-06)
     direction = (product * rms_scale).astype(jnp.bfloat16)
 
-    fresh, direction = lax.optimization_barrier((fresh, direction))
     my_slots = lax.dynamic_slice_in_dim(refresh_stat, my_index * slot_count, slot_count, 0)
-    fresh_roots = jnp.where(
-        (my_slots >= 0)[:, None, None, None],
-        fresh.transpose(1, 0, 2, 3),
-        jnp.zeros((), jnp.bfloat16),
-    ).reshape(slot_count, block_width, block_width)
+    core_slots = lax.dynamic_slice_in_dim(
+        refresh_stat, (my_index - parity) * slot_count, slot_count, 0
+    )
+    is_fourth = (parity == 1) & jnp.all(core_slots >= 0)
+    doubled = jnp.where(is_fourth, LATE, HALVES)
+    codes = jnp.stack(
+        [
+            jnp.where(my_slots[0] >= 0, PLAIN, EMPTY),
+            jnp.where(my_slots[1] >= 0, jnp.where(my_slots[0] >= 0, doubled, PLAIN), EMPTY),
+            parity,
+        ]
+    ).astype(jnp.int32)
+    fresh, direction, codes, late = lax.optimization_barrier((fresh, direction, codes, late))
+    fresh_roots = place(codes, fresh, swapped(fresh[:, block_width:], "dev", 0), late)
     return (new_stat[None], merged[None], direction, fresh_roots)
 
 

time: 199 us -> 199 us (level)
  waiting for transfers between devices: 108 us -> 71 us
  blocking collectives: 0 us -> 35.8 us
  starting transfers between devices: 30.7 us -> 26.5 us
  local copies, waits for them, and re-layouts: 5.14 us -> 8.04 us
  between operations: 2.78 us -> 5.66 us
    all_to_all x4 -> x3, waiting for transfers between devices: 103 us -> 65.6 us  [spread(): return lax.all_to_all(parts, 'dev', split_axis=0, concat_axis=0, tiled=True)]
    all_to_all x0 -> x1, blocking collectives: none -> 35.8 us  [spread(): return lax.all_to_all(parts, 'dev', split_axis=0, concat_axis=0, tiled=True)]
    select_n x3 -> x4, other arithmetic: 0.02 us -> 7.2 us  [the longest x1 7.17 us: per_device(): jnp.where(my_found, jnp.where(partner_found, spare.reshape(block_width, b...]
    all_to_all x4 -> x3, starting transfers between devices: 28.1 us -> 21.3 us  [spread(): return lax.all_to_all(parts, 'dev', split_axis=0, concat_axis=0, tiled=True)]
    reshape x1 -> x0, other arithmetic: 5.79 us -> none  [per_device(): fresh_roots = jnp.where((my_slots >= 0)[:, None, None, None], fresh.trans...]
    select_n x2 -> x1, other arithmetic: 8.39 us -> 3.88 us  [per_device(): merged = jnp.where(my_found, returned, held_roots[0])]
    ppermute x4 -> x6, starting transfers between devices: 2.6 us -> 5.17 us  [swapped(): lax.ppermute(shard, axis, [(i, i ^ 1 << bit) for i in range(lax.axis_size...]
    ppermute x4 -> x6, waiting for transfers between devices: 5.11 us -> 5.37 us  [swapped(): lax.ppermute(shard, axis, [(i, i ^ 1 << bit) for i in range(lax.axis_size...]
  transfers between devices with their start and end apart: 8 -> 9, of which waited for: 7 -> 7; matrix products, arithmetic and copies ran while one was open for 11% -> 14% of each run, Pallas kernels for 9% -> 8%
where the time goes in v4:
time: 199 us; the launch traced here: 198 us
  waiting for transfers between devices  71 us (36%)
  blocking collectives  35.8 us (18%)
  starting transfers between devices  26.5 us (13%)
  Pallas kernels  26 us (13%)
  other arithmetic  17.6 us (9%)
  local copies, waits for them, and re-layouts  8.04 us (4%)
  matrix products  7.14 us (4%)
  between operations  5.66 us (3%)
    all_to_all x3, waiting for transfers between devices, spread(): return lax.all_to_all(parts, 'dev', split_axis=0, concat_axis=0, tiled=True)  65.6 us
    all_to_all x1, blocking collectives, spread(): return lax.all_to_all(parts, 'dev', split_axis=0, concat_axis=0, tiled=True)  35.8 us
    all_to_all x3, starting transfers between devices, spread(): return lax.all_to_all(parts, 'dev', split_axis=0, concat_axis=0, tiled=True)  21.3 us
    pallas_call x1, Pallas kernels, updated_and_root(): pl.pallas_call(root_kernel, out_shape=(jax.ShapeDtypeStruct((width, width...  9.06 us
    select_n x1, other arithmetic, per_device(): jnp.where(my_found, jnp.where(partner_found, spare.reshape(block_width, b...  7.17 us
    dot_general x1, matrix products, per_device(): jnp.dot(left_times, right_root, preferred_element_type=jnp.float32)  7.14 us
    pallas_call x1, Pallas kernels, route(): pl.pallas_call(route_kernel, out_shape=jax.ShapeDtypeStruct(own.shape, ow...  5.84 us
    ppermute x6, waiting for transfers between devices, swapped(): lax.ppermute(shard, axis, [(i, i ^ 1 << bit) for i in range(lax.axis_size...  5.37 us
  transfers between devices with their start and end apart: 9, of which 7 were waited for; matrix products, arithmetic and copies ran while one was open for 14% of the time, Pallas kernels for 8%

profile of v4, /device:TPU:1, one launch (start us, length us, event | category | flops | bytes accessed | tf_op | source)
XLA Modules:
  0.0 197.8 jit_solution(12029389807670860129)
XLA Ops:
  1.3 3.0 %first_used.1 = (bf16[1024,1024]{1,0:T(8,128)(2,1)}, bf16[1024,512]{1,0:T(8,128)(2,1)S(1)}) custom-call(s32[1]{0:T(128)} %bitcast.6.index_ref, s32[256]{0:T(256)S(1)} %copy-done.2, bf16[2,1024,1024]{2,1,0:T(8,128)(2,1)} %pending_ref.3), custom_call_target="tpu_custom_call" | custom-call | tf_op jit(solution)/shard_map/first_used/pallas_call | solution.py:229
  4.4 12.0 %all-to-all-start.5 = ((bf16[128,8,1024]{2,1,0:T(8,128)(2,1)}), bf16[128,8,1024]{2,1,0:T(8,128)(2,1)}, u32[]{:S(2)}, u32[]{:S(2)}) async-start(bf16[128,8,1024]{2,1,0:T(8,128)(2,1)} %bitcast.10), calls=%async_computation.5 | async-start | bytes 4194304 | tf_op jit(solution)/shard_map/all_to_all | solution.py:20
  16.3 1.2 collective-permute-start.1
  17.6 2.2 %collective-permute-done.1.other_ref = bf16[1024,512]{1,0:T(8,128)(2,1)S(1)} collective-permute-done((bf16[1024,512]{1,0:T(8,128)(2,1)S(1)}, bf16[1024,512]{1,0:T(8,128)(2,1)S(1)}, u32[]{:S(2)}, u32[]{:S(2)}) %collective-permute-start.1) | collective-permute-done | bytes 1048608 | tf_op jit(solution)/shard_map/ppermute | solution.py:16
  19.8 1.5 collective-permute-done.other_grad_ref
  21.3 9.1 %root.1 = (f32[1024,1024]{1,0:T(8,128)}, bf16[1024,1536]{1,0:T(8,128)(2,1)}, bf16[1024,1024]{1,0:T(8,128)(2,1)S(1)}) custom-call(s32[1]{0:T(128)} %bitcast.6.index_ref, s32[256]{0:T(256)S(1)} %copy-done.3, s32[256]{0:T(256)S(1)} %copy-done.4, bf16[512,1024]{1,0:T(8,128)(2,1)S(1)} %copy-done.5, bf16[512,1024]{1,0:T(8,128)(2,1)S(1)} %collective-permute-done.other_grad_ref, ...), custom_call_target="tpu_custom_call" | custom-call | flops 8589934592 | bytes 17825792 | tf_op jit(solution)/shard_map/root/pallas_call | solution.py:472
  30.4 1.4 copy-done.6
  31.8 14.3 %all-to-all-done.5 = bf16[128,8,1024]{2,1,0:T(8,128)(2,1)} async-done(((bf16[128,8,1024]{2,1,0:T(8,128)(2,1)}), bf16[128,8,1024]{2,1,0:T(8,128)(2,1)}, u32[]{:S(2)}, u32[]{:S(2)}) %all-to-all-start.5) | async-done | bytes 2097184 | tf_op jit(solution)/shard_map/all_to_all | solution.py:20
  46.1 5.8 %all-to-all-start.4 = ((bf16[128,8,1536]{2,1,0:T(8,128)(2,1)}), bf16[128,8,1536]{2,1,0:T(8,128)(2,1)}, u32[]{:S(2)}, u32[]{:S(2)}) async-start(bf16[128,8,1536]{2,1,0:T(8,128)(2,1)} %bitcast.9), calls=%async_computation.4 | async-start | bytes 6291456 | tf_op jit(solution)/shard_map/all_to_all | solution.py:20
  58.7 34.6 %all-to-all-done.4.own_ref = bf16[128,8,1536]{2,1,0:T(8,128)(2,1)} async-done(((bf16[128,8,1536]{2,1,0:T(8,128)(2,1)}), bf16[128,8,1536]{2,1,0:T(8,128)(2,1)}, u32[]{:S(2)}, u32[]{:S(2)}) %all-to-all-start.4) | async-done | bytes 3145760 | tf_op jit(solution)/shard_map/all_to_all | solution.py:20
  93.3 5.2 %conditional.1 = ((bf16[128,8,1024]{2,1,0:T(8,128)(2,1)}, bf16[128,8,1024]{2,1,0:T(8,128)(2,1)})) conditional(s32[]{:T(128)} %clamp.3, (s32[128]{0:T(128)S(1)}, s32[128]{0:T(128)S(1)}, bf16[128,8,1536]{2,1,0:T(8,128)(2,1)}, bf16[128,8,1024]{2,1,0:T(8,128)(2,1)}) %tuple.23, (s32[]{:T(128)}, ...), branch_computations={%region_9.10_spmd, %region_10.11_spmd, %region_11.12_spmd, %region... | conditional | flops 8000524288 | bytes 32780902 | solution.py:598
  93.3 5.2 %pick.6 = (bf16[128,8,1024]{2,1,0:T(8,128)(2,1)}, bf16[128,8,1024]{2,1,0:T(8,128)(2,1)}) custom-call(s32[128]{0:T(128)S(1)} %get-tuple-element.48.kind_ref, s32[128]{0:T(128)S(1)} %get-tuple-element.49.row_ref, bf16[128,8,1536]{2,1,0:T(8,128)(2,1)} %get-tuple-element.50.own_ref, bf16[128,8,1024]{2,1,0:T(8,128)(2,1)} %get-tuple-element.51.refs_0_), custom_call_target="tpu_custom_call" | custom-call | flops 4000000000 | bytes 8000000 | tf_op jit(solution)/shard_map/cond/branch_0_fun/pick/pallas_call | solution.py:76
  98.5 35.8 %all_to_all.37 = bf16[128,8,1024]{2,1,0:T(8,128)(2,1)} all-to-all(bf16[128,8,1024]{2,1,0:T(8,128)(2,1)} %get-tuple-element.95), channel_id=1, replica_groups=mesh['dev'=128] {'dev'}, dimensions={0} | all-to-all | bytes 4194304 | tf_op jit(solution)/shard_map/all_to_all | solution.py:20
  134.4 1.3 collective-permute-start.4
  136.3 5.8 %route.1 = bf16[128,8,1536]{2,1,0:T(8,128)(2,1)S(1)} custom-call(s32[128]{0:T(128)S(1)} %fusion.24.row_ref, s32[64]{0:T(128)S(1)} %select_n.159.shared_row_ref, bf16[128,8,1536]{2,1,0:T(8,128)(2,1)} %all-to-all-done.4.own_ref), custom_call_target="tpu_custom_call" | custom-call | flops 4000000000 | bytes 12000000 | tf_op jit(solution)/shard_map/route/pallas_call | solution.py:114
  142.2 1.7 copy-done.1
  143.9 3.6 %all-to-all-start.7 = ((bf16[128,8,1536]{2,1,0:T(8,128)(2,1)}), bf16[128,8,1536]{2,1,0:T(8,128)(2,1)S(1)}, u32[]{:S(2)}, u32[]{:S(2)}) async-start(bf16[128,8,1536]{2,1,0:T(8,128)(2,1)} %copy-done.1), calls=%async_computation.7 | async-start | bytes 6291456 | tf_op jit(solution)/shard_map/all_to_all | solution.py:20
  147.5 7.2 %fusion.2 = (bf16[1024,1024]{1,0:T(8,128)(2,1)}, bf16[1024,1024]{1,0:T(8,128)(2,1)}) fusion(bf16[1024,1024]{1,0:T(8,128)(2,1)} %collective-permute-done.4, bf16[128,8,1024]{2,1,0:T(8,128)(2,1)} %get-tuple-element.97, pred[]{:T(512)} %get-tuple-element.154, pred[]{:T(512)} %get-tuple-element.155, bf16[128,8,1024]{2,1,0:T(8,128)(2,1)} %all_to_all.37, ...), kind=kLoop, calls=%fused_computation.9 | loop fusion | flops 3145728 | bytes 12582914 | tf_op jit(solution)/shard_map/jit(_where)/select_n | solution.py:610
  159.9 7.1 %multiply_reduce_fusion = (f32[]{:T(128)}, f32[512,1024]{1,0:T(8,128)}) fusion(bf16[1024,1024]{1,0:T(8,128)(2,1)} %collective-permute-done.2, bf16[1024,1024]{1,0:T(8,128)(2,1)} %get-tuple-element.165, pred[]{:T(512)S(6)} %eq.86, bf16[1024,1024]{1,0:T(8,128)(2,1)} %copy-done.6, s32[]{:T(128)S(6)} %select_n.164), kind=kOutput, calls=%fused_computation.13 | convolution fusion | flops 2150629376 | bytes 10487300 | tf_op jit(solution)/shard_map/dot_general | solution.py:625
  169.6 2.8 %multiply_convert_fusion = bf16[512,1024]{1,0:T(8,128)(2,1)} fusion(f32[512,1024]{1,0:T(8,128)} %get-tuple-element.169, f32[]{:T(128)S(6)} %rsqrt.3), kind=kLoop, calls=%fused_computation.12 | loop fusion | flops 1048576 | bytes 3145732 | tf_op jit(solution)/shard_map/convert_element_type | solution.py:629
  172.4 16.7 %all-to-all-done.7 = bf16[128,8,1536]{2,1,0:T(8,128)(2,1)S(1)} async-done(((bf16[128,8,1536]{2,1,0:T(8,128)(2,1)}), bf16[128,8,1536]{2,1,0:T(8,128)(2,1)S(1)}, u32[]{:S(2)}, u32[]{:S(2)}) %all-to-all-start.7) | async-done | bytes 3145760 | tf_op jit(solution)/shard_map/all_to_all | solution.py:20
  189.2 1.1 collective-permute-start.5
  190.7 3.9 %bitcast_select_fusion.2 = bf16[1,1024,1024]{2,1,0:T(8,128)(2,1)} fusion(bf16[1,1024,1024]{2,1,0:T(8,128)(2,1)S(1)} %copy-done.7, bf16[128,8,1024]{2,1,0:T(8,128)(2,1)} %all_to_all.37, pred[]{:T(512)} %get-tuple-element.155), kind=kLoop, calls=%fused_computation.11 | loop fusion | flops 1048576 | bytes 6291457 | tf_op jit(solution)/shard_map/jit(_where)/select_n | solution.py:609
  194.7 3.0 %place.1 = bf16[2,1024,1024]{2,1,0:T(8,128)(2,1)} custom-call(s32[3]{0:T(128)S(1)} %pad_add_fusion.code_ref, bf16[1024,1536]{1,0:T(8,128)(2,1)S(1)} %bitcast.36, bf16[1024,512]{1,0:T(8,128)(2,1)S(1)} %collective-permute-done.5.other_ref, bf16[1024,1024]{1,0:T(8,128)(2,1)S(1)} %copy-done, bf16[256,1024]{1,0:T(8,128)(2,1)S(1)} %broadcast_in_dim.65.zero_ref), custom_call_target="tpu_custom_call" | custom-call | tf_op jit(solution)/shard_map/place/pallas_call | solution.py:182
  (65 shorter events, 12.0 us)
Async XLA Ops:
  0.6 0.7 copy-start.2
  4.3 13.2 %copy-start.5 = (bf16[512,1024]{1,0:T(8,128)(2,1)S(1)}, bf16[512,1024]{1,0:T(8,128)(2,1)}, u32[]{:S(2)}) copy-start(bf16[512,1024]{1,0:T(8,128)(2,1)} %own_grad_ref.1) | copy-start | bytes 3145732
  4.3 17.0 %copy-start.3 = (s32[256]{0:T(256)S(1)}, s32[256]{0:T(256)}, u32[]{:S(2)}) copy-start(s32[256]{0:T(256)} %pending_stat_ref.1) | copy-start | bytes 3076
  4.3 17.0 %copy-start.4 = (s32[256]{0:T(256)S(1)}, s32[256]{0:T(256)}, u32[]{:S(2)}) copy-start(s32[256]{0:T(256)} %refresh_stat_ref.1) | copy-start | bytes 3076
  4.4 41.7 %all-to-all-start.5 = ((bf16[128,8,1024]{2,1,0:T(8,128)(2,1)}), bf16[128,8,1024]{2,1,0:T(8,128)(2,1)}, u32[]{:S(2)}, u32[]{:S(2)}) async-start(bf16[128,8,1024]{2,1,0:T(8,128)(2,1)} %bitcast.10), calls=%async_computation.5 | async-start | bytes 4194304 | tf_op jit(solution)/shard_map/all_to_all | solution.py:20
  16.3 3.5 %collective-permute-start.1 = (bf16[1024,512]{1,0:T(8,128)(2,1)S(1)}, bf16[1024,512]{1,0:T(8,128)(2,1)S(1)}, u32[]{:S(2)}, u32[]{:S(2)}) collective-permute-start(bf16[1024,512]{1,0:T(8,128)(2,1)S(1)} %get-tuple-element.91), channel_id=1, source_target_pairs={{0,1},{1,0},{2,3},{3,2},{4,5},{5,4},{6,7},{7,6},{8,9},{9,8},{10,11... | collective-permute-start | bytes 3145736 | tf_op jit(solution)/shard_map/ppermute | solution.py:16
  17.5 3.8 %collective-permute-start = (bf16[512,1024]{1,0:T(8,128)(2,1)S(1)}, bf16[512,1024]{1,0:T(8,128)(2,1)S(1)}, u32[]{:S(2)}, u32[]{:S(2)}) collective-permute-start(bf16[512,1024]{1,0:T(8,128)(2,1)S(1)} %copy-done.5), channel_id=1, source_target_pairs={{0,1},{1,0},{2,3},{3,2},{4,5},{5,4},{6,7},{7,6},{8,9},{9,8},{10,11... | collective-permute-start | bytes 3145736 | tf_op jit(solution)/shard_map/ppermute | solution.py:16
  30.4 1.4 copy-start.6
  46.1 47.3 %all-to-all-start.4 = ((bf16[128,8,1536]{2,1,0:T(8,128)(2,1)}), bf16[128,8,1536]{2,1,0:T(8,128)(2,1)}, u32[]{:S(2)}, u32[]{:S(2)}) async-start(bf16[128,8,1536]{2,1,0:T(8,128)(2,1)} %bitcast.9), calls=%async_computation.4 | async-start | bytes 6291456 | tf_op jit(solution)/shard_map/all_to_all | solution.py:20
  134.4 13.1 %collective-permute-start.4 = (bf16[1024,1024]{1,0:T(8,128)(2,1)}, bf16[1024,1024]{1,0:T(8,128)(2,1)}, u32[]{:S(2)}, u32[]{:S(2)}) collective-permute-start(bf16[1024,1024]{1,0:T(8,128)(2,1)} %bitcast.13), channel_id=1, source_target_pairs={{0,1},{1,0},{2,3},{3,2},{4,5},{5,4},{6,7},{7,6},{8,9},{9,8},{10,11... | collective-permute-start | bytes 6291464 | tf_op jit(solution)/shard_map/ppermute | solution.py:16
  142.2 1.7 copy-start.1
  143.9 45.3 %all-to-all-start.7 = ((bf16[128,8,1536]{2,1,0:T(8,128)(2,1)}), bf16[128,8,1536]{2,1,0:T(8,128)(2,1)S(1)}, u32[]{:S(2)}, u32[]{:S(2)}) async-start(bf16[128,8,1536]{2,1,0:T(8,128)(2,1)} %copy-done.1), calls=%async_computation.7 | async-start | bytes 6291456 | tf_op jit(solution)/shard_map/all_to_all | solution.py:20
  154.7 5.2 %collective-permute-start.2 = (bf16[1024,1024]{1,0:T(8,128)(2,1)}, bf16[1024,1024]{1,0:T(8,128)(2,1)}, u32[]{:S(2)}, u32[]{:S(2)}) collective-permute-start(bf16[1024,1024]{1,0:T(8,128)(2,1)} %get-tuple-element.165), channel_id=1, source_target_pairs={{0,1},{1,0},{2,3},{3,2},{4,5},{5,4},{6,7},{7,6},{8,9},{9,8},{10,11... | collective-permute-start | bytes 6291464 | tf_op jit(solution)/shard_map/ppermute | solution.py:16
  167.0 1.3 collective-permute-start.3
  189.1 1.6 copy-start.7
  189.2 5.5 %copy-start = (bf16[1024,1024]{1,0:T(8,128)(2,1)S(1)}, bf16[1024,1024]{1,0:T(8,128)(2,1)}, u32[]{:S(2)}) copy-start(bf16[1024,1024]{1,0:T(8,128)(2,1)} %get-tuple-element.101.late_ref) | copy-start | bytes 6291460
  189.2 5.4 %collective-permute-start.5 = (bf16[1024,512]{1,0:T(8,128)(2,1)S(1)}, bf16[1024,512]{1,0:T(8,128)(2,1)S(1)}, u32[]{:S(2)}, u32[]{:S(2)}) collective-permute-start(bf16[1024,512]{1,0:T(8,128)(2,1)S(1)} %slice.86), channel_id=1, source_target_pairs={{0,1},{1,0},{2,3},{3,2},{4,5},{5,4},{6,7},{7,6},{8,9},{9,8},{10,11... | collective-permute-start | bytes 3145736 | tf_op jit(solution)/shard_map/ppermute | solution.py:16

commit v5 on v4

--- a/solution.py
+++ b/solution.py
@@ -197,21 +197,17 @@
 CHUNKS = 4
 
 
-def first_kernel(index_ref, stat_ref, pending_ref, first_ref, columns_ref, held, cut, sems):
-    rows, width = first_ref.shape
-    half, step = width // 2, rows // CHUNKS
+def first_kernel(index_ref, stat_ref, pending_ref, first_ref, held, sems):
+    step = first_ref.shape[0] // CHUNKS
     slot = jnp.where(stat_ref[index_ref[0] * 2] >= 0, 0, 1)
-    other_half = pl.ds(pl.multiple_of((1 - index_ref[0] % 2) * half, half), half)
-    moves = []
-    for chunk in range(CHUNKS):
-        part = pl.ds(chunk * step, step)
-        moves.append((pending_ref.at[slot, part, :], held.at[part, :], first_ref.at[part, :]))
-    moves.append((pending_ref.at[1, :, other_half], cut, columns_ref))
+    parts = [pl.ds(chunk * step, step) for chunk in range(CHUNKS)]
     loads = [
-        pltpu.make_async_copy(src, mid, sems.at[0, pos]) for pos, (src, mid, dst) in enumerate(moves)
+        pltpu.make_async_copy(pending_ref.at[slot, part, :], held.at[part, :], sems.at[0, pos])
+        for pos, part in enumerate(parts)
     ]
     stores = [
-        pltpu.make_async_copy(mid, dst, sems.at[1, pos]) for pos, (src, mid, dst) in enumerate(moves)
+        pltpu.make_async_copy(held.at[part, :], first_ref.at[part, :], sems.at[1, pos])
+        for pos, part in enumerate(parts)
     ]
     for load in loads:
         load.start()
@@ -223,22 +219,14 @@
 
 
 def first_used(my_index, pending_stat, pending_roots):
-    rows, width = pending_roots.shape[1:]
-    kind = pending_roots.dtype
+    shape, kind = pending_roots.shape[1:], pending_roots.dtype
     anywhere = pl.BlockSpec(memory_space=pl.ANY)
     return pl.pallas_call(
         first_kernel,
-        out_shape=(
-            jax.ShapeDtypeStruct((rows, width), kind),
-            jax.ShapeDtypeStruct((rows, width // 2), kind),
-        ),
+        out_shape=jax.ShapeDtypeStruct(shape, kind),
         in_specs=[pl.BlockSpec(memory_space=pltpu.SMEM)] * 2 + [anywhere],
-        out_specs=(anywhere, anywhere),
-        scratch_shapes=[
-            pltpu.VMEM((rows, width), kind),
-            pltpu.VMEM((rows, width // 2), kind),
-            pltpu.SemaphoreType.DMA((2, CHUNKS + 1)),
-        ],
+        out_specs=anywhere,
+        scratch_shapes=[pltpu.VMEM(shape, kind), pltpu.SemaphoreType.DMA((2, CHUNKS))],
         compiler_params=pltpu.CompilerParams(vmem_limit_bytes=8 * 1024 * 1024),
         name="first_used",
     )(my_index, pending_stat, pending_roots)
@@ -522,8 +510,11 @@
     device_ids = jnp.arange(devices, dtype=jnp.int32)
 
     index_table = my_index.reshape(1)
-    first_root, cut_columns = first_used(index_table, pending_stat, pending_roots)
+    first_root = first_used(index_table, pending_stat, pending_roots)
     first_parts = spread(first_root.reshape(devices, piece_rows, block_width))
+    cut_columns = lax.dynamic_slice(
+        pending_roots, (1, 0, (1 - parity) * half_columns), (1, block_width, half_columns)
+    )[0]
     other_columns = swapped(cut_columns, "dev", 0)
 
     new_stat, own_matrix, full_grad = updated_and_root(
@@ -606,12 +597,11 @@
 
     my_found = jnp.any(pending_stat == my_index)
     partner_found = jnp.any(pending_stat == my_index + 1 - 2 * parity)
-    merged = jnp.where(my_found, returned, held_roots[0])
+    other_returned = swapped(returned, "dev", 0)
+    merged = lax.optimization_barrier(jnp.where(my_found, returned, held_roots[0]))
     late = jnp.where(
         my_found,
-        jnp.where(
-            partner_found, spare.reshape(block_width, block_width), swapped(returned, "dev", 0)
-        ),
+        jnp.where(partner_found, spare.reshape(block_width, block_width), other_returned),
         returned,
     )
 

time: 199 us -> 197 us (0.990)
  other arithmetic: 17.6 us -> 13.7 us
    select_n x1 -> x0, other arithmetic: 3.88 us -> none  [per_device(): merged = jnp.where(my_found, returned, held_roots[0])]
    ppermute x6, waiting for transfers between devices: 5.37 us -> 7.78 us  [swapped(): lax.ppermute(shard, axis, [(i, i ^ 1 << bit) for i in range(lax.axis_size...]
    unnamed x16 -> x14, local copies, waits for them, and re-layouts: 4.13 us -> 3.72 us
  transfers between devices with their start and end apart: 9 -> 9, of which waited for: 7 -> 8; matrix products, arithmetic and copies ran while one was open for 14% -> 13% of each run, Pallas kernels for 8% -> 8%
where the time goes in v5:
time: 197 us; the launch traced here: 196 us
  waiting for transfers between devices  71.8 us (36%)
  blocking collectives  35.8 us (18%)
  starting transfers between devices  26.5 us (13%)
  Pallas kernels  26 us (13%)
  other arithmetic  13.7 us (7%)
  local copies, waits for them, and re-layouts  9.03 us (5%)
  matrix products  7.22 us (4%)
  between operations  5.65 us (3%)
    all_to_all x3, waiting for transfers between devices, spread(): return lax.all_to_all(parts, 'dev', split_axis=0, concat_axis=0, tiled=True)  64 us
    all_to_all x1, blocking collectives, spread(): return lax.all_to_all(parts, 'dev', split_axis=0, concat_axis=0, tiled=True)  35.8 us
    all_to_all x3, starting transfers between devices, spread(): return lax.all_to_all(parts, 'dev', split_axis=0, concat_axis=0, tiled=True)  21.3 us
    pallas_call x1, Pallas kernels, updated_and_root(): pl.pallas_call(root_kernel, out_shape=(jax.ShapeDtypeStruct((width, width...  9.06 us
    ppermute x6, waiting for transfers between devices, swapped(): lax.ppermute(shard, axis, [(i, i ^ 1 << bit) for i in range(lax.axis_size...  7.78 us
    dot_general x1, matrix products, per_device(): jnp.dot(left_times, right_root, preferred_element_type=jnp.float32)  7.22 us
    select_n x1, other arithmetic, per_device(): jnp.where(my_found, jnp.where(partner_found, spare.reshape(block_width, b...  7.17 us
    pallas_call x1, Pallas kernels, route(): pl.pallas_call(route_kernel, out_shape=jax.ShapeDtypeStruct(own.shape, ow...  5.84 us
  transfers between devices with their start and end apart: 9, of which 8 were waited for; matrix products, arithmetic and copies ran while one was open for 13% of the time, Pallas kernels for 8%

profile of v5, /device:TPU:1, one launch (start us, length us, event | category | flops | bytes accessed | tf_op | source)
XLA Modules:
  0.0 195.7 jit_solution(8761453437031284125)
XLA Ops:
  1.3 3.0 %first_used.1 = bf16[1024,1024]{1,0:T(8,128)(2,1)} custom-call(s32[1]{0:T(128)} %bitcast.6.index_ref, s32[256]{0:T(256)S(1)} %copy-done.2, bf16[2,1024,1024]{2,1,0:T(8,128)(2,1)} %pending_ref.3), custom_call_target="tpu_custom_call" | custom-call | tf_op jit(solution)/shard_map/first_used/pallas_call | solution.py:224
  4.3 12.0 %all-to-all-start.5 = ((bf16[128,8,1024]{2,1,0:T(8,128)(2,1)}), bf16[128,8,1024]{2,1,0:T(8,128)(2,1)}, u32[]{:S(2)}, u32[]{:S(2)}) async-start(bf16[128,8,1024]{2,1,0:T(8,128)(2,1)} %bitcast.11), calls=%async_computation.5 | async-start | bytes 4194304 | tf_op jit(solution)/shard_map/all_to_all | solution.py:20
  16.3 1.4 dynamic-slice_bitcast_fusion
  17.7 1.2 collective-permute-start.1
  19.0 2.2 %collective-permute-done.1.other_ref = bf16[1024,512]{1,0:T(8,128)(2,1)S(1)} collective-permute-done((bf16[1024,512]{1,0:T(8,128)(2,1)S(1)}, bf16[1024,512]{1,0:T(8,128)(2,1)S(1)}, u32[]{:S(2)}, u32[]{:S(2)}) %collective-permute-start.1) | collective-permute-done | bytes 1048608 | tf_op jit(solution)/shard_map/ppermute | solution.py:16
  21.2 1.5 collective-permute-done.other_grad_ref
  22.7 9.1 %root.1 = (f32[1024,1024]{1,0:T(8,128)}, bf16[1024,1536]{1,0:T(8,128)(2,1)}, bf16[1024,1024]{1,0:T(8,128)(2,1)S(1)}) custom-call(s32[1]{0:T(128)} %bitcast.6.index_ref, s32[256]{0:T(256)S(1)} %copy-done.3, s32[256]{0:T(256)S(1)} %copy-done.4, bf16[512,1024]{1,0:T(8,128)(2,1)S(1)} %copy-done.5, bf16[512,1024]{1,0:T(8,128)(2,1)S(1)} %collective-permute-done.other_grad_ref, ...), custom_call_target="tpu_custom_call" | custom-call | flops 8589934592 | bytes 17825792 | tf_op jit(solution)/shard_map/root/pallas_call | solution.py:460
  31.8 1.4 copy-done.6
  33.1 12.9 %all-to-all-done.5 = bf16[128,8,1024]{2,1,0:T(8,128)(2,1)} async-done(((bf16[128,8,1024]{2,1,0:T(8,128)(2,1)}), bf16[128,8,1024]{2,1,0:T(8,128)(2,1)}, u32[]{:S(2)}, u32[]{:S(2)}) %all-to-all-start.5) | async-done | bytes 2097184 | tf_op jit(solution)/shard_map/all_to_all | solution.py:20
  46.0 5.8 %all-to-all-start.4 = ((bf16[128,8,1536]{2,1,0:T(8,128)(2,1)}), bf16[128,8,1536]{2,1,0:T(8,128)(2,1)}, u32[]{:S(2)}, u32[]{:S(2)}) async-start(bf16[128,8,1536]{2,1,0:T(8,128)(2,1)} %bitcast.10), calls=%async_computation.4 | async-start | bytes 6291456 | tf_op jit(solution)/shard_map/all_to_all | solution.py:20
  58.6 34.6 %all-to-all-done.4.own_ref = bf16[128,8,1536]{2,1,0:T(8,128)(2,1)} async-done(((bf16[128,8,1536]{2,1,0:T(8,128)(2,1)}), bf16[128,8,1536]{2,1,0:T(8,128)(2,1)}, u32[]{:S(2)}, u32[]{:S(2)}) %all-to-all-start.4) | async-done | bytes 3145760 | tf_op jit(solution)/shard_map/all_to_all | solution.py:20
  93.3 5.2 %conditional.1 = ((bf16[128,8,1024]{2,1,0:T(8,128)(2,1)}, bf16[128,8,1024]{2,1,0:T(8,128)(2,1)})) conditional(s32[]{:T(128)} %clamp.3, (s32[128]{0:T(128)S(1)}, s32[128]{0:T(128)S(1)}, bf16[128,8,1536]{2,1,0:T(8,128)(2,1)}, bf16[128,8,1024]{2,1,0:T(8,128)(2,1)}) %tuple.23, (s32[]{:T(128)}, ...), branch_computations={%region_9.10_spmd, %region_10.11_spmd, %region_11.12_spmd, %region... | conditional | flops 8000524288 | bytes 32780902 | solution.py:589
  93.3 5.2 %pick.6 = (bf16[128,8,1024]{2,1,0:T(8,128)(2,1)}, bf16[128,8,1024]{2,1,0:T(8,128)(2,1)}) custom-call(s32[128]{0:T(128)S(1)} %get-tuple-element.48.kind_ref, s32[128]{0:T(128)S(1)} %get-tuple-element.49.row_ref, bf16[128,8,1536]{2,1,0:T(8,128)(2,1)} %get-tuple-element.50.own_ref, bf16[128,8,1024]{2,1,0:T(8,128)(2,1)} %get-tuple-element.51.refs_0_), custom_call_target="tpu_custom_call" | custom-call | flops 4000000000 | bytes 8000000 | tf_op jit(solution)/shard_map/cond/branch_0_fun/pick/pallas_call | solution.py:76
  98.5 35.8 %all_to_all.37 = bf16[128,8,1024]{2,1,0:T(8,128)(2,1)} all-to-all(bf16[128,8,1024]{2,1,0:T(8,128)(2,1)} %get-tuple-element.91), channel_id=1, replica_groups=mesh['dev'=128] {'dev'}, dimensions={0} | all-to-all | bytes 4194304 | tf_op jit(solution)/shard_map/all_to_all | solution.py:20
  134.3 1.3 collective-permute-start.4
  136.3 5.8 %route.1 = bf16[128,8,1536]{2,1,0:T(8,128)(2,1)S(1)} custom-call(s32[128]{0:T(128)S(1)} %fusion.26.row_ref, s32[64]{0:T(128)S(1)} %select_n.158.shared_row_ref, bf16[128,8,1536]{2,1,0:T(8,128)(2,1)} %all-to-all-done.4.own_ref), custom_call_target="tpu_custom_call" | custom-call | flops 4000000000 | bytes 12000000 | tf_op jit(solution)/shard_map/route/pallas_call | solution.py:114
  142.1 1.7 copy-done.1
  143.8 3.6 %all-to-all-start.7 = ((bf16[128,8,1536]{2,1,0:T(8,128)(2,1)}), bf16[128,8,1536]{2,1,0:T(8,128)(2,1)S(1)}, u32[]{:S(2)}, u32[]{:S(2)}) async-start(bf16[128,8,1536]{2,1,0:T(8,128)(2,1)} %copy-done.1), calls=%async_computation.7 | async-start | bytes 6291456 | tf_op jit(solution)/shard_map/all_to_all | solution.py:20
  147.4 7.2 %fusion.2 = (bf16[1024,1024]{1,0:T(8,128)(2,1)}, bf16[1024,1024]{1,0:T(8,128)(2,1)}) fusion(bf16[1024,1024]{1,0:T(8,128)(2,1)} %collective-permute-done.4, bf16[128,8,1024]{2,1,0:T(8,128)(2,1)} %get-tuple-element.93, pred[]{:T(512)} %get-tuple-element.150, pred[]{:T(512)} %get-tuple-element.151, bf16[128,8,1024]{2,1,0:T(8,128)(2,1)} %all_to_all.37, ...), kind=kLoop, calls=%fused_computation.9 | loop fusion | flops 3145728 | bytes 12582914 | tf_op jit(solution)/shard_map/jit(_where)/select_n | solution.py:602
  159.8 7.2 %multiply_reduce_fusion = (f32[]{:T(128)}, f32[512,1024]{1,0:T(8,128)}) fusion(bf16[1024,1024]{1,0:T(8,128)(2,1)} %collective-permute-done.2, bf16[1024,1024]{1,0:T(8,128)(2,1)} %get-tuple-element.161, pred[]{:T(512)S(6)} %eq.86, bf16[1024,1024]{1,0:T(8,128)(2,1)} %copy-done.6, s32[]{:T(128)S(6)} %select_n.161), kind=kOutput, calls=%fused_computation.12 | convolution fusion | flops 2150629376 | bytes 10487300 | tf_op jit(solution)/shard_map/dot_general | solution.py:615
  169.8 2.8 %multiply_convert_fusion = bf16[512,1024]{1,0:T(8,128)(2,1)} fusion(f32[512,1024]{1,0:T(8,128)} %get-tuple-element.165, f32[]{:T(128)S(6)} %rsqrt.3), kind=kLoop, calls=%fused_computation.11 | loop fusion | flops 1048576 | bytes 3145732 | tf_op jit(solution)/shard_map/convert_element_type | solution.py:619
  172.6 16.5 %all-to-all-done.7 = bf16[128,8,1536]{2,1,0:T(8,128)(2,1)S(1)} async-done(((bf16[128,8,1536]{2,1,0:T(8,128)(2,1)}), bf16[128,8,1536]{2,1,0:T(8,128)(2,1)S(1)}, u32[]{:S(2)}, u32[]{:S(2)}) %all-to-all-start.7) | async-done | bytes 3145760 | tf_op jit(solution)/shard_map/all_to_all | solution.py:20
  190.3 2.3 %collective-permute-done.5.other_ref = bf16[1024,512]{1,0:T(8,128)(2,1)S(1)} collective-permute-done((bf16[1024,512]{1,0:T(8,128)(2,1)S(1)}, bf16[1024,512]{1,0:T(8,128)(2,1)S(1)}, u32[]{:S(2)}, u32[]{:S(2)}) %collective-permute-start.5) | collective-permute-done | bytes 1048608 | tf_op jit(solution)/shard_map/ppermute | solution.py:16
  192.6 3.0 %place.1 = bf16[2,1024,1024]{2,1,0:T(8,128)(2,1)} custom-call(s32[3]{0:T(128)S(1)} %pad_add_fusion.code_ref, bf16[1024,1536]{1,0:T(8,128)(2,1)S(1)} %bitcast.37, bf16[1024,512]{1,0:T(8,128)(2,1)S(1)} %collective-permute-done.5.other_ref, bf16[1024,1024]{1,0:T(8,128)(2,1)S(1)} %copy-done, bf16[256,1024]{1,0:T(8,128)(2,1)S(1)} %broadcast_in_dim.68.zero_ref), custom_call_target="tpu_custom_call" | custom-call | tf_op jit(solution)/shard_map/place/pallas_call | solution.py:182
  (63 shorter events, 12.8 us)
Async XLA Ops:
  0.6 0.7 copy-start.2
  4.3 41.7 %all-to-all-start.5 = ((bf16[128,8,1024]{2,1,0:T(8,128)(2,1)}), bf16[128,8,1024]{2,1,0:T(8,128)(2,1)}, u32[]{:S(2)}, u32[]{:S(2)}) async-start(bf16[128,8,1024]{2,1,0:T(8,128)(2,1)} %bitcast.11), calls=%async_computation.5 | async-start | bytes 4194304 | tf_op jit(solution)/shard_map/all_to_all | solution.py:20
  16.3 2.7 %copy-start.5 = (bf16[512,1024]{1,0:T(8,128)(2,1)S(1)}, bf16[512,1024]{1,0:T(8,128)(2,1)}, u32[]{:S(2)}) copy-start(bf16[512,1024]{1,0:T(8,128)(2,1)} %own_grad_ref.1) | copy-start | bytes 3145732
  16.3 6.4 %copy-start.3 = (s32[256]{0:T(256)S(1)}, s32[256]{0:T(256)}, u32[]{:S(2)}) copy-start(s32[256]{0:T(256)} %stat_ref.1) | copy-start | bytes 3076
  16.3 6.4 %copy-start.4 = (s32[256]{0:T(256)S(1)}, s32[256]{0:T(256)}, u32[]{:S(2)}) copy-start(s32[256]{0:T(256)} %refresh_stat_ref.1) | copy-start | bytes 3076
  17.7 3.5 %collective-permute-start.1 = (bf16[1024,512]{1,0:T(8,128)(2,1)S(1)}, bf16[1024,512]{1,0:T(8,128)(2,1)S(1)}, u32[]{:S(2)}, u32[]{:S(2)}) collective-permute-start(bf16[1024,512]{1,0:T(8,128)(2,1)S(1)} %dynamic-slice_bitcast_fusion), channel_id=1, source_target_pairs={{0,1},{1,0},{2,3},{3,2},{4,5},{5,4},{6,7},{7,6},{8,9},{9,8},{10,11... | collective-permute-start | bytes 3145736 | tf_op jit(solution)/shard_map/ppermute | solution.py:16
  18.9 3.8 %collective-permute-start = (bf16[512,1024]{1,0:T(8,128)(2,1)S(1)}, bf16[512,1024]{1,0:T(8,128)(2,1)S(1)}, u32[]{:S(2)}, u32[]{:S(2)}) collective-permute-start(bf16[512,1024]{1,0:T(8,128)(2,1)S(1)} %copy-done.5), channel_id=1, source_target_pairs={{0,1},{1,0},{2,3},{3,2},{4,5},{5,4},{6,7},{7,6},{8,9},{9,8},{10,11... | collective-permute-start | bytes 3145736 | tf_op jit(solution)/shard_map/ppermute | solution.py:16
  31.8 1.4 copy-start.6
  46.0 47.3 %all-to-all-start.4 = ((bf16[128,8,1536]{2,1,0:T(8,128)(2,1)}), bf16[128,8,1536]{2,1,0:T(8,128)(2,1)}, u32[]{:S(2)}, u32[]{:S(2)}) async-start(bf16[128,8,1536]{2,1,0:T(8,128)(2,1)} %bitcast.10), calls=%async_computation.4 | async-start | bytes 6291456 | tf_op jit(solution)/shard_map/all_to_all | solution.py:20
  134.3 13.1 %collective-permute-start.4 = (bf16[1024,1024]{1,0:T(8,128)(2,1)}, bf16[1024,1024]{1,0:T(8,128)(2,1)}, u32[]{:S(2)}, u32[]{:S(2)}) collective-permute-start(bf16[1024,1024]{1,0:T(8,128)(2,1)} %bitcast.12), channel_id=1, source_target_pairs={{0,1},{1,0},{2,3},{3,2},{4,5},{5,4},{6,7},{7,6},{8,9},{9,8},{10,11... | collective-permute-start | bytes 6291464 | tf_op jit(solution)/shard_map/ppermute | solution.py:16
  142.1 1.7 copy-start.1
  143.8 45.3 %all-to-all-start.7 = ((bf16[128,8,1536]{2,1,0:T(8,128)(2,1)}), bf16[128,8,1536]{2,1,0:T(8,128)(2,1)S(1)}, u32[]{:S(2)}, u32[]{:S(2)}) async-start(bf16[128,8,1536]{2,1,0:T(8,128)(2,1)} %copy-done.1), calls=%async_computation.7 | async-start | bytes 6291456 | tf_op jit(solution)/shard_map/all_to_all | solution.py:20
  154.6 5.2 %collective-permute-start.2 = (bf16[1024,1024]{1,0:T(8,128)(2,1)}, bf16[1024,1024]{1,0:T(8,128)(2,1)}, u32[]{:S(2)}, u32[]{:S(2)}) collective-permute-start(bf16[1024,1024]{1,0:T(8,128)(2,1)} %get-tuple-element.161), channel_id=1, source_target_pairs={{0,1},{1,0},{2,3},{3,2},{4,5},{5,4},{6,7},{7,6},{8,9},{9,8},{10,11... | collective-permute-start | bytes 6291464 | tf_op jit(solution)/shard_map/ppermute | solution.py:16
  167.0 1.5 collective-permute-start.3
  189.1 3.5 %copy-start = (bf16[1024,1024]{1,0:T(8,128)(2,1)S(1)}, bf16[1024,1024]{1,0:T(8,128)(2,1)}, u32[]{:S(2)}) copy-start(bf16[1024,1024]{1,0:T(8,128)(2,1)} %get-tuple-element.97.late_ref) | copy-start | bytes 6291460
  189.2 3.4 %collective-permute-start.5 = (bf16[1024,512]{1,0:T(8,128)(2,1)S(1)}, bf16[1024,512]{1,0:T(8,128)(2,1)S(1)}, u32[]{:S(2)}, u32[]{:S(2)}) collective-permute-start(bf16[1024,512]{1,0:T(8,128)(2,1)S(1)} %slice.86), channel_id=1, source_target_pairs={{0,1},{1,0},{2,3},{3,2},{4,5},{5,4},{6,7},{7,6},{8,9},{9,8},{10,11... | collective-permute-start | bytes 3145736 | tf_op jit(solution)/shard_map/ppermute | solution.py:16

commit v6 on v5

--- a/solution.py
+++ b/solution.py
@@ -24,20 +24,46 @@
 EMPTY, PLAIN, HALVES, LATE = range(4)
 
 
-def pick_kernel(kind_ref, row_ref, own_ref, *refs):
-    tables, out_ref, sem = refs[:-3], refs[-3], refs[-1]
-    width = out_ref.shape[2]
+def gather_kernel(row_ref, table_ref, out_ref, sem):
+    def issue(item, carry):
+        pltpu.make_async_copy(table_ref.at[row_ref[item]], out_ref.at[item], sem).start()
+        return carry
+
+    lax.fori_loop(0, out_ref.shape[0], issue, 0, unroll=8)
+    pltpu.make_async_copy(out_ref, out_ref, sem).wait()
+
+
+def gather(row, table):
+    return pl.pallas_call(
+        gather_kernel,
+        out_shape=jax.ShapeDtypeStruct(table.shape, table.dtype),
+        in_specs=[
+            pl.BlockSpec(memory_space=pltpu.SMEM),
+            pl.BlockSpec(memory_space=pl.ANY),
+        ],
+        out_specs=pl.BlockSpec(memory_space=pltpu.VMEM),
+        scratch_shapes=[pltpu.SemaphoreType.DMA],
+        compiler_params=pltpu.CompilerParams(vmem_limit_bytes=8 * 1024 * 1024),
+        cost_estimate=pl.CostEstimate(
+            flops=4 * 1000 * 1000 * 1000, bytes_accessed=8 * 1000 * 1000, transcendentals=0
+        ),
+        name="gather",
+    )(row, table)
+
+
+def pick_kernel(kind_ref, row_ref, base_ref, own_ref, *refs):
+    tables, out_ref, base_sem, sems = refs[:-4], refs[-4], refs[-2], refs[-1]
+    items, _, width = out_ref.shape
     half = width // 2
-
-    def start(src, dst):
-        pltpu.make_async_copy(src, dst, sem).start()
+    base = pltpu.make_async_copy(base_ref, out_ref, base_sem)
+    base.start()
+    base.wait()
 
     def issue(item, carry):
         row, kind = row_ref[item], kind_ref[item]
 
-        @pl.when(kind == FIRST)
-        def _():
-            start(tables[0].at[row], out_ref.at[item])
+        def start(src, dst):
+            pltpu.make_async_copy(src, dst, sems.at[item]).start()
 
         @pl.when(kind != FIRST)
         def _():
@@ -53,38 +79,47 @@
                         out_ref.at[item, :, pl.ds(core * half, half)],
                     )
 
-            if len(tables) > 1:
+            if tables:
 
                 @pl.when(kind == EXTRA)
                 def _():
                     for core in range(2):
                         start(
-                            tables[1].at[row // 2 * 2 + core],
+                            tables[0].at[row // 2 * 2 + core],
                             out_ref.at[item, :, pl.ds(core * half, half)],
                         )
 
         return carry
 
-    lax.fori_loop(0, out_ref.shape[0], issue, 0, unroll=8)
-    pltpu.make_async_copy(out_ref, out_ref, sem).wait()
-
-
-def pick(kind, row, *tables):
-    items, (_, piece_rows, width) = row.shape[0], tables[1].shape
-    shape = jax.ShapeDtypeStruct((items, piece_rows, width), tables[0].dtype)
+    def finish(item, carry):
+        @pl.when(kind_ref[item] != FIRST)
+        def _():
+            pltpu.make_async_copy(out_ref.at[item], out_ref.at[item], sems.at[item]).wait()
+
+        return carry
+
+    lax.fori_loop(0, items, issue, 0, unroll=8)
+    lax.fori_loop(0, items, finish, 0, unroll=8)
+
+
+def pick(kind, row, base, *tables):
+    shape = jax.ShapeDtypeStruct(base.shape, base.dtype)
     anywhere = pl.BlockSpec(memory_space=pl.ANY)
     return pl.pallas_call(
         pick_kernel,
         out_shape=(shape, shape),
-        in_specs=[pl.BlockSpec(memory_space=pltpu.SMEM)] * 2 + [anywhere] * len(tables),
+        in_specs=[pl.BlockSpec(memory_space=pltpu.SMEM)] * 2 + [anywhere] * (1 + len(tables)),
         out_specs=(pl.BlockSpec(memory_space=pltpu.VMEM), anywhere),
-        scratch_shapes=[pltpu.SemaphoreType.DMA],
+        scratch_shapes=[
+            pltpu.SemaphoreType.DMA,
+            pltpu.SemaphoreType.DMA((base.shape[0],)),
+        ],
         compiler_params=pltpu.CompilerParams(vmem_limit_bytes=8 * 1024 * 1024),
         cost_estimate=pl.CostEstimate(
             flops=4 * 1000 * 1000 * 1000, bytes_accessed=8 * 1000 * 1000, transcendentals=0
         ),
         name="pick",
-    )(kind, row, *tables)
+    )(kind, row, base, *tables)
 
 
 def route_kernel(row_ref, shared_row_ref, own_ref, out_ref, sem):
@@ -568,9 +603,11 @@
     kind = jnp.where(carries, OWN, kind).astype(jnp.int32)
     source = jnp.where(carries, jnp.repeat(second_pairs[:, 1], 2), slot_of // slot_count)
 
+    base = gather(slot_of // slot_count, first_parts)
+
     def choose(more_pending, more_fresh):
         def run():
-            tables = [root_parts, first_parts]
+            tables = [base, root_parts]
             if more_pending:
                 columns = jnp.where(
                     parity == 0, other_columns, pending_roots[1][:, half_columns:]
@@ -597,7 +634,7 @@
 
     my_found = jnp.any(pending_stat == my_index)
     partner_found = jnp.any(pending_stat == my_index + 1 - 2 * parity)
-    other_returned = swapped(returned, "dev", 0)
+    other_returned = swapped(jnp.where(my_found, held_roots[0], returned), "dev", 0)
     merged = lax.optimization_barrier(jnp.where(my_found, returned, held_roots[0]))
     late = jnp.where(
         my_found,

time: 197 us -> 200 us (1.015)
  blocking collectives: 35.8 us -> 0 us
  waiting for transfers between devices: 71.8 us -> 98.3 us
  Pallas kernels: 26 us -> 31.4 us
  starting transfers between devices: 26.5 us -> 30.2 us
  other arithmetic: 13.7 us -> 17.1 us
    all_to_all x1 -> x0, blocking collectives: 35.8 us -> none  [spread(): return lax.all_to_all(parts, 'dev', split_axis=0, concat_axis=0, tiled=True)]
    all_to_all x3 -> x4, waiting for transfers between devices: 64 us -> 92.3 us  [spread(): return lax.all_to_all(parts, 'dev', split_axis=0, concat_axis=0, tiled=True)]
    pallas_call x0 -> x1, Pallas kernels: none -> 5.17 us  [gather(): pl.pallas_call(gather_kernel, out_shape=jax.ShapeDtypeStruct(table.shape,...]
    select_n x0 -> x1, other arithmetic: none -> 4.85 us  [per_device(): jnp.where(my_found, held_roots[0], returned)]
    all_to_all x3 -> x4, starting transfers between devices: 21.3 us -> 25.3 us  [spread(): return lax.all_to_all(parts, 'dev', split_axis=0, concat_axis=0, tiled=True)]
  transfers between devices with their start and end apart: 9 -> 10, of which waited for: 8 -> 7; matrix products, arithmetic and copies ran while one was open for 13% -> 12% of each run, Pallas kernels for 8% -> 10%
where the time goes in v6:
time: 200 us; the launch traced here: 199 us
  waiting for transfers between devices  98.3 us (49%)
  Pallas kernels  31.4 us (16%)
  starting transfers between devices  30.2 us (15%)
  other arithmetic  17.1 us (9%)
  local copies, waits for them, and re-layouts  9.04 us (5%)
  matrix products  7.32 us (4%)
  between operations  5.61 us (3%)
    all_to_all x4, waiting for transfers between devices, spread(): return lax.all_to_all(parts, 'dev', split_axis=0, concat_axis=0, tiled=True)  92.3 us
    all_to_all x4, starting transfers between devices, spread(): return lax.all_to_all(parts, 'dev', split_axis=0, concat_axis=0, tiled=True)  25.3 us
    pallas_call x1, Pallas kernels, updated_and_root(): pl.pallas_call(root_kernel, out_shape=(jax.ShapeDtypeStruct((width, width...  9.06 us
    dot_general x1, matrix products, per_device(): jnp.dot(left_times, right_root, preferred_element_type=jnp.float32)  7.32 us
    ppermute x6, waiting for transfers between devices, swapped(): lax.ppermute(shard, axis, [(i, i ^ 1 << bit) for i in range(lax.axis_size...  5.98 us
    pallas_call x1, Pallas kernels, route(): pl.pallas_call(route_kernel, out_shape=jax.ShapeDtypeStruct(own.shape, ow...  5.84 us
    select_n x1, other arithmetic, per_device(): jnp.where(my_found, jnp.where(partner_found, spare.reshape(block_width, b...  5.71 us
    pallas_call x1, Pallas kernels, pick(): pl.pallas_call(pick_kernel, out_shape=(shape, shape), in_specs=[pl.BlockS...  5.41 us
  transfers between devices with their start and end apart: 10, of which 7 were waited for; matrix products, arithmetic and copies ran while one was open for 12% of the time, Pallas kernels for 10%

profile of v6, /device:TPU:1, one launch (start us, length us, event | category | flops | bytes accessed | tf_op | source)
XLA Modules:
  0.0 199.2 jit_solution(4769654895195436686)
XLA Ops:
  1.3 3.0 %first_used.1 = bf16[1024,1024]{1,0:T(8,128)(2,1)} custom-call(s32[1]{0:T(128)} %bitcast.6.index_ref, s32[256]{0:T(256)S(1)} %copy-done.2, bf16[2,1024,1024]{2,1,0:T(8,128)(2,1)} %pending_ref.3), custom_call_target="tpu_custom_call" | custom-call | tf_op jit(solution)/shard_map/first_used/pallas_call | solution.py:259
  4.3 11.5 %all-to-all-start.4 = ((bf16[128,8,1024]{2,1,0:T(8,128)(2,1)}), bf16[128,8,1024]{2,1,0:T(8,128)(2,1)S(1)}, u32[]{:S(2)}, u32[]{:S(2)}) async-start(bf16[128,8,1024]{2,1,0:T(8,128)(2,1)} %bitcast.10), calls=%async_computation.4 | async-start | bytes 4194304 | tf_op jit(solution)/shard_map/all_to_all | solution.py:20
  15.8 1.4 dynamic-slice_bitcast_fusion
  18.5 2.2 %collective-permute-done.1.other_ref = bf16[1024,512]{1,0:T(8,128)(2,1)S(1)} collective-permute-done((bf16[1024,512]{1,0:T(8,128)(2,1)S(1)}, bf16[1024,512]{1,0:T(8,128)(2,1)S(1)}, u32[]{:S(2)}, u32[]{:S(2)}) %collective-permute-start.1) | collective-permute-done | bytes 1048608 | tf_op jit(solution)/shard_map/ppermute | solution.py:16
  20.7 1.5 collective-permute-done.other_grad_ref
  22.2 9.1 %root.1 = (f32[1024,1024]{1,0:T(8,128)}, bf16[1024,1536]{1,0:T(8,128)(2,1)}, bf16[1024,1024]{1,0:T(8,128)(2,1)S(1)}) custom-call(s32[1]{0:T(128)} %bitcast.6.index_ref, s32[256]{0:T(256)S(1)} %copy-done.3, s32[256]{0:T(256)S(1)} %copy-done.4, bf16[512,1024]{1,0:T(8,128)(2,1)S(1)} %copy-done.5, bf16[512,1024]{1,0:T(8,128)(2,1)S(1)} %collective-permute-done.other_grad_ref, ...), custom_call_target="tpu_custom_call" | custom-call | flops 8589934592 | bytes 17825792 | tf_op jit(solution)/shard_map/root/pallas_call | solution.py:495
  32.6 13.3 %all-to-all-done.4.table_ref = bf16[128,8,1024]{2,1,0:T(8,128)(2,1)S(1)} async-done(((bf16[128,8,1024]{2,1,0:T(8,128)(2,1)}), bf16[128,8,1024]{2,1,0:T(8,128)(2,1)S(1)}, u32[]{:S(2)}, u32[]{:S(2)}) %all-to-all-start.4) | async-done | bytes 2097184 | tf_op jit(solution)/shard_map/all_to_all | solution.py:20
  45.9 5.8 %all-to-all-start.5 = ((bf16[128,8,1536]{2,1,0:T(8,128)(2,1)}), bf16[128,8,1536]{2,1,0:T(8,128)(2,1)}, u32[]{:S(2)}, u32[]{:S(2)}) async-start(bf16[128,8,1536]{2,1,0:T(8,128)(2,1)} %bitcast.11), calls=%async_computation.5 | async-start | bytes 6291456 | tf_op jit(solution)/shard_map/all_to_all | solution.py:20
  58.5 5.2 %gather.1 = bf16[128,8,1024]{2,1,0:T(8,128)(2,1)} custom-call(s32[128]{0:T(128)S(1)} %get-tuple-element.157.row_ref, bf16[128,8,1024]{2,1,0:T(8,128)(2,1)S(1)} %all-to-all-done.4.table_ref), custom_call_target="tpu_custom_call" | custom-call | flops 4000000000 | bytes 8000000 | tf_op jit(solution)/shard_map/gather/pallas_call | solution.py:37
  63.7 29.5 %all-to-all-done.5.own_ref = bf16[128,8,1536]{2,1,0:T(8,128)(2,1)} async-done(((bf16[128,8,1536]{2,1,0:T(8,128)(2,1)}), bf16[128,8,1536]{2,1,0:T(8,128)(2,1)}, u32[]{:S(2)}, u32[]{:S(2)}) %all-to-all-start.5) | async-done | bytes 3145760 | tf_op jit(solution)/shard_map/all_to_all | solution.py:20
  93.2 5.6 %conditional.1 = ((bf16[128,8,1024]{2,1,0:T(8,128)(2,1)}, bf16[128,8,1024]{2,1,0:T(8,128)(2,1)})) conditional(s32[]{:T(128)} %clamp.3, (s32[128]{0:T(128)S(1)}, s32[128]{0:T(128)S(1)}, bf16[128,8,1024]{2,1,0:T(8,128)(2,1)}, bf16[128,8,1536]{2,1,0:T(8,128)(2,1)}) %tuple.23, (s32[]{:T(128)}, ...), branch_computations={%region_9.10_spmd, %region_10.11_spmd, %region_11.12_spmd, %region... | conditional | flops 8000524288 | bytes 41169536 | solution.py:626
  93.2 5.4 %pick.6 = (bf16[128,8,1024]{2,1,0:T(8,128)(2,1)}, bf16[128,8,1024]{2,1,0:T(8,128)(2,1)}) custom-call(s32[128]{0:T(128)S(1)} %get-tuple-element.48.kind_ref, s32[128]{0:T(128)S(1)} %get-tuple-element.49.row_ref, bf16[128,8,1024]{2,1,0:T(8,128)(2,1)} %get-tuple-element.50.base_ref, bf16[128,8,1536]{2,1,0:T(8,128)(2,1)} %get-tuple-element.51.own_ref), custom_call_target="tpu_custom_call" | custom-call | flops 4000000000 | bytes 8000000 | tf_op jit(solution)/shard_map/cond/branch_0_fun/pick/pallas_call | solution.py:108
  98.8 4.5 %all-to-all-start.6 = ((bf16[128,8,1024]{2,1,0:T(8,128)(2,1)}), bf16[128,8,1024]{2,1,0:T(8,128)(2,1)S(1)}, u32[]{:S(2)}, u32[]{:S(2)}) async-start(bf16[128,8,1024]{2,1,0:T(8,128)(2,1)} %get-tuple-element.91), calls=%async_computation.6 | async-start | bytes 4194304 | tf_op jit(solution)/shard_map/all_to_all | solution.py:20
  104.0 29.6 %all-to-all-done.6 = bf16[128,8,1024]{2,1,0:T(8,128)(2,1)S(1)} async-done(((bf16[128,8,1024]{2,1,0:T(8,128)(2,1)}), bf16[128,8,1024]{2,1,0:T(8,128)(2,1)S(1)}, u32[]{:S(2)}, u32[]{:S(2)}) %all-to-all-start.6) | async-done | bytes 2097184 | tf_op jit(solution)/shard_map/all_to_all | solution.py:20
  133.5 4.9 %bitcast_select_fusion.1 = (bf16[1024,1024]{1,0:T(8,128)(2,1)}, bf16[1024,1024]{1,0:T(8,128)(2,1)}) fusion(bf16[1,1024,1024]{2,1,0:T(8,128)(2,1)} %param.12, bf16[128,8,1024]{2,1,0:T(8,128)(2,1)S(1)} %all-to-all-done.6, pred[]{:T(512)} %get-tuple-element.151), kind=kLoop, calls=%fused_computation.10 | loop fusion | flops 2097152 | bytes 8388609 | tf_op jit(solution)/shard_map/jit(_where)/select_n | solution.py:637
  139.7 5.8 %route.1 = bf16[128,8,1536]{2,1,0:T(8,128)(2,1)S(1)} custom-call(s32[128]{0:T(128)S(1)} %fusion.26.row_ref, s32[64]{0:T(128)S(1)} %select_n.163.shared_row_ref, bf16[128,8,1536]{2,1,0:T(8,128)(2,1)} %all-to-all-done.5.own_ref), custom_call_target="tpu_custom_call" | custom-call | flops 4000000000 | bytes 12000000 | tf_op jit(solution)/shard_map/route/pallas_call | solution.py:149
  145.6 1.7 copy-done.1
  147.2 3.6 %all-to-all-start.7 = ((bf16[128,8,1536]{2,1,0:T(8,128)(2,1)}), bf16[128,8,1536]{2,1,0:T(8,128)(2,1)S(1)}, u32[]{:S(2)}, u32[]{:S(2)}) async-start(bf16[128,8,1536]{2,1,0:T(8,128)(2,1)} %copy-done.1), calls=%async_computation.7 | async-start | bytes 6291456 | tf_op jit(solution)/shard_map/all_to_all | solution.py:20
  155.3 7.3 %multiply_reduce_fusion = (f32[]{:T(128)}, f32[512,1024]{1,0:T(8,128)}) fusion(bf16[1024,1024]{1,0:T(8,128)(2,1)} %collective-permute-done.2, bf16[1024,1024]{1,0:T(8,128)(2,1)} %get-tuple-element.162, pred[]{:T(512)S(6)} %eq.86, bf16[1024,1024]{1,0:T(8,128)(2,1)} %copy-done.6, s32[]{:T(128)S(6)} %select_n.166), kind=kOutput, calls=%fused_computation.13 | convolution fusion | flops 2150629376 | bytes 10487300 | tf_op jit(solution)/shard_map/dot_general | solution.py:652
  162.7 5.7 %fusion.2.late_ref = bf16[1024,1024]{1,0:T(8,128)(2,1)} fusion(bf16[1024,1024]{1,0:T(8,128)(2,1)} %collective-permute-done.4, bf16[128,8,1024]{2,1,0:T(8,128)(2,1)} %get-tuple-element.93, bf16[128,8,1024]{2,1,0:T(8,128)(2,1)} %copy-done.7, pred[]{:T(512)} %get-tuple-element.150, pred[]{:T(512)} %get-tuple-element.151), kind=kLoop, calls=%fused_computation.9 | loop fusion | flops 2097152 | bytes 8388610 | tf_op jit(solution)/shard_map/jit(_where)/select_n | solution.py:639
  169.7 2.8 %multiply_convert_fusion = bf16[512,1024]{1,0:T(8,128)(2,1)} fusion(f32[512,1024]{1,0:T(8,128)} %get-tuple-element.166, f32[]{:T(128)S(6)} %rsqrt.3), kind=kLoop, calls=%fused_computation.12 | loop fusion | flops 1048576 | bytes 3145732 | tf_op jit(solution)/shard_map/convert_element_type | solution.py:656
  172.5 20.0 %all-to-all-done.7 = bf16[128,8,1536]{2,1,0:T(8,128)(2,1)S(1)} async-done(((bf16[128,8,1536]{2,1,0:T(8,128)(2,1)}), bf16[128,8,1536]{2,1,0:T(8,128)(2,1)S(1)}, u32[]{:S(2)}, u32[]{:S(2)}) %all-to-all-start.7) | async-done | bytes 3145760 | tf_op jit(solution)/shard_map/all_to_all | solution.py:20
  193.7 2.3 %collective-permute-done.5.other_ref = bf16[1024,512]{1,0:T(8,128)(2,1)S(1)} collective-permute-done((bf16[1024,512]{1,0:T(8,128)(2,1)S(1)}, bf16[1024,512]{1,0:T(8,128)(2,1)S(1)}, u32[]{:S(2)}, u32[]{:S(2)}) %collective-permute-start.5) | collective-permute-done | bytes 1048608 | tf_op jit(solution)/shard_map/ppermute | solution.py:16
  196.0 3.0 %place.1 = bf16[2,1024,1024]{2,1,0:T(8,128)(2,1)} custom-call(s32[3]{0:T(128)S(1)} %pad_add_fusion.code_ref, bf16[1024,1536]{1,0:T(8,128)(2,1)S(1)} %bitcast.39, bf16[1024,512]{1,0:T(8,128)(2,1)S(1)} %collective-permute-done.5.other_ref, bf16[1024,1024]{1,0:T(8,128)(2,1)S(1)} %copy-done, bf16[256,1024]{1,0:T(8,128)(2,1)S(1)} %broadcast_in_dim.68.zero_ref), custom_call_target="tpu_custom_call" | custom-call | tf_op jit(solution)/shard_map/place/pallas_call | solution.py:217
  (72 shorter events, 14.6 us)
Async XLA Ops:
  0.6 0.7 copy-start.2
  4.3 41.6 %all-to-all-start.4 = ((bf16[128,8,1024]{2,1,0:T(8,128)(2,1)}), bf16[128,8,1024]{2,1,0:T(8,128)(2,1)S(1)}, u32[]{:S(2)}, u32[]{:S(2)}) async-start(bf16[128,8,1024]{2,1,0:T(8,128)(2,1)} %bitcast.10), calls=%async_computation.4 | async-start | bytes 4194304 | tf_op jit(solution)/shard_map/all_to_all | solution.py:20
  15.8 2.6 %copy-start.5 = (bf16[512,1024]{1,0:T(8,128)(2,1)S(1)}, bf16[512,1024]{1,0:T(8,128)(2,1)}, u32[]{:S(2)}) copy-start(bf16[512,1024]{1,0:T(8,128)(2,1)} %own_grad_ref.1) | copy-start | bytes 3145732
  15.8 6.4 %copy-start.3 = (s32[256]{0:T(256)S(1)}, s32[256]{0:T(256)}, u32[]{:S(2)}) copy-start(s32[256]{0:T(256)} %stat_ref.1) | copy-start | bytes 3076
  15.8 6.3 %copy-start.4 = (s32[256]{0:T(256)S(1)}, s32[256]{0:T(256)}, u32[]{:S(2)}) copy-start(s32[256]{0:T(256)} %refresh_stat_ref.1) | copy-start | bytes 3076
  17.2 3.4 %collective-permute-start.1 = (bf16[1024,512]{1,0:T(8,128)(2,1)S(1)}, bf16[1024,512]{1,0:T(8,128)(2,1)S(1)}, u32[]{:S(2)}, u32[]{:S(2)}) collective-permute-start(bf16[1024,512]{1,0:T(8,128)(2,1)S(1)} %dynamic-slice_bitcast_fusion), channel_id=1, source_target_pairs={{0,1},{1,0},{2,3},{3,2},{4,5},{5,4},{6,7},{7,6},{8,9},{9,8},{10,11... | collective-permute-start | bytes 3145736 | tf_op jit(solution)/shard_map/ppermute | solution.py:16
  18.4 3.8 %collective-permute-start = (bf16[512,1024]{1,0:T(8,128)(2,1)S(1)}, bf16[512,1024]{1,0:T(8,128)(2,1)S(1)}, u32[]{:S(2)}, u32[]{:S(2)}) collective-permute-start(bf16[512,1024]{1,0:T(8,128)(2,1)S(1)} %copy-done.5), channel_id=1, source_target_pairs={{0,1},{1,0},{2,3},{3,2},{4,5},{5,4},{6,7},{7,6},{8,9},{9,8},{10,11... | collective-permute-start | bytes 3145736 | tf_op jit(solution)/shard_map/ppermute | solution.py:16
  20.7 1.5 copy-start.8
  31.2 1.4 copy-start.6
  45.9 47.3 %all-to-all-start.5 = ((bf16[128,8,1536]{2,1,0:T(8,128)(2,1)}), bf16[128,8,1536]{2,1,0:T(8,128)(2,1)}, u32[]{:S(2)}, u32[]{:S(2)}) async-start(bf16[128,8,1536]{2,1,0:T(8,128)(2,1)} %bitcast.11), calls=%async_computation.5 | async-start | bytes 6291456 | tf_op jit(solution)/shard_map/all_to_all | solution.py:20
  58.5 34.7 %copy-start.9 = (bf16[1024,512]{1,0:T(8,128)(2,1)S(1)}, bf16[1024,512]{1,0:T(8,128)(2,1)}, u32[]{:S(2)}) copy-start(bf16[1024,512]{1,0:T(8,128)(2,1)} %copy-done.8) | copy-start | bytes 3145732
  98.8 34.7 %all-to-all-start.6 = ((bf16[128,8,1024]{2,1,0:T(8,128)(2,1)}), bf16[128,8,1024]{2,1,0:T(8,128)(2,1)S(1)}, u32[]{:S(2)}, u32[]{:S(2)}) async-start(bf16[128,8,1024]{2,1,0:T(8,128)(2,1)} %get-tuple-element.91), calls=%async_computation.6 | async-start | bytes 4194304 | tf_op jit(solution)/shard_map/all_to_all | solution.py:20
  133.5 4.9 %copy-start.7 = (bf16[128,8,1024]{2,1,0:T(8,128)(2,1)}, bf16[128,8,1024]{2,1,0:T(8,128)(2,1)S(1)}, u32[]{:S(2)}) copy-start(bf16[128,8,1024]{2,1,0:T(8,128)(2,1)S(1)} %all-to-all-done.6) | copy-start | bytes 6291460
  138.4 17.0 %collective-permute-start.2 = (bf16[1024,1024]{1,0:T(8,128)(2,1)}, bf16[1024,1024]{1,0:T(8,128)(2,1)}, u32[]{:S(2)}, u32[]{:S(2)}) collective-permute-start(bf16[1024,1024]{1,0:T(8,128)(2,1)} %get-tuple-element.162), channel_id=1, source_target_pairs={{0,1},{1,0},{2,3},{3,2},{4,5},{5,4},{6,7},{7,6},{8,9},{9,8},{10,11... | collective-permute-start | bytes 6291464 | tf_op jit(solution)/shard_map/ppermute | solution.py:16
  145.6 1.7 copy-start.1
  147.2 45.3 %all-to-all-start.7 = ((bf16[128,8,1536]{2,1,0:T(8,128)(2,1)}), bf16[128,8,1536]{2,1,0:T(8,128)(2,1)S(1)}, u32[]{:S(2)}, u32[]{:S(2)}) async-start(bf16[128,8,1536]{2,1,0:T(8,128)(2,1)} %copy-done.1), calls=%async_computation.7 | async-start | bytes 6291456 | tf_op jit(solution)/shard_map/all_to_all | solution.py:20
  150.8 11.9 %collective-permute-start.4 = (bf16[1024,1024]{1,0:T(8,128)(2,1)}, bf16[1024,1024]{1,0:T(8,128)(2,1)}, u32[]{:S(2)}, u32[]{:S(2)}) collective-permute-start(bf16[1024,1024]{1,0:T(8,128)(2,1)} %get-tuple-element.161), channel_id=1, source_target_pairs={{0,1},{1,0},{2,3},{3,2},{4,5},{5,4},{6,7},{7,6},{8,9},{9,8},{10,11... | collective-permute-start | bytes 6291464 | tf_op jit(solution)/shard_map/ppermute | solution.py:16
  162.7 5.8 %collective-permute-start.3 = (f32[]{:T(128)}, f32[]{:T(128)}, u32[]{:S(2)}, u32[]{:S(2)}) collective-permute-start(f32[]{:T(128)} %get-tuple-element.165), channel_id=1, source_target_pairs={{0,1},{1,0},{2,3},{3,2},{4,5},{5,4},{6,7},{7,6},{8,9},{9,8},{10,11... | collective-permute-start | bytes 20 | tf_op jit(solution)/shard_map/ppermute | solution.py:16
  192.5 3.5 %copy-start = (bf16[1024,1024]{1,0:T(8,128)(2,1)S(1)}, bf16[1024,1024]{1,0:T(8,128)(2,1)}, u32[]{:S(2)}) copy-start(bf16[1024,1024]{1,0:T(8,128)(2,1)} %fusion.2.late_ref) | copy-start | bytes 6291460
  192.6 3.4 %collective-permute-start.5 = (bf16[1024,512]{1,0:T(8,128)(2,1)S(1)}, bf16[1024,512]{1,0:T(8,128)(2,1)S(1)}, u32[]{:S(2)}, u32[]{:S(2)}) collective-permute-start(bf16[1024,512]{1,0:T(8,128)(2,1)S(1)} %slice.86), channel_id=1, source_target_pairs={{0,1},{1,0},{2,3},{3,2},{4,5},{5,4},{6,7},{7,6},{8,9},{9,8},{10,11... | collective-permute-start | bytes 3145736 | tf_op jit(solution)/shard_map/ppermute | solution.py:16

commit v7 on v5

--- a/solution.py
+++ b/solution.py
@@ -20,20 +20,21 @@
     return lax.all_to_all(parts, "dev", split_axis=0, concat_axis=0, tiled=True)
 
 
+CHUNKS = 4
 FIRST, OWN, SHARED, EXTRA = range(4)
 EMPTY, PLAIN, HALVES, LATE = range(4)
 
 
 def pick_kernel(kind_ref, row_ref, own_ref, *refs):
-    tables, out_ref, sem = refs[:-3], refs[-3], refs[-1]
+    tables, result_ref, out_ref, sems = refs[:-4], refs[-4], refs[-2], refs[-1]
     width = out_ref.shape[2]
-    half = width // 2
-
-    def start(src, dst):
-        pltpu.make_async_copy(src, dst, sem).start()
+    half, span = width // 2, out_ref.shape[0] // CHUNKS
 
     def issue(item, carry):
         row, kind = row_ref[item], kind_ref[item]
+
+        def start(src, dst):
+            pltpu.make_async_copy(src, dst, sems.at[0, item // span]).start()
 
         @pl.when(kind == FIRST)
         def _():
@@ -65,8 +66,24 @@
 
         return carry
 
-    lax.fori_loop(0, out_ref.shape[0], issue, 0, unroll=8)
-    pltpu.make_async_copy(out_ref, out_ref, sem).wait()
+    parts = [pl.ds(chunk * span, span) for chunk in range(CHUNKS)]
+    stores = [
+        pltpu.make_async_copy(out_ref.at[part], result_ref.at[part], sems.at[1, chunk])
+        for chunk, part in enumerate(parts)
+    ]
+
+    def pass_on(chunk):
+        part = out_ref.at[parts[chunk]]
+        pltpu.make_async_copy(part, part, sems.at[0, chunk]).wait()
+        stores[chunk].start()
+
+    for chunk in range(CHUNKS):
+        lax.fori_loop(chunk * span, (chunk + 1) * span, issue, 0, unroll=8)
+        if chunk:
+            pass_on(chunk - 1)
+    pass_on(CHUNKS - 1)
+    for store in stores:
+        store.wait()
 
 
 def pick(kind, row, *tables):
@@ -77,8 +94,11 @@
         pick_kernel,
         out_shape=(shape, shape),
         in_specs=[pl.BlockSpec(memory_space=pltpu.SMEM)] * 2 + [anywhere] * len(tables),
-        out_specs=(pl.BlockSpec(memory_space=pltpu.VMEM), anywhere),
-        scratch_shapes=[pltpu.SemaphoreType.DMA],
+        out_specs=(anywhere, anywhere),
+        scratch_shapes=[
+            pltpu.VMEM(shape.shape, shape.dtype),
+            pltpu.SemaphoreType.DMA((2, CHUNKS)),
+        ],
         compiler_params=pltpu.CompilerParams(vmem_limit_bytes=8 * 1024 * 1024),
         cost_estimate=pl.CostEstimate(
             flops=4 * 1000 * 1000 * 1000, bytes_accessed=8 * 1000 * 1000, transcendentals=0
@@ -192,9 +212,6 @@
         compiler_params=pltpu.CompilerParams(vmem_limit_bytes=8 * 1024 * 1024),
         name="place",
     )(codes, got, other, late, jnp.zeros((rows // CHUNKS, width), late.dtype))
-
-
-CHUNKS = 4
 
 
 def first_kernel(index_ref, stat_ref, pending_ref, first_ref, held, sems):

time: 197 us -> 197 us (level)
  no operation moved by 1% of the time
where the time goes in v7:
time: 197 us; the launch traced here: 196 us
  waiting for transfers between devices  71.8 us (36%)
  blocking collectives  35.7 us (18%)
  starting transfers between devices  26.5 us (13%)
  Pallas kernels  25.8 us (13%)
  other arithmetic  13.7 us (7%)
  local copies, waits for them, and re-layouts  9.03 us (5%)
  matrix products  7.22 us (4%)
  between operations  5.67 us (3%)
    all_to_all x3, waiting for transfers between devices, spread(): return lax.all_to_all(parts, 'dev', split_axis=0, concat_axis=0, tiled=True)  64 us
    all_to_all x1, blocking collectives, spread(): return lax.all_to_all(parts, 'dev', split_axis=0, concat_axis=0, tiled=True)  35.7 us
    all_to_all x3, starting transfers between devices, spread(): return lax.all_to_all(parts, 'dev', split_axis=0, concat_axis=0, tiled=True)  21.3 us
    pallas_call x1, Pallas kernels, updated_and_root(): pl.pallas_call(root_kernel, out_shape=(jax.ShapeDtypeStruct((width, width...  9.06 us
    ppermute x6, waiting for transfers between devices, swapped(): lax.ppermute(shard, axis, [(i, i ^ 1 << bit) for i in range(lax.axis_size...  7.78 us
    dot_general x1, matrix products, per_device(): jnp.dot(left_times, right_root, preferred_element_type=jnp.float32)  7.22 us
    select_n x1, other arithmetic, per_device(): jnp.where(my_found, jnp.where(partner_found, spare.reshape(block_width, b...  7.17 us
    pallas_call x1, Pallas kernels, route(): pl.pallas_call(route_kernel, out_shape=jax.ShapeDtypeStruct(own.shape, ow...  5.84 us
  transfers between devices with their start and end apart: 9, of which 8 were waited for; matrix products, arithmetic and copies ran while one was open for 13% of the time, Pallas kernels for 8%

profile of v7, /device:TPU:1, one launch (start us, length us, event | category | flops | bytes accessed | tf_op | source)
XLA Modules:
  0.0 195.6 jit_solution(14507485972841296458)
XLA Ops:
  1.3 3.0 %first_used.1 = bf16[1024,1024]{1,0:T(8,128)(2,1)} custom-call(s32[1]{0:T(128)} %bitcast.6.index_ref, s32[256]{0:T(256)S(1)} %copy-done.2, bf16[2,1024,1024]{2,1,0:T(8,128)(2,1)} %pending_ref.3), custom_call_target="tpu_custom_call" | custom-call | tf_op jit(solution)/shard_map/first_used/pallas_call | solution.py:241
  4.3 12.0 %all-to-all-start.5 = ((bf16[128,8,1024]{2,1,0:T(8,128)(2,1)}), bf16[128,8,1024]{2,1,0:T(8,128)(2,1)}, u32[]{:S(2)}, u32[]{:S(2)}) async-start(bf16[128,8,1024]{2,1,0:T(8,128)(2,1)} %bitcast.11), calls=%async_computation.5 | async-start | bytes 4194304 | tf_op jit(solution)/shard_map/all_to_all | solution.py:20
  16.3 1.4 dynamic-slice_bitcast_fusion
  17.7 1.2 collective-permute-start.1
  19.0 2.2 %collective-permute-done.1.other_ref = bf16[1024,512]{1,0:T(8,128)(2,1)S(1)} collective-permute-done((bf16[1024,512]{1,0:T(8,128)(2,1)S(1)}, bf16[1024,512]{1,0:T(8,128)(2,1)S(1)}, u32[]{:S(2)}, u32[]{:S(2)}) %collective-permute-start.1) | collective-permute-done | bytes 1048608 | tf_op jit(solution)/shard_map/ppermute | solution.py:16
  21.2 1.5 collective-permute-done.other_grad_ref
  22.7 9.1 %root.1 = (f32[1024,1024]{1,0:T(8,128)}, bf16[1024,1536]{1,0:T(8,128)(2,1)}, bf16[1024,1024]{1,0:T(8,128)(2,1)S(1)}) custom-call(s32[1]{0:T(128)} %bitcast.6.index_ref, s32[256]{0:T(256)S(1)} %copy-done.3, s32[256]{0:T(256)S(1)} %copy-done.4, bf16[512,1024]{1,0:T(8,128)(2,1)S(1)} %copy-done.5, bf16[512,1024]{1,0:T(8,128)(2,1)S(1)} %collective-permute-done.other_grad_ref, ...), custom_call_target="tpu_custom_call" | custom-call | flops 8589934592 | bytes 17825792 | tf_op jit(solution)/shard_map/root/pallas_call | solution.py:477
  31.8 1.4 copy-done.6
  33.1 12.9 %all-to-all-done.5 = bf16[128,8,1024]{2,1,0:T(8,128)(2,1)} async-done(((bf16[128,8,1024]{2,1,0:T(8,128)(2,1)}), bf16[128,8,1024]{2,1,0:T(8,128)(2,1)}, u32[]{:S(2)}, u32[]{:S(2)}) %all-to-all-start.5) | async-done | bytes 2097184 | tf_op jit(solution)/shard_map/all_to_all | solution.py:20
  46.0 5.8 %all-to-all-start.4 = ((bf16[128,8,1536]{2,1,0:T(8,128)(2,1)}), bf16[128,8,1536]{2,1,0:T(8,128)(2,1)}, u32[]{:S(2)}, u32[]{:S(2)}) async-start(bf16[128,8,1536]{2,1,0:T(8,128)(2,1)} %bitcast.10), calls=%async_computation.4 | async-start | bytes 6291456 | tf_op jit(solution)/shard_map/all_to_all | solution.py:20
  58.6 34.6 %all-to-all-done.4.own_ref = bf16[128,8,1536]{2,1,0:T(8,128)(2,1)} async-done(((bf16[128,8,1536]{2,1,0:T(8,128)(2,1)}), bf16[128,8,1536]{2,1,0:T(8,128)(2,1)}, u32[]{:S(2)}, u32[]{:S(2)}) %all-to-all-start.4) | async-done | bytes 3145760 | tf_op jit(solution)/shard_map/all_to_all | solution.py:20
  93.3 5.2 %conditional.1 = ((bf16[128,8,1024]{2,1,0:T(8,128)(2,1)}, bf16[128,8,1024]{2,1,0:T(8,128)(2,1)})) conditional(s32[]{:T(128)} %clamp.3, (s32[128]{0:T(128)S(1)}, s32[128]{0:T(128)S(1)}, bf16[128,8,1536]{2,1,0:T(8,128)(2,1)}, bf16[128,8,1024]{2,1,0:T(8,128)(2,1)}) %tuple.23, (s32[]{:T(128)}, ...), branch_computations={%region_9.10_spmd, %region_10.11_spmd, %region_11.12_spmd, %region... | conditional | flops 8000524288 | bytes 32780902 | solution.py:606
  93.3 5.0 %pick.6 = (bf16[128,8,1024]{2,1,0:T(8,128)(2,1)}, bf16[128,8,1024]{2,1,0:T(8,128)(2,1)}) custom-call(s32[128]{0:T(128)S(1)} %get-tuple-element.48.kind_ref, s32[128]{0:T(128)S(1)} %get-tuple-element.49.row_ref, bf16[128,8,1536]{2,1,0:T(8,128)(2,1)} %get-tuple-element.50.own_ref, bf16[128,8,1024]{2,1,0:T(8,128)(2,1)} %get-tuple-element.51.refs_0_), custom_call_target="tpu_custom_call" | custom-call | flops 4000000000 | bytes 8000000 | tf_op jit(solution)/shard_map/cond/branch_0_fun/pick/pallas_call | solution.py:93
  98.5 35.7 %all_to_all.37 = bf16[128,8,1024]{2,1,0:T(8,128)(2,1)} all-to-all(bf16[128,8,1024]{2,1,0:T(8,128)(2,1)} %get-tuple-element.91), channel_id=1, replica_groups=mesh['dev'=128] {'dev'}, dimensions={0} | all-to-all | bytes 4194304 | tf_op jit(solution)/shard_map/all_to_all | solution.py:20
  134.2 1.3 collective-permute-start.4
  136.2 5.8 %route.1 = bf16[128,8,1536]{2,1,0:T(8,128)(2,1)S(1)} custom-call(s32[128]{0:T(128)S(1)} %fusion.26.row_ref, s32[64]{0:T(128)S(1)} %select_n.158.shared_row_ref, bf16[128,8,1536]{2,1,0:T(8,128)(2,1)} %all-to-all-done.4.own_ref), custom_call_target="tpu_custom_call" | custom-call | flops 4000000000 | bytes 12000000 | tf_op jit(solution)/shard_map/route/pallas_call | solution.py:134
  142.0 1.7 copy-done.1
  143.7 3.6 %all-to-all-start.7 = ((bf16[128,8,1536]{2,1,0:T(8,128)(2,1)}), bf16[128,8,1536]{2,1,0:T(8,128)(2,1)S(1)}, u32[]{:S(2)}, u32[]{:S(2)}) async-start(bf16[128,8,1536]{2,1,0:T(8,128)(2,1)} %copy-done.1), calls=%async_computation.7 | async-start | bytes 6291456 | tf_op jit(solution)/shard_map/all_to_all | solution.py:20
  147.3 7.2 %fusion.2 = (bf16[1024,1024]{1,0:T(8,128)(2,1)}, bf16[1024,1024]{1,0:T(8,128)(2,1)}) fusion(bf16[1024,1024]{1,0:T(8,128)(2,1)} %collective-permute-done.4, bf16[128,8,1024]{2,1,0:T(8,128)(2,1)} %get-tuple-element.93, pred[]{:T(512)} %get-tuple-element.150, pred[]{:T(512)} %get-tuple-element.151, bf16[128,8,1024]{2,1,0:T(8,128)(2,1)} %all_to_all.37, ...), kind=kLoop, calls=%fused_computation.9 | loop fusion | flops 3145728 | bytes 12582914 | tf_op jit(solution)/shard_map/jit(_where)/select_n | solution.py:619
  159.7 7.2 %multiply_reduce_fusion = (f32[]{:T(128)}, f32[512,1024]{1,0:T(8,128)}) fusion(bf16[1024,1024]{1,0:T(8,128)(2,1)} %collective-permute-done.2, bf16[1024,1024]{1,0:T(8,128)(2,1)} %get-tuple-element.161, pred[]{:T(512)S(6)} %eq.86, bf16[1024,1024]{1,0:T(8,128)(2,1)} %copy-done.6, s32[]{:T(128)S(6)} %select_n.161), kind=kOutput, calls=%fused_computation.12 | convolution fusion | flops 2150629376 | bytes 10487300 | tf_op jit(solution)/shard_map/dot_general | solution.py:632
  169.7 2.8 %multiply_convert_fusion = bf16[512,1024]{1,0:T(8,128)(2,1)} fusion(f32[512,1024]{1,0:T(8,128)} %get-tuple-element.165, f32[]{:T(128)S(6)} %rsqrt.3), kind=kLoop, calls=%fused_computation.11 | loop fusion | flops 1048576 | bytes 3145732 | tf_op jit(solution)/shard_map/convert_element_type | solution.py:636
  172.5 16.5 %all-to-all-done.7 = bf16[128,8,1536]{2,1,0:T(8,128)(2,1)S(1)} async-done(((bf16[128,8,1536]{2,1,0:T(8,128)(2,1)}), bf16[128,8,1536]{2,1,0:T(8,128)(2,1)S(1)}, u32[]{:S(2)}, u32[]{:S(2)}) %all-to-all-start.7) | async-done | bytes 3145760 | tf_op jit(solution)/shard_map/all_to_all | solution.py:20
  190.1 2.3 %collective-permute-done.5.other_ref = bf16[1024,512]{1,0:T(8,128)(2,1)S(1)} collective-permute-done((bf16[1024,512]{1,0:T(8,128)(2,1)S(1)}, bf16[1024,512]{1,0:T(8,128)(2,1)S(1)}, u32[]{:S(2)}, u32[]{:S(2)}) %collective-permute-start.5) | collective-permute-done | bytes 1048608 | tf_op jit(solution)/shard_map/ppermute | solution.py:16
  192.5 3.0 %place.1 = bf16[2,1024,1024]{2,1,0:T(8,128)(2,1)} custom-call(s32[3]{0:T(128)S(1)} %pad_add_fusion.code_ref, bf16[1024,1536]{1,0:T(8,128)(2,1)S(1)} %bitcast.37, bf16[1024,512]{1,0:T(8,128)(2,1)S(1)} %collective-permute-done.5.other_ref, bf16[1024,1024]{1,0:T(8,128)(2,1)S(1)} %copy-done, bf16[256,1024]{1,0:T(8,128)(2,1)S(1)} %broadcast_in_dim.68.zero_ref), custom_call_target="tpu_custom_call" | custom-call | tf_op jit(solution)/shard_map/place/pallas_call | solution.py:202
  (63 shorter events, 12.8 us)
Async XLA Ops:
  0.6 0.7 copy-start.2
  4.3 41.7 %all-to-all-start.5 = ((bf16[128,8,1024]{2,1,0:T(8,128)(2,1)}), bf16[128,8,1024]{2,1,0:T(8,128)(2,1)}, u32[]{:S(2)}, u32[]{:S(2)}) async-start(bf16[128,8,1024]{2,1,0:T(8,128)(2,1)} %bitcast.11), calls=%async_computation.5 | async-start | bytes 4194304 | tf_op jit(solution)/shard_map/all_to_all | solution.py:20
  16.3 2.7 %copy-start.5 = (bf16[512,1024]{1,0:T(8,128)(2,1)S(1)}, bf16[512,1024]{1,0:T(8,128)(2,1)}, u32[]{:S(2)}) copy-start(bf16[512,1024]{1,0:T(8,128)(2,1)} %own_grad_ref.1) | copy-start | bytes 3145732
  16.3 6.4 %copy-start.3 = (s32[256]{0:T(256)S(1)}, s32[256]{0:T(256)}, u32[]{:S(2)}) copy-start(s32[256]{0:T(256)} %stat_ref.1) | copy-start | bytes 3076
  16.3 6.4 %copy-start.4 = (s32[256]{0:T(256)S(1)}, s32[256]{0:T(256)}, u32[]{:S(2)}) copy-start(s32[256]{0:T(256)} %refresh_stat_ref.1) | copy-start | bytes 3076
  17.7 3.5 %collective-permute-start.1 = (bf16[1024,512]{1,0:T(8,128)(2,1)S(1)}, bf16[1024,512]{1,0:T(8,128)(2,1)S(1)}, u32[]{:S(2)}, u32[]{:S(2)}) collective-permute-start(bf16[1024,512]{1,0:T(8,128)(2,1)S(1)} %dynamic-slice_bitcast_fusion), channel_id=1, source_target_pairs={{0,1},{1,0},{2,3},{3,2},{4,5},{5,4},{6,7},{7,6},{8,9},{9,8},{10,11... | collective-permute-start | bytes 3145736 | tf_op jit(solution)/shard_map/ppermute | solution.py:16
  18.9 3.8 %collective-permute-start = (bf16[512,1024]{1,0:T(8,128)(2,1)S(1)}, bf16[512,1024]{1,0:T(8,128)(2,1)S(1)}, u32[]{:S(2)}, u32[]{:S(2)}) collective-permute-start(bf16[512,1024]{1,0:T(8,128)(2,1)S(1)} %copy-done.5), channel_id=1, source_target_pairs={{0,1},{1,0},{2,3},{3,2},{4,5},{5,4},{6,7},{7,6},{8,9},{9,8},{10,11... | collective-permute-start | bytes 3145736 | tf_op jit(solution)/shard_map/ppermute | solution.py:16
  31.8 1.4 copy-start.6
  46.0 47.3 %all-to-all-start.4 = ((bf16[128,8,1536]{2,1,0:T(8,128)(2,1)}), bf16[128,8,1536]{2,1,0:T(8,128)(2,1)}, u32[]{:S(2)}, u32[]{:S(2)}) async-start(bf16[128,8,1536]{2,1,0:T(8,128)(2,1)} %bitcast.10), calls=%async_computation.4 | async-start | bytes 6291456 | tf_op jit(solution)/shard_map/all_to_all | solution.py:20
  134.2 13.1 %collective-permute-start.4 = (bf16[1024,1024]{1,0:T(8,128)(2,1)}, bf16[1024,1024]{1,0:T(8,128)(2,1)}, u32[]{:S(2)}, u32[]{:S(2)}) collective-permute-start(bf16[1024,1024]{1,0:T(8,128)(2,1)} %bitcast.12), channel_id=1, source_target_pairs={{0,1},{1,0},{2,3},{3,2},{4,5},{5,4},{6,7},{7,6},{8,9},{9,8},{10,11... | collective-permute-start | bytes 6291464 | tf_op jit(solution)/shard_map/ppermute | solution.py:16
  142.0 1.7 copy-start.1
  143.7 45.3 %all-to-all-start.7 = ((bf16[128,8,1536]{2,1,0:T(8,128)(2,1)}), bf16[128,8,1536]{2,1,0:T(8,128)(2,1)S(1)}, u32[]{:S(2)}, u32[]{:S(2)}) async-start(bf16[128,8,1536]{2,1,0:T(8,128)(2,1)} %copy-done.1), calls=%async_computation.7 | async-start | bytes 6291456 | tf_op jit(solution)/shard_map/all_to_all | solution.py:20
  154.5 5.2 %collective-permute-start.2 = (bf16[1024,1024]{1,0:T(8,128)(2,1)}, bf16[1024,1024]{1,0:T(8,128)(2,1)}, u32[]{:S(2)}, u32[]{:S(2)}) collective-permute-start(bf16[1024,1024]{1,0:T(8,128)(2,1)} %get-tuple-element.161), channel_id=1, source_target_pairs={{0,1},{1,0},{2,3},{3,2},{4,5},{5,4},{6,7},{7,6},{8,9},{9,8},{10,11... | collective-permute-start | bytes 6291464 | tf_op jit(solution)/shard_map/ppermute | solution.py:16
  166.9 1.5 collective-permute-start.3
  189.0 3.5 %copy-start = (bf16[1024,1024]{1,0:T(8,128)(2,1)S(1)}, bf16[1024,1024]{1,0:T(8,128)(2,1)}, u32[]{:S(2)}) copy-start(bf16[1024,1024]{1,0:T(8,128)(2,1)} %get-tuple-element.97.late_ref) | copy-start | bytes 6291460
  189.0 3.4 %collective-permute-start.5 = (bf16[1024,512]{1,0:T(8,128)(2,1)S(1)}, bf16[1024,512]{1,0:T(8,128)(2,1)S(1)}, u32[]{:S(2)}, u32[]{:S(2)}) collective-permute-start(bf16[1024,512]{1,0:T(8,128)(2,1)S(1)} %slice.86), channel_id=1, source_target_pairs={{0,1},{1,0},{2,3},{3,2},{4,5},{5,4},{6,7},{7,6},{8,9},{9,8},{10,11... | collective-permute-start | bytes 3145736 | tf_op jit(solution)/shard_map/ppermute | solution.py:16
